TPU v7x, 32 devices: a 4x2x2 block of a 4x4x8 slice. The times are simulated.
32 devices in a mesh: dp: 4 (over y, z), tp: 8 (over x, core).
Axes of the slice: x: 4, y: 2, z: 2, core: 2. Of those that a mesh axis runs over, the one named last changes fastest.
The devices are a block of a 4x4x8 slice.
Arguments:
- x_in: bfloat16 [32, 256, 3072], P('dp'), parts along dimension 0
- gain_attn: float32 [1, 3072], replicated
- w_qkv: bfloat16 [1, 3072, 3, 32, 96], P(None, None, None, 'tp')
- w_out: bfloat16 [1, 32, 96, 3072], P(None, 'tp')
- gain_mlp: float32 [1, 3072], replicated
- w_up: bfloat16 [1, 3072, 12288], P(None, None, 'tp')
- w_down: bfloat16 [1, 12288, 3072], P(None, 'tp')
- dy_out: bfloat16 [32, 256, 3072], P('dp'), parts along dimension 0
Outputs:
- output 1: bfloat16 [32, 256, 3072], P('dp'), parts along dimension 0
- output 2: bfloat16 [32, 256, 3072], P('dp'), parts along dimension 0
- output 3: float32 [4, 3072], P('dp'), parts along dimension 0
- output 4: bfloat16 [4, 3072, 3, 32, 96], P('dp', None, None, 'tp'), parts along dimension 0
- output 5: bfloat16 [4, 32, 96, 3072], P('dp', 'tp'), parts along dimension 0
- output 6: float32 [4, 3072], P('dp'), parts along dimension 0
- output 7: bfloat16 [4, 3072, 12288], P('dp', None, 'tp'), parts along dimension 0
- output 8: bfloat16 [4, 12288, 3072], P('dp', 'tp'), parts along dimension 0
There are 4 independent parts. A program takes and returns all parts, laid end to end along the dimension named above; an argument that names none is the same for every part.
All inputs are finite; a program needn't handle non-finite values.
Results may differ from a plain program's by a relative error of at most 0.0187187.
Values are sent between devices in bfloat16 or wider.
A program may use at most 768 MiB of HBM per device.

v0:
```python
import jax
import jax.numpy as jnp
from jax import lax
from jax.sharding import PartitionSpec as P

LN_EPS = 1e-5


def layer_norm(resid_f32, gain_vec):
    mean_val = jnp.mean(resid_f32, axis=-1, keepdims=True)
    centered = resid_f32 - mean_val
    variance = jnp.mean(centered * centered, axis=-1, keepdims=True)
    return centered * lax.rsqrt(variance + LN_EPS) * gain_vec


def causal_probs(queries, keys_loc, score_scale):
    seq_len = queries.shape[1]
    scores = jnp.einsum('bqne,bkne->bnqk', queries, keys_loc, preferred_element_type=jnp.float32) * score_scale
    causal = jnp.arange(seq_len)[:, None] >= jnp.arange(seq_len)[None, :]
    return jax.nn.softmax(jnp.where(causal, scores, -1e30), axis=-1)


def layer_forward(x_in, gain_attn, w_qkv, w_out, gain_mlp, w_up, w_down):
    resid_in = x_in.astype(jnp.float32)
    normed_a = layer_norm(resid_in, gain_attn).astype(jnp.bfloat16)
    qkv_act = jnp.einsum('bsd,dcne->bscne', normed_a, w_qkv, preferred_element_type=jnp.float32).astype(jnp.bfloat16)
    score_scale = w_qkv.shape[-1] ** -0.5
    attn_probs = causal_probs(qkv_act[:, :, 0], qkv_act[:, :, 1], score_scale).astype(jnp.bfloat16)
    attn_out = jnp.einsum('bnqk,bkne->bqne', attn_probs, qkv_act[:, :, 2], preferred_element_type=jnp.float32).astype(jnp.bfloat16)
    attn_part = jnp.einsum('bqne,nef->bqf', attn_out, w_out, preferred_element_type=jnp.float32).astype(jnp.bfloat16)
    attn_sum = lax.psum(attn_part, 'tp')
    x_mid = (resid_in + attn_sum.astype(jnp.float32)).astype(jnp.bfloat16)
    resid_mid = x_mid.astype(jnp.float32)
    normed_m = layer_norm(resid_mid, gain_mlp).astype(jnp.bfloat16)
    pre_act = jnp.einsum('bsd,df->bsf', normed_m, w_up, preferred_element_type=jnp.float32)
    hidden = jax.nn.gelu(pre_act).astype(jnp.bfloat16)
    mlp_part = jnp.einsum('bsf,fd->bsd', hidden, w_down, preferred_element_type=jnp.float32).astype(jnp.bfloat16)
    mlp_sum = lax.psum(mlp_part, 'tp')
    x_out = (resid_mid + mlp_sum.astype(jnp.float32)).astype(jnp.bfloat16)
    return x_out, (x_in, normed_a, qkv_act, attn_out, x_mid, normed_m, pre_act, hidden)


def layer_backward(grad_out, saved_acts, gain_attn, w_qkv, w_out, gain_mlp, w_up, w_down):
    x_in, normed_a, qkv_act, attn_out, x_mid, normed_m, pre_act, hidden = saved_acts
    dw_down = jnp.einsum('bsf,bsd->fd', hidden, grad_out, preferred_element_type=jnp.float32).astype(jnp.bfloat16)
    d_hidden = jnp.einsum('bsd,fd->bsf', grad_out, w_down, preferred_element_type=jnp.float32).astype(jnp.bfloat16)
    gelu_pull = jax.vjp(jax.nn.gelu, pre_act)[1]
    d_pre = gelu_pull(d_hidden.astype(jnp.float32))[0].astype(jnp.bfloat16)
    dw_up = jnp.einsum('bsd,bsf->df', normed_m, d_pre, preferred_element_type=jnp.float32).astype(jnp.bfloat16)
    d_norm_part = jnp.einsum('bsf,df->bsd', d_pre, w_up, preferred_element_type=jnp.float32).astype(jnp.bfloat16)
    d_normed_m = lax.psum(d_norm_part, 'tp')
    norm_pull = jax.vjp(layer_norm, x_mid.astype(jnp.float32), gain_mlp)[1]
    d_resid_m, dgain_mlp = norm_pull(d_normed_m.astype(jnp.float32))
    grad_mid = (grad_out.astype(jnp.float32) + d_resid_m).astype(jnp.bfloat16)
    dw_out = jnp.einsum('bqne,bqf->nef', attn_out, grad_mid, preferred_element_type=jnp.float32).astype(jnp.bfloat16)
    d_attn = jnp.einsum('bqf,nef->bqne', grad_mid, w_out, preferred_element_type=jnp.float32).astype(jnp.bfloat16)
    queries = qkv_act[:, :, 0]
    keys_loc = qkv_act[:, :, 1]
    values = qkv_act[:, :, 2]
    score_scale = w_qkv.shape[-1] ** -0.5
    prob_f32 = causal_probs(queries, keys_loc, score_scale)
    attn_probs = prob_f32.astype(jnp.bfloat16)
    d_values = jnp.einsum('bnqk,bqne->bkne', attn_probs, d_attn, preferred_element_type=jnp.float32).astype(jnp.bfloat16)
    d_probs = jnp.einsum('bqne,bkne->bnqk', d_attn, values, preferred_element_type=jnp.float32).astype(jnp.bfloat16).astype(jnp.float32)
    d_scores = prob_f32 * (d_probs - jnp.sum(d_probs * prob_f32, axis=-1, keepdims=True))
    d_scores = (d_scores * score_scale).astype(jnp.bfloat16)
    d_queries = jnp.einsum('bnqk,bkne->bqne', d_scores, keys_loc, preferred_element_type=jnp.float32).astype(jnp.bfloat16)
    d_keys = jnp.einsum('bnqk,bqne->bkne', d_scores, queries, preferred_element_type=jnp.float32).astype(jnp.bfloat16)
    d_qkv = jnp.stack([d_queries, d_keys, d_values], axis=2)
    dw_qkv = jnp.einsum('bsd,bscne->dcne', normed_a, d_qkv, preferred_element_type=jnp.float32).astype(jnp.bfloat16)
    d_norm_part_a = jnp.einsum('bscne,dcne->bsd', d_qkv, w_qkv, preferred_element_type=jnp.float32).astype(jnp.bfloat16)
    d_normed_a = lax.psum(d_norm_part_a, 'tp')
    norm_pull_a = jax.vjp(layer_norm, x_in.astype(jnp.float32), gain_attn)[1]
    d_resid_a, dgain_attn = norm_pull_a(d_normed_a.astype(jnp.float32))
    grad_in = (grad_mid.astype(jnp.float32) + d_resid_a).astype(jnp.bfloat16)
    return grad_in, (dgain_attn, dw_qkv, dw_out, dgain_mlp, dw_up, dw_down)


def solution(mesh):
    def group_step(x_in, gain_attn, w_qkv, w_out, gain_mlp, w_up, w_down, dy_out):
        num_layers = w_qkv.shape[0]
        weights = [(gain_attn[layer_idx], w_qkv[layer_idx], w_out[layer_idx], gain_mlp[layer_idx], w_up[layer_idx], w_down[layer_idx]) for layer_idx in range(num_layers)]
        x_cur = x_in
        saved_list = []
        for layer_idx in range(num_layers):
            x_cur, saved_acts = layer_forward(x_cur, *weights[layer_idx])
            saved_list.append(saved_acts)
        grad_cur = dy_out
        layer_grads = []
        for layer_idx in reversed(range(num_layers)):
            grad_cur, grads_here = layer_backward(grad_cur, saved_list[layer_idx], *weights[layer_idx])
            layer_grads.insert(0, grads_here)
        stacked = tuple(jnp.stack([grad_set[slot_idx] for grad_set in layer_grads]) for slot_idx in range(6))
        return (x_cur, grad_cur) + stacked

    act_spec = P('dp', None, None)
    in_specs = (act_spec, P(None, None), P(None, None, None, 'tp', None), P(None, 'tp', None, None), P(None, None), P(None, None, 'tp'), P(None, 'tp', None), act_spec)
    out_specs = (act_spec, act_spec, P('dp', None), P('dp', None, None, 'tp', None), P('dp', 'tp', None, None), P('dp', None), P('dp', None, 'tp'), P('dp', 'tp', None))
    return jax.shard_map(group_step, mesh=mesh, in_specs=in_specs, out_specs=out_specs, check_vma=False)
```

profile of v0, /device:TPU:81, one launch (start us, length us, event | category | flops | bytes accessed | tf_op | source)
XLA Modules:
  0.0 886.5 jit_solution(6089404879385551039)
XLA Ops:
  7.2 0.0 copy-start
  7.2 0.1 all-reduce.5.cloned.1.call-start
  7.3 6.4 convert_reduce_fusion.1
  13.8 8.0 fusion.18
  21.8 20.6 %fusion.86 = bf16[8,256,3,4,96]{1,4,3,2,0:T(8,128)(2,1)S(1)} fusion(bf16[1,3072,3,4,96]{1,4,3,2,0:T(8,128)(2,1)} %param.10, f32[3072]{0:T(1024)S(1)} %bitcast.146, f32[8,256]{1,0:T(8,128)S(1)} %fusion.118, f32[8,256]{1,0:T(8,128)S(1)} %broadcast_multiply_fusion.1, bf16[8,256,3072]{2,1,0:T(8,128)(2,1)} %param.8), kind=kOutput, calls=%fused_computation.101 | convolution fusion | flops 14529331200 | bytes 24408064 | tf_op jit(solution)/shard_map/bsd,dcne->bscne/dot_general | solution.py:26
  42.4 1.3 fusion.117
  43.7 4.6 fusion.129
  48.3 4.3 fusion.102
  52.6 1.2 copy-done.22
  53.7 9.7 %bitcast_convert_fusion.1 = bf16[8,256,3072]{2,1,0:T(8,128)(2,1)} fusion(bf16[1,4,96,3072]{3,2,1,0:T(8,128)(2,1)S(1)} %copy-done, bf16[8,4,96,256]{3,2,1,0:T(8,128)(2,1)S(1)} %fusion.102), kind=kOutput, calls=%fused_computation.37 | convolution fusion | flops 4838129664 | bytes 16515072 | tf_op jit(solution)/shard_map/bqne,nef->bqf/dot_general | solution.py:30
  63.4 0.1 all-reduce.5.cloned.1.call-update
  63.4 0.1 all-reduce.7.cloned.1.call-start
  63.5 141.5 %all-reduce.5.cloned.1.call-done = bf16[8,256,3072]{2,1,0:T(8,128)(2,1)} async-done(((bf16[8,256,3072]{2,1,0:T(8,128)(2,1)}), bf16[8,256,3072]{2,1,0:T(8,128)(2,1)}) %all-reduce.5.cloned.1.call-update) | async-done | bytes 12582928 | tf_op jit(solution)/shard_map/psum | solution.py:31
  205.0 14.5 %convert_reduce_fusion = (f32[8,256]{1,0:T(8,128)S(1)}, bf16[8,256,3072]{2,1,0:T(8,128)(2,1)}) fusion(bf16[8,256,3072]{2,1,0:T(8,128)(2,1)} %all-reduce.5.cloned.1.call-done, bf16[8,256,3072]{2,1,0:T(8,128)(2,1)} %param.8), kind=kLoop, calls=%fused_computation.6 | loop fusion | flops 37746688 | bytes 37756928 | tf_op jit(solution)/shard_map/reduce_sum | solution.py:10
  219.5 8.0 fusion.21
  227.6 0.6 copy-done.14
  228.2 26.8 %fusion.52 = f32[8,256,1536]{2,1,0:T(8,128)} fusion(bf16[1,3072,1536]{2,1,0:T(8,128)(2,1)} %param.13, bf16[8,256,3072]{2,1,0:T(8,128)(2,1)} %get-tuple-element.15, f32[3072]{0:T(1024)S(1)} %bitcast.141, f32[8,256]{1,0:T(8,128)S(1)} %fusion.119, f32[8,256]{1,0:T(8,128)S(1)} %broadcast_multiply_fusion), kind=kOutput, calls=%fused_computation.78 | convolution fusion | flops 19358810112 | bytes 34631680 | tf_op jit(solution)/shard_map/bsd,df->bsf/dot_general | solution.py:35
  254.9 33.9 %fusion.28 = bf16[8,256,1536]{2,1,0:T(8,128)(2,1)} fusion(f32[8,256,1536]{2,1,0:T(8,128)} %fusion.52, bf16[8,256,3072]{2,1,0:T(8,128)(2,1)} %param.15, bf16[1,1536,3072]{2,1,0:T(8,128)(2,1)} %param.14), kind=kOutput, calls=%fused_computation.51 | convolution fusion | flops 19396558848 | bytes 40894464 | tf_op jit(solution)/shard_map/bsd,fd->bsf/dot_general | solution.py:46
  288.8 26.0 %fusion.61 = bf16[8,256,3072]{2,1,0:T(8,128)(2,1)} fusion(bf16[8,256,1536]{2,1,0:T(8,128)(2,1)} %fusion.28, bf16[1,3072,1536]{2,1,0:T(8,128)(2,1)} %param.13), kind=kOutput, calls=%fused_computation.85 | convolution fusion | flops 19333644288 | bytes 28311552 | tf_op jit(solution)/shard_map/bsf,df->bsd/dot_general | solution.py:50
  314.8 0.1 all-reduce.7.cloned.1.call-update
  314.9 0.1 all-reduce.9.cloned.1.call-start
  315.0 0.0 slice-start
  315.0 0.0 slice-start.1
  315.0 32.4 %fusion.64 = bf16[8,256,3072]{2,1,0:T(8,128)(2,1)} fusion(bf16[1,1536,3072]{2,1,0:T(8,128)(2,1)} %param.14, f32[8,256,1536]{2,1,0:T(8,128)} %fusion.52), kind=kOutput, calls=%fused_computation.86 | convolution fusion | flops 19361955840 | bytes 34603008 | tf_op jit(solution)/shard_map/bsf,fd->bsd/dot_general | solution.py:37
  347.4 29.4 %fusion.45 = bf16[1,1536,3072]{2,1,0:T(8,128)(2,1)} fusion(bf16[8,256,3072]{2,1,0:T(8,128)(2,1)} %param.15, f32[8,256,1536]{2,1,0:T(8,128)} %fusion.52), kind=kOutput, calls=%fused_computation.71 | convolution fusion | flops 19360382976 | bytes 34603008 | tf_op jit(solution)/shard_map/bsf,bsd->fd/dot_general | solution.py:45
  376.9 28.7 %fusion.44 = bf16[1,3072,1536]{2,1,0:T(8,128)(2,1)} fusion(bf16[8,256,1536]{2,1,0:T(8,128)(2,1)} %fusion.28, bf16[8,256,3072]{2,1,0:T(8,128)(2,1)S(1)} %bitcast.138, f32[3072]{0:T(1024)S(1)} %bitcast.142, f32[8,256]{1,0:T(8,128)S(1)} %copy-done.15, f32[8,256]{1,0:T(8,128)S(1)} %copy-done.7), kind=kOutput, calls=%fused_computation.70 | convolution fusion | flops 19363528704 | bytes 28340224 | tf_op jit(solution)/shard_map/bsd,bsf->df/dot_general | solution.py:49
  405.6 46.8 %all-reduce.7.cloned.1.call-done = bf16[8,256,3072]{2,1,0:T(8,128)(2,1)} async-done(((bf16[8,256,3072]{2,1,0:T(8,128)(2,1)}), bf16[8,256,3072]{2,1,0:T(8,128)(2,1)}) %all-reduce.7.cloned.1.call-update) | async-done | bytes 12582928 | tf_op jit(solution)/shard_map/psum | solution.py:51
  452.4 12.9 %fusion.22 = f32[8,256]{1,0:T(8,128)S(1)} fusion(bf16[8,256,3072]{2,1,0:T(8,128)(2,1)} %all-reduce.7.cloned.1.call-done, bf16[8,256,3072]{2,1,0:T(8,128)(2,1)} %get-tuple-element.15, f32[3072]{0:T(1024)S(1)} %bitcast.143, f32[8,256]{1,0:T(8,128)S(1)} %copy-done.7), kind=kLoop, calls=%fused_computation.34 | loop fusion | flops 37746688 | bytes 25194496 | tf_op jit(solution)/shard_map/transpose(jvp())/reduce_sum | solution.py:13
  465.4 0.0 slice-start.5
  465.4 15.0 %fusion.16 = (f32[3072]{0:T(1024)}, f32[8,256]{1,0:T(8,128)S(1)}) fusion(bf16[8,256,3072]{2,1,0:T(8,128)(2,1)S(1)} %copy-done.4, bf16[8,256,3072]{2,1,0:T(8,128)(2,1)} %get-tuple-element.15, f32[8,256]{1,0:T(8,128)S(1)} %copy-done.15, f32[8,256]{1,0:T(8,128)S(1)} %copy-done.7, f32[8,256]{1,0:T(8,128)S(1)} %multiply_multiply_fusion.3, f32[3072]{0:T(1024)S(1)} %bitcast.144), kind=kLoop, calls=%fused_computation.28 | loop fusion | flops 75492352 | bytes 25223168 | tf_op jit(solution)/shard_map/transpose(jvp())/reduce_sum | solution.py:13
  480.4 18.7 %add_convert_fusion.1 = bf16[8,256,3072]{2,1,0:T(8,128)(2,1)} fusion(bf16[8,256,3072]{2,1,0:T(8,128)(2,1)} %param.15, bf16[8,256,3072]{2,1,0:T(8,128)(2,1)S(1)} %bitcast.140, bf16[8,256,3072]{2,1,0:T(8,128)(2,1)S(1)} %copy-done.4, f32[8,256]{1,0:T(8,128)S(1)} %negate_multiply_fusion.1, f32[8,256]{1,0:T(8,128)S(1)} %multiply_multiply_fusion.3, ...), kind=kLoop, calls=%fused_computation.39 | loop fusion | flops 75497472 | bytes 50376704 | tf_op jit(solution)/shard_map/convert_element_type | solution.py:54
  499.2 8.2 fusion.97
  507.4 4.8 fusion.112
  512.2 5.3 convolution_convert_fusion
  517.5 13.0 %fusion.115 = bf16[8,256,1,4,96]{1,4,3,0,2:T(8,128)(2,1)} fusion(bf16[8,4,256,256]{2,3,1,0:T(8,128)(2,1)} %convolution_convert_fusion, bf16[8,256,3,4,96]{1,4,3,2,0:T(8,128)(2,1)} %copy-done.5, f32[8,4,256,256]{2,3,1,0:T(8,128)} %get-tuple-element.17, f32[8,4,256]{2,1,0:T(4,128)S(1)} %copy-done.26), kind=kOutput, calls=%fused_computation.120 | convolution fusion | flops 422322432 | bytes 28377088 | tf_op jit(solution)/shard_map/bnqk,bqne->bkne/dot_general | solution.py:68
  530.5 13.0 %fusion.116 = bf16[8,256,1,4,96]{1,4,3,0,2:T(8,128)(2,1)} fusion(bf16[8,4,256,256]{2,3,1,0:T(8,128)(2,1)} %convolution_convert_fusion, bf16[8,256,3,4,96]{1,4,3,2,0:T(8,128)(2,1)} %copy-done.5, f32[8,4,256,256]{2,3,1,0:T(8,128)} %get-tuple-element.17, f32[8,4,256]{2,1,0:T(4,128)S(1)} %copy-done.26), kind=kOutput, calls=%fused_computation.121 | convolution fusion | flops 422322432 | bytes 28377088 | tf_op jit(solution)/shard_map/bnqk,bkne->bqne/dot_general | solution.py:67
  543.6 21.7 %bitcast_convert_fusion = bf16[8,256,3072]{2,1,0:T(8,128)(2,1)} fusion(bf16[1,3072,3,4,96]{1,4,3,2,0:T(8,128)(2,1)} %param.10, bf16[8,256,1,4,96]{1,4,3,0,2:T(8,128)(2,1)S(1)} %fusion.112, bf16[8,256,1,4,96]{1,4,3,0,2:T(8,128)(2,1)} %fusion.115, bf16[8,256,1,4,96]{1,4,3,0,2:T(8,128)(2,1)} %fusion.116), kind=kOutput, calls=%fused_computation.36 | convolution fusion | flops 14506524672 | bytes 24379392 | tf_op jit(solution)/shard_map/bscne,dcne->bsd/dot_general | solution.py:71
  565.3 0.1 all-reduce.9.cloned.1.call-update
  565.4 0.6 copy-done.9
  566.0 0.0 copy-done.13
  566.0 0.0 copy-done.17
  566.0 23.3 %fusion.67 = bf16[1,3072,3,4,96]{1,4,3,2,0:T(8,128)(2,1)} fusion(f32[3072]{0:T(1024)S(1)} %bitcast.147, f32[8,256]{1,0:T(8,128)S(1)} %copy-done.17, f32[8,256]{1,0:T(8,128)S(1)} %copy-done.9, bf16[8,256,3072]{2,1,0:T(8,128)(2,1)} %param.8, bf16[8,256,1,4,96]{1,4,3,0,2:T(8,128)(2,1)} %copy-done.24, bf16[8,256,1,4,96]{1,4,3,0,2:T(8,128)(2,1)} %fusion.115, ...), kind=kOutput, calls=%fused_computation.87 | convolution fusion | flops 14544666624 | bytes 24408064 | tf_op jit(solution)/shard_map/bsd,bscne->dcne/dot_general | solution.py:70
  589.3 11.0 %fusion.83 = bf16[1,4,96,3072]{3,2,1,0:T(8,128)(2,1)} fusion(bf16[8,256,3072]{2,1,0:T(8,128)(2,1)} %add_convert_fusion.1, bf16[8,4,96,256]{3,2,1,0:T(8,128)(2,1)S(1)} %copy-done.23), kind=kOutput, calls=%fused_computation.100 | convolution fusion | flops 4833017856 | bytes 16515072 | tf_op jit(solution)/shard_map/bqne,bqf->nef/dot_general | solution.py:55
  600.3 220.5 %all-reduce.9.cloned.1.call-done = (bf16[8,256,3072]{2,1,0:T(8,128)(2,1)}, bf16[8,256,3072]{2,1,0:T(8,128)(2,1)}) async-done(((bf16[8,256,3072]{2,1,0:T(8,128)(2,1)}, bf16[8,256,3072]{2,1,0:T(8,128)(2,1)}), (bf16[8,256,3072]{2,1,0:T(8,128)(2,1)}, bf16[8,256,3072]{2,1,0:T(8,128)(2,1)})) %all-reduce.9.cloned.1.call-update) | async-done | bytes 25165840 | tf_op jit(solution)/shard_map/psum | solution.py:38
  820.8 12.9 %fusion.19 = f32[8,256]{1,0:T(8,128)S(1)} fusion(bf16[8,256,3072]{2,1,0:T(8,128)(2,1)} %get-tuple-element.13, bf16[8,256,3072]{2,1,0:T(8,128)(2,1)} %param.8, f32[3072]{0:T(1024)S(1)} %bitcast.148, f32[8,256]{1,0:T(8,128)S(1)} %copy-done.9), kind=kLoop, calls=%fused_computation.31 | loop fusion | flops 37746688 | bytes 25194496 | tf_op jit(solution)/shard_map/transpose(jvp())/reduce_sum | solution.py:13
  833.8 2.6 copy-done.3
  836.4 23.7 %fusion.17 = (f32[3072]{0:T(1024)}, f32[8,256]{1,0:T(8,128)S(1)}, bf16[8,256,3072]{2,1,0:T(8,128)(2,1)}) fusion(bf16[8,256,3072]{2,1,0:T(8,128)(2,1)} %get-tuple-element.13, bf16[8,256,3072]{2,1,0:T(8,128)(2,1)S(1)} %copy-done.2, f32[8,256]{1,0:T(8,128)S(1)} %copy-done.17, f32[8,256]{1,0:T(8,128)S(1)} %copy-done.9, f32[8,256]{1,0:T(8,128)S(1)} %multiply_multiply_fusion.2, ...), kind=kLoop, calls=%fused_computation.29 | loop fusion | flops 100658176 | bytes 62971904 | tf_op jit(solution)/shard_map/transpose(jvp())/reduce_sum | solution.py:13
  860.1 19.7 %add_convert_fusion = bf16[8,256,3072]{2,1,0:T(8,128)(2,1)} fusion(bf16[8,256,3072]{2,1,0:T(8,128)(2,1)} %add_convert_fusion.1, bf16[8,256,3072]{2,1,0:T(8,128)(2,1)S(1)} %copy-done.2, bf16[8,256,3072]{2,1,0:T(8,128)(2,1)} %get-tuple-element.13, f32[8,256]{1,0:T(8,128)S(1)} %negate_multiply_fusion, f32[8,256]{1,0:T(8,128)S(1)} %multiply_multiply_fusion.2, ...), kind=kLoop, calls=%fused_computation.38 | loop fusion | flops 75497472 | bytes 50376704 | tf_op jit(solution)/shard_map/convert_element_type | solution.py:75
  (67 shorter events, 0.2 us)
Async XLA Ops:
  7.2 46.5 %copy-start = (bf16[1,4,96,3072]{3,2,1,0:T(8,128)(2,1)S(1)}, bf16[1,4,96,3072]{3,2,1,0:T(8,128)(2,1)}, u32[]{:S(2)}) copy-start(bf16[1,4,96,3072]{3,2,1,0:T(8,128)(2,1)} %param.11) | copy-start | bytes 7077892
  7.2 197.8 %all-reduce.5.cloned.1.call-start = ((), (), s32[]{:S(2)}) async-start(), calls=%async_computation | async-start | bytes 25165824 | tf_op jit(solution)/shard_map/psum | solution.py:31
  7.3 14.5 %copy-start.12 = (f32[1,3072]{1,0:T(1,128)S(1)}, f32[1,3072]{1,0:T(1,128)}, u32[]{:S(2)}) copy-start(f32[1,3072]{1,0:T(1,128)} %param.9) | copy-start | bytes 36868
  13.8 28.6 %copy-start.8 = (f32[8,256]{1,0:T(8,128)}, f32[8,256]{1,0:T(8,128)S(1)}, u32[]{:S(2)}) copy-start(f32[8,256]{1,0:T(8,128)S(1)} %broadcast_multiply_fusion.1) | copy-start | bytes 24580
  21.7 20.6 %copy-start.18 = (f32[8,256]{1,0:T(8,128)}, f32[8,256]{1,0:T(8,128)S(1)}, u32[]{:S(2)}) copy-start(f32[8,256]{1,0:T(8,128)S(1)} %fusion.18) | copy-start | bytes 24580
  21.8 20.6 %copy-start.16 = (f32[8,256]{1,0:T(8,128)}, f32[8,256]{1,0:T(8,128)S(1)}, u32[]{:S(2)}) copy-start(f32[8,256]{1,0:T(8,128)S(1)} %fusion.118) | copy-start | bytes 24580
  42.4 5.9 copy-start.5
  48.3 4.3 copy-start.25
  52.6 1.2 copy-start.22
  63.4 388.9 %all-reduce.7.cloned.1.call-start = ((), (), s32[]{:S(2)}) async-start(), calls=%async_computation.1 | async-start | bytes 25165824 | tf_op jit(solution)/shard_map/psum | solution.py:51
  219.5 8.6 copy-start.10
  219.5 35.4 %copy-start.6 = (f32[8,256]{1,0:T(8,128)}, f32[8,256]{1,0:T(8,128)S(1)}, u32[]{:S(2)}) copy-start(f32[8,256]{1,0:T(8,128)S(1)} %broadcast_multiply_fusion) | copy-start | bytes 24580
  227.5 27.4 %copy-start.20 = (f32[8,256]{1,0:T(8,128)}, f32[8,256]{1,0:T(8,128)S(1)}, u32[]{:S(2)}) copy-start(f32[8,256]{1,0:T(8,128)S(1)} %fusion.21) | copy-start | bytes 24580
  227.5 0.6 copy-start.14
  314.9 505.9 %all-reduce.9.cloned.1.call-start = ((), (), s32[]{:S(2)}) async-start(), calls=%async_computation.2 | async-start | bytes 50331648 | tf_op jit(solution)/shard_map/psum | solution.py:38
  315.0 61.9 %slice-start = ((s8[12582912]{0:T(1024)(128)(4,1)}), s8[4194304]{0:T(1024)(128)(4,1)S(1)}, s32[]{:S(2)}) async-start(s8[12582912]{0:T(1024)(128)(4,1)} %bitcast.137), calls=%async_computation.3 | async-start | bytes 8388608
  315.0 61.9 %slice-start.1 = ((s8[12582912]{0:T(1024)(128)(4,1)}), s8[4194304]{0:T(1024)(128)(4,1)S(1)}, s32[]{:S(2)}) async-start(s8[12582912]{0:T(1024)(128)(4,1)} %bitcast.137), calls=%async_computation.4 | async-start | bytes 8388608
  347.4 29.5 %slice-start.2 = ((s8[12582912]{0:T(1024)(128)(4,1)}), s8[4194304]{0:T(1024)(128)(4,1)S(1)}, s32[]{:S(2)}) async-start(s8[12582912]{0:T(1024)(128)(4,1)} %bitcast.137), calls=%async_computation.5 | async-start | bytes 8388608
  347.4 29.5 %copy-start.7 = (f32[8,256]{1,0:T(8,128)S(1)}, f32[8,256]{1,0:T(8,128)}, u32[]{:S(2)}) copy-start(f32[8,256]{1,0:T(8,128)} %copy-done.6) | copy-start | bytes 24580
  347.4 29.5 %copy-start.11 = (f32[1,3072]{1,0:T(1,128)S(1)}, f32[1,3072]{1,0:T(1,128)}, u32[]{:S(2)}) copy-start(f32[1,3072]{1,0:T(1,128)} %param.12) | copy-start | bytes 36868
  347.4 29.5 %copy-start.15 = (f32[8,256]{1,0:T(8,128)S(1)}, f32[8,256]{1,0:T(8,128)}, u32[]{:S(2)}) copy-start(f32[8,256]{1,0:T(8,128)} %copy-done.14) | copy-start | bytes 24580
  405.6 59.8 %copy-start.21 = (f32[8,256]{1,0:T(8,128)S(1)}, f32[8,256]{1,0:T(8,128)}, u32[]{:S(2)}) copy-start(f32[8,256]{1,0:T(8,128)} %copy-done.20) | copy-start | bytes 24580
  452.4 13.0 %copy-start.4 = (bf16[8,256,3072]{2,1,0:T(8,128)(2,1)S(1)}, bf16[8,256,3072]{2,1,0:T(8,128)(2,1)}, u32[]{:S(2)}) copy-start(bf16[8,256,3072]{2,1,0:T(8,128)(2,1)} %all-reduce.7.cloned.1.call-done) | copy-start | bytes 37748740
  452.4 28.0 %slice-start.3 = ((s8[12582912]{0:T(1024)(128)(4,1)}), s8[4194304]{0:T(1024)(128)(4,1)S(1)}, s32[]{:S(2)}) async-start(s8[12582912]{0:T(1024)(128)(4,1)} %bitcast.139), calls=%async_computation.6 | async-start | bytes 8388608
  452.4 28.0 %slice-start.4 = ((s8[12582912]{0:T(1024)(128)(4,1)}), s8[4194304]{0:T(1024)(128)(4,1)S(1)}, s32[]{:S(2)}) async-start(s8[12582912]{0:T(1024)(128)(4,1)} %bitcast.139), calls=%async_computation.7 | async-start | bytes 8388608
  465.4 15.1 %slice-start.5 = ((s8[12582912]{0:T(1024)(128)(4,1)}), s8[4194304]{0:T(1024)(128)(4,1)S(1)}, s32[]{:S(2)}) async-start(s8[12582912]{0:T(1024)(128)(4,1)} %bitcast.139), calls=%async_computation.8 | async-start | bytes 8388608
  499.1 8.2 copy-start.26
  512.2 31.3 %copy-start.24 = (bf16[8,256,1,4,96]{1,4,3,0,2:T(8,128)(2,1)}, bf16[8,256,1,4,96]{1,4,3,0,2:T(8,128)(2,1)S(1)}, u32[]{:S(2)}) copy-start(bf16[8,256,1,4,96]{1,4,3,0,2:T(8,128)(2,1)S(1)} %fusion.112) | copy-start | bytes 4718596
  565.3 0.7 copy-start.9
  565.3 0.7 copy-start.13
  565.3 0.7 copy-start.17
  566.0 23.3 %copy-start.23 = (bf16[8,4,96,256]{3,2,1,0:T(8,128)(2,1)S(1)}, bf16[8,4,96,256]{3,2,1,0:T(8,128)(2,1)}, u32[]{:S(2)}) copy-start(bf16[8,4,96,256]{3,2,1,0:T(8,128)(2,1)} %copy-done.22) | copy-start | bytes 4718596
  820.8 13.0 %copy-start.19 = (f32[8,256]{1,0:T(8,128)S(1)}, f32[8,256]{1,0:T(8,128)}, u32[]{:S(2)}) copy-start(f32[8,256]{1,0:T(8,128)} %copy-done.18) | copy-start | bytes 24580
  820.8 13.0 %copy-start.2 = (bf16[8,256,3072]{2,1,0:T(8,128)(2,1)S(1)}, bf16[8,256,3072]{2,1,0:T(8,128)(2,1)}, u32[]{:S(2)}) copy-start(bf16[8,256,3072]{2,1,0:T(8,128)(2,1)} %param.8) | copy-start | bytes 37748740
  820.8 15.6 %copy-start.3 = (bf16[8,256,3072]{2,1,0:T(8,128)(2,1)S(1)}, bf16[8,256,3072]{2,1,0:T(8,128)(2,1)}, u32[]{:S(2)}) copy-start(bf16[8,256,3072]{2,1,0:T(8,128)(2,1)} %get-tuple-element.15) | copy-start | bytes 37748740
  860.1 19.7 %copy-start.1 = (bf16[1,4,96,3072]{3,2,1,0:T(8,128)(2,1)S(1)}, bf16[1,4,96,3072]{3,2,1,0:T(8,128)(2,1)}, u32[]{:S(2)}) copy-start(bf16[1,4,96,3072]{3,2,1,0:T(8,128)(2,1)} %param.11) | copy-start | bytes 7077892
Sparse Core Ops, SparseCore 0:
  63.6 141.3 all-reduce.4
  315.0 137.3 all-reduce.6
  565.5 255.2 all-reduce.8
where the time goes:
time: 891 us; the launch traced here: 887 us
  waiting for transfers between devices  409 us (46%)
  matrix products  313 us (35%)
  other arithmetic  145 us (16%)
  between operations  14.3 us (2%)
    psum x1, waiting for transfers between devices, layer_forward(): mlp_sum = lax.psum(mlp_part, 'tp')  221 us
    psum x1, waiting for transfers between devices, layer_forward(): attn_sum = lax.psum(attn_part, 'tp')  141 us
    reduce_sum x4, other arithmetic, layer_norm(): return centered * lax.rsqrt(variance + LN_EPS) * gain_vec  64.6 us
    psum x1, waiting for transfers between devices, layer_backward(): d_normed_m = lax.psum(d_norm_part, 'tp')  46.8 us
    dot_general x1, matrix products, layer_backward(): jnp.einsum('bsd,fd->bsf', grad_out, w_down, preferred_element_type=jnp.fl...  33.9 us
    dot_general x1, matrix products, layer_forward(): jnp.einsum('bsf,fd->bsd', hidden, w_down, preferred_element_type=jnp.floa...  32.4 us
    dot_general x1, matrix products, layer_backward(): jnp.einsum('bsf,bsd->fd', hidden, grad_out, preferred_element_type=jnp.fl...  29.4 us
    dot_general x1, matrix products, layer_backward(): jnp.einsum('bsd,bsf->df', normed_m, d_pre, preferred_element_type=jnp.flo...  28.7 us
  transfers between devices with their start and end apart: 3, of which 3 were waited for; matrix products, arithmetic and copies ran while one was open for 14% of the time, Pallas kernels for 0%

commit v1 on v0

v1 whole, which is shorter than its diff:
```python
import jax
import jax.numpy as jnp
from jax import lax
from jax.sharding import Mesh
from jax.sharding import PartitionSpec as P

LN_EPS = 1e-5
CORES = 2
NSUB = 2
BF = jnp.bfloat16
F32 = jnp.float32


def dot(spec, a, b):
    return jnp.einsum(spec, a, b, preferred_element_type=F32)


def ln_parts(z):
    mu = jnp.mean(z, axis=-1, keepdims=True)
    c = z - mu
    var = jnp.mean(c * c, axis=-1, keepdims=True)
    r = lax.rsqrt(var + LN_EPS)
    return c * r, r


def ln_bwd(z, gain, d):
    xhat, r = ln_parts(z)
    dgain = jnp.sum(d * xhat, axis=0)
    h = d * gain
    m1 = jnp.mean(h, axis=-1, keepdims=True)
    m2 = jnp.mean(h * xhat, axis=-1, keepdims=True)
    return r * (h - m1 - xhat * m2), dgain


def probs(q, k, scale):
    n = q.shape[1]
    s = dot('bqne,bkne->bnqk', q, k) * scale
    causal = jnp.arange(n)[:, None] >= jnp.arange(n)[None, :]
    return jax.nn.softmax(jnp.where(causal, s, -1e30), axis=-1)


def solution(mesh):
    chips = mesh.shape['tp'] // CORES
    mesh3 = Mesh(mesh.devices.reshape(mesh.shape['dp'], chips, CORES), ('dp', 'chip', 'core'))
    TP = ('chip', 'core')

    def swap(v):
        return lax.ppermute(v, 'core', [(0, 1), (1, 0)])

    def step(x_in, gain_attn, w_qkv, w_out, gain_mlp, w_up, w_down, dy_out):
        ga, gm = gain_attn[0], gain_mlp[0]
        wqkv, wo, wu, wd = w_qkv[0], w_out[0], w_up[0], w_down[0]
        nseq, slen, dm = x_in.shape
        scale = wqkv.shape[-1] ** -0.5
        core = lax.axis_index('core')
        chip = lax.axis_index('chip')
        half = nseq // CORES
        cs = half // NSUB
        rows = cs * slen // chips

        def cut(v, mine, k):
            first = core if mine else 1 - core
            return lax.dynamic_slice_in_dim(v, first * half + cs * k, cs, axis=0)

        def shard(v):
            return lax.dynamic_slice_in_dim(v.reshape(cs * slen, dm), chip * rows, rows, axis=0)

        def rs(part_mine, part_other):
            got = swap(part_other.astype(BF))
            s = (part_mine + got.astype(F32)).astype(BF)
            return lax.psum_scatter(s.reshape(cs * slen, dm), 'chip', scatter_dimension=0, tiled=True)

        def ag(v):
            mine = lax.all_gather(v, 'chip', axis=0, tiled=True)
            return mine, swap(mine)

        A, QKV, O = {}, {}, {}
        xm, nm, nmg = [], [], {}
        for k in range(NSUB):
            part = {}
            for mine in (False, True):
                xc = cut(x_in, mine, k)
                xh, _ = ln_parts(xc.astype(F32))
                a = (xh * ga).astype(BF)
                qkv = dot('bsd,dcne->bscne', a, wqkv).astype(BF)
                p = probs(qkv[:, :, 0], qkv[:, :, 1], scale).astype(BF)
                o = dot('bnqk,bkne->bqne', p, qkv[:, :, 2]).astype(BF)
                part[mine] = dot('bqne,nef->bqf', o, wo)
                A[mine, k], QKV[mine, k], O[mine, k] = a, qkv, o
            r = rs(part[True], part[False])
            xs = (shard(cut(x_in, True, k)).astype(F32) + r.astype(F32)).astype(BF)
            xm.append(xs)
            xh, _ = ln_parts(xs.astype(F32))
            nmg[True, k], nmg[False, k] = ag((xh * gm).astype(BF))
        H, DP = {}, {}
        gmid, gms, ys, dgm = {}, [], [], 0.
        for k in range(NSUB):
            part, part_y = {}, {}
            for mine in (False, True):
                b = nmg[mine, k]
                pre = dot('td,df->tf', b, wu)
                act, pull = jax.vjp(jax.nn.gelu, pre)
                h = act.astype(BF)
                dyc = cut(dy_out, mine, k).reshape(cs * slen, dm)
                dh = dot('td,fd->tf', dyc, wd).astype(BF)
                dp = pull(dh.astype(F32))[0].astype(BF)
                part[mine] = dot('tf,df->td', dp, wu)
                part_y[mine] = dot('tf,fd->td', h, wd)
                H[mine, k], DP[mine, k] = h, dp
            r = rs(part[True], part[False])
            dr, dg = ln_bwd(xm[k].astype(F32), gm, r.astype(F32))
            dgm = dgm + dg
            gs = (shard(cut(dy_out, True, k)).astype(F32) + dr).astype(BF)
            gms.append(gs)
            gmid[True, k], gmid[False, k] = ag(gs)
            ry = rs(part_y[True], part_y[False])
            ys.append((xm[k].astype(F32) + ry.astype(F32)).astype(BF))
        DQKV = {}
        dxs, dga = [], 0.
        for k in range(NSUB):
            part = {}
            for mine in (False, True):
                g = gmid[mine, k].reshape(cs, slen, dm)
                qkv = QKV[mine, k]
                q, kk, v = qkv[:, :, 0], qkv[:, :, 1], qkv[:, :, 2]
                do = dot('bqf,nef->bqne', g, wo).astype(BF)
                pf = probs(q, kk, scale)
                pb = pf.astype(BF)
                dv = dot('bnqk,bqne->bkne', pb, do).astype(BF)
                dpr = dot('bqne,bkne->bnqk', do, v).astype(BF).astype(F32)
                ds = pf * (dpr - jnp.sum(dpr * pf, axis=-1, keepdims=True))
                ds = (ds * scale).astype(BF)
                dq = dot('bnqk,bkne->bqne', ds, kk).astype(BF)
                dk = dot('bnqk,bqne->bkne', ds, q).astype(BF)
                dqkv = jnp.stack([dq, dk, dv], axis=2)
                DQKV[mine, k] = dqkv
                part[mine] = dot('bscne,dcne->bsd', dqkv, wqkv)
            r = rs(part[True], part[False])
            dr, dg = ln_bwd(shard(cut(x_in, True, k)).astype(F32), ga, r.astype(F32))
            dga = dga + dg
            dxs.append((gms[k].astype(F32) + dr).astype(BF))

        order = [(m, k) for k in range(NSUB) for m in (False, True)]

        def cat(d):
            return jnp.concatenate([d[o] for o in order], axis=0)

        dys = jnp.concatenate([cut(dy_out, m, k) for m, k in order], axis=0).reshape(nseq * slen, dm)
        dw_down = dot('tf,td->fd', cat(H), dys).astype(BF)
        dw_up = dot('td,tf->df', cat(nmg), cat(DP)).astype(BF)
        g_all = cat(gmid).reshape(nseq, slen, dm)
        dw_out = dot('bqne,bqf->nef', cat(O), g_all).astype(BF)
        dw_qkv = dot('bsd,bscne->dcne', cat(A), cat(DQKV)).astype(BF)

        def full(parts):
            mine = jnp.concatenate([lax.all_gather(v, 'chip', axis=0, tiled=True) for v in parts], axis=0)
            return lax.all_gather(mine, 'core', axis=0, tiled=True).reshape(nseq, slen, dm)

        y = full(ys)
        dx = full(dxs)
        dgains = lax.psum(jnp.stack([dgm, dga]), TP)
        return (y, dx, dgains[1:2], dw_qkv[None], dw_out[None], dgains[0:1], dw_up[None], dw_down[None])

    act = P('dp', None, None)
    in_specs = (act, P(None, None), P(None, None, None, TP, None), P(None, TP, None, None), P(None, None), P(None, None, TP), P(None, TP, None), act)
    out_specs = (act, act, P('dp', None), P('dp', None, None, TP, None), P('dp', TP, None, None), P('dp', None), P('dp', None, TP), P('dp', TP, None))
    return jax.shard_map(step, mesh=mesh3, in_specs=in_specs, out_specs=out_specs, check_vma=False)
```

time: 891 us -> 872 us (0.979)
  waiting for transfers between devices: 409 us -> 306 us
  matrix products: 313 us -> 388 us
  other arithmetic: 145 us -> 84.3 us
  local copies, waits for them, and re-layouts: 5.15 us -> 38.8 us
  blocking collectives: 0 us -> 21.1 us
  starting transfers between devices: 0.19 us -> 10.2 us
    psum x3 -> x0, waiting for transfers between devices: 409 us -> none  [the longest x1 221 us: layer_forward(): mlp_sum = lax.psum(mlp_part, 'tp')]
    reduce_scatter x0 -> x8, waiting for transfers between devices: none -> 153 us  [rs(): lax.psum_scatter(s.reshape(cs * slen, dm), 'chip', scatter_dimension=0, t...]
    all_gather x0 -> x10, waiting for transfers between devices: none -> 134 us  [the longest x4 66.1 us: full(): lax.all_gather(v, 'chip', axis=0, tiled=True)]
    reduce_sum x8 -> x13, other arithmetic: 102 us -> 29.2 us  [the longest x6 17.6 us: ln_parts(): mu = jnp.mean(z, axis=-1, keepdims=True)]
    dot_general x18 -> x56, matrix products: 313 us -> 375 us  [dot(): return jnp.einsum(spec, a, b, preferred_element_type=F32)]
    concatenate x0 -> x4, other arithmetic: none -> 26.1 us  [the longest x2 12 us: full(): jnp.concatenate([lax.all_gather(v, 'chip', axis=0, tiled=True) for v in p...]
    unnamed x66 -> x196, local copies, waits for them, and re-layouts: 5.15 us -> 28.5 us
    psum x0 -> x1, blocking collectives: none -> 21.1 us  [step(): dgains = lax.psum(jnp.stack([dgm, dga]), TP)]
  transfers between devices with their start and end apart: 3 -> 30, of which waited for: 3 -> 15; matrix products, arithmetic and copies ran while one was open for 14% -> 50% of each run, Pallas kernels for 0% -> 0%
where the time goes in v1:
time: 872 us; the launch traced here: 864 us
  matrix products  388 us (44%)
  waiting for transfers between devices  306 us (35%)
  other arithmetic  84.3 us (10%)
  local copies, waits for them, and re-layouts  38.8 us (4%)
  blocking collectives  21.1 us (2%)
  between operations  15.9 us (2%)
  starting transfers between devices  10.2 us (1%)
    dot_general x56, matrix products, dot(): return jnp.einsum(spec, a, b, preferred_element_type=F32)  375 us
    reduce_scatter x8, waiting for transfers between devices, rs(): lax.psum_scatter(s.reshape(cs * slen, dm), 'chip', scatter_dimension=0, t...  153 us
    all_gather x4, waiting for transfers between devices, full(): lax.all_gather(v, 'chip', axis=0, tiled=True)  66.1 us
    all_gather x4, waiting for transfers between devices, ag(): mine = lax.all_gather(v, 'chip', axis=0, tiled=True)  62.9 us
    unnamed x196, local copies, waits for them, and re-layouts  28.5 us
    psum x1, blocking collectives, step(): dgains = lax.psum(jnp.stack([dgm, dga]), TP)  21.1 us
    reduce_sum x6, other arithmetic, ln_parts(): mu = jnp.mean(z, axis=-1, keepdims=True)  17.6 us
  transfers between devices with their start and end apart: 30, of which 15 were waited for; matrix products, arithmetic and copies ran while one was open for 50% of the time, Pallas kernels for 0%

profile of v1, /device:TPU:81, one launch (start us, length us, event | category | flops | bytes accessed | tf_op | source)
XLA Modules:
  0.0 864.2 jit_solution(17445621280070557136)
XLA Ops:
  11.7 6.2 convert_reduce_fusion.3
  22.3 9.3 %fusion.97 = (bf16[2,256,3072]{2,1,0:T(8,128)(2,1)S(1)}, bf16[2,256,3072]{2,1,0:T(8,128)(2,1)}, bf16[2,256,3072]{2,1,0:T(8,128)(2,1)}, bf16[2,256,3072]{2,1,0:T(8,128)(2,1)}) fusion(f32[2,256]{1,0:T(2,128)S(1)} %add_rsqrt_fusion.2, f32[2,256]{1,0:T(2,128)S(1)} %get-tuple-element.75, f32[3072]{0:T(1024)S(1)} %bitcast.511, ...), kind=kLoop, calls=%fused_computation.105 | loop fusion | flops 31457280 | bytes 25194504 | tf_op jit(solution)/shard_map/convert_element_type | solution.py:84
  33.3 6.9 fusion.329
  50.8 6.9 fusion.324
  62.8 5.8 fusion.118
  70.1 35.9 %reduce-scatter.9.cloned.1.call-done = bf16[128,3072]{1,0:T(8,128)(2,1)} async-done(((bf16[512,3072]{1,0:T(8,128)(2,1)}), bf16[128,3072]{1,0:T(8,128)(2,1)}) %reduce-scatter.9.cloned.1.call-update) | async-done | bytes 786448 | tf_op jit(solution)/shard_map/reduce_scatter | solution.py:71
  110.2 8.9 %fusion.339 = bf16[2,256,3,4,96]{1,4,3,2,0:T(8,128)(2,1)} fusion(bf16[1,3072,3,4,96]{1,4,3,2,0:T(8,128)(2,1)} %param.10, bf16[2,256,3072]{2,1,0:T(8,128)(2,1)} %get-tuple-element.33), kind=kOutput, calls=%fused_computation.372 | convolution fusion | flops 3624468480 | bytes 11403264 | tf_op jit(solution)/shard_map/bsd,dcne->bscne/dot_general | solution.py:15
  128.9 17.2 %all-gather.11.cloned.1.call-done = bf16[512,3072]{1,0:T(8,128)(2,1)} async-done(((bf16[128,3072]{1,0:T(8,128)(2,1)}), bf16[512,3072]{1,0:T(8,128)(2,1)}) %all-gather.11.cloned.1.call-update) | async-done | bytes 3145744 | tf_op jit(solution)/shard_map/all_gather | solution.py:74
  147.0 8.9 %fusion.334 = bf16[2,256,3,4,96]{1,4,3,2,0:T(8,128)(2,1)} fusion(bf16[1,3072,3,4,96]{1,4,3,2,0:T(8,128)(2,1)} %param.10, bf16[2,256,3072]{2,1,0:T(8,128)(2,1)} %get-tuple-element.57), kind=kOutput, calls=%fused_computation.371 | convolution fusion | flops 3624468480 | bytes 11403264 | tf_op jit(solution)/shard_map/bsd,dcne->bscne/dot_general | solution.py:15
  161.3 9.6 %constant_dynamic-slice_fusion.2 = (bf16[2,256,3072]{2,1,0:T(8,128)(2,1)}, bf16[2,256,3072]{2,1,0:T(8,128)(2,1)}, bf16[2,256,3072]{2,1,0:T(8,128)(2,1)}, bf16[2,256,3072]{2,1,0:T(8,128)(2,1)}) fusion(bf16[8,256,3072]{2,1,0:T(8,128)(2,1)} %param.15, s32[]{:T(128)S(6)} %select_n.54, s32[]{:T(128)S(6)} %select_n.51, s32[]{:T(128)S(6)} %select_n.58, ...), kind=kLoop, calls=%fused_computation.497 | loop fusion | bytes 25165840 | tf_op jit(solution)/shard_map/dynamic_slice | solution.py:63
  176.5 11.3 %multiply_convert_fusion.2 = (bf16[512,1536]{1,0:T(8,128)(2,1)}, f32[512,1536]{1,0:T(8,128)}) fusion(bf16[512,3072]{1,0:T(8,128)(2,1)} %collective-permute-done.1, bf16[1,3072,1536]{2,1,0:T(8,128)(2,1)} %param.13), kind=kOutput, calls=%fused_computation.232 | convolution fusion | flops 4838916096 | bytes 17301504 | tf_op jit(solution)/shard_map/td,df->tf/dot_general | solution.py:15
  187.8 11.4 %fusion.172 = bf16[512,1536]{1,0:T(8,128)(2,1)S(1)} fusion(f32[512,1536]{1,0:T(8,128)} %get-tuple-element.69, bf16[512,3072]{1,0:T(8,128)(2,1)S(1)} %bitcast.494, bf16[1,1536,3072]{2,1,0:T(8,128)(2,1)} %param.14), kind=kOutput, calls=%fused_computation.193 | convolution fusion | flops 4849139712 | bytes 17301504 | tf_op jit(solution)/shard_map/td,fd->tf/dot_general | solution.py:15
  199.3 6.4 fusion.152
  205.7 7.1 multiply_convert_fusion.3
  212.8 11.5 %fusion.167 = bf16[512,1536]{1,0:T(8,128)(2,1)S(1)} fusion(f32[512,1536]{1,0:T(8,128)} %get-tuple-element.67, bf16[512,3072]{1,0:T(8,128)(2,1)S(1)} %bitcast.491, bf16[1,1536,3072]{2,1,0:T(8,128)(2,1)} %param.14), kind=kOutput, calls=%fused_computation.188 | convolution fusion | flops 4849139712 | bytes 17301504 | tf_op jit(solution)/shard_map/td,fd->tf/dot_general | solution.py:15
  225.4 7.8 add_convert_fusion.1
  233.4 8.2 fusion.158
  247.5 10.5 %add_convert_fusion.3 = bf16[512,3072]{1,0:T(8,128)(2,1)} fusion(bf16[512,3072]{1,0:T(8,128)(2,1)S(1)} %collective-permute-done.2, bf16[512,1536]{1,0:T(8,128)(2,1)S(1)} %copy-done.70, bf16[1,1536,3072]{2,1,0:T(8,128)(2,1)} %param.14), kind=kOutput, calls=%fused_computation.140 | convolution fusion | flops 4836556800 | bytes 17301504 | tf_op jit(solution)/shard_map/tf,fd->td/dot_general | solution.py:15
  271.0 34.6 %reduce-scatter.11.cloned.1.call-done = bf16[128,3072]{1,0:T(8,128)(2,1)} async-done(((bf16[512,3072]{1,0:T(8,128)(2,1)}), bf16[128,3072]{1,0:T(8,128)(2,1)}) %reduce-scatter.11.cloned.1.call-update) | async-done | bytes 786448 | tf_op jit(solution)/shard_map/reduce_scatter | solution.py:71
  310.4 35.7 %all-gather.15.cloned.1.call-done = bf16[512,3072]{1,0:T(8,128)(2,1)} async-done(((bf16[128,3072]{1,0:T(8,128)(2,1)}), bf16[512,3072]{1,0:T(8,128)(2,1)}) %all-gather.15.cloned.1.call-update) | async-done | bytes 3145744 | tf_op jit(solution)/shard_map/all_gather | solution.py:74
  352.4 11.2 %multiply_convert_fusion = (bf16[512,1536]{1,0:T(8,128)(2,1)}, f32[512,1536]{1,0:T(8,128)}) fusion(bf16[512,3072]{1,0:T(8,128)(2,1)} %collective-permute-done.4, bf16[1,3072,1536]{2,1,0:T(8,128)(2,1)} %param.13), kind=kOutput, calls=%fused_computation.230 | convolution fusion | flops 4838916096 | bytes 17301504 | tf_op jit(solution)/shard_map/td,df->tf/dot_general | solution.py:15
  363.6 11.4 %fusion.182 = bf16[512,1536]{1,0:T(8,128)(2,1)S(1)} fusion(f32[512,1536]{1,0:T(8,128)} %get-tuple-element.73, bf16[512,3072]{1,0:T(8,128)(2,1)S(1)} %bitcast.495, bf16[1,1536,3072]{2,1,0:T(8,128)(2,1)} %param.14), kind=kOutput, calls=%fused_computation.203 | convolution fusion | flops 4849139712 | bytes 17301504 | tf_op jit(solution)/shard_map/td,fd->tf/dot_general | solution.py:15
  375.1 6.4 fusion.155
  381.9 7.0 multiply_convert_fusion.1
  388.9 11.7 %fusion.177 = bf16[512,1536]{1,0:T(8,128)(2,1)S(1)} fusion(f32[512,1536]{1,0:T(8,128)} %get-tuple-element.71, bf16[512,3072]{1,0:T(8,128)(2,1)S(1)} %bitcast.493, bf16[1,1536,3072]{2,1,0:T(8,128)(2,1)} %param.14), kind=kOutput, calls=%fused_computation.198 | convolution fusion | flops 4849139712 | bytes 17301504 | tf_op jit(solution)/shard_map/td,fd->tf/dot_general | solution.py:15
  401.8 7.8 add_convert_fusion
  409.8 8.2 fusion.161
  423.8 10.4 %add_convert_fusion.2 = bf16[512,3072]{1,0:T(8,128)(2,1)} fusion(bf16[512,3072]{1,0:T(8,128)(2,1)S(1)} %collective-permute-done.5, bf16[512,1536]{1,0:T(8,128)(2,1)S(1)} %copy-done.72, bf16[1,1536,3072]{2,1,0:T(8,128)(2,1)} %param.14), kind=kOutput, calls=%fused_computation.139 | convolution fusion | flops 4836556800 | bytes 17301504 | tf_op jit(solution)/shard_map/tf,fd->td/dot_general | solution.py:15
  434.6 9.9 %reduce-scatter.21.cloned.1.call-done = bf16[128,3072]{1,0:T(8,128)(2,1)} async-done(((bf16[512,3072]{1,0:T(8,128)(2,1)}), bf16[128,3072]{1,0:T(8,128)(2,1)}) %reduce-scatter.21.cloned.1.call-update) | async-done | bytes 786448 | tf_op jit(solution)/shard_map/reduce_scatter | solution.py:71
  447.1 35.3 %reduce-scatter.15.cloned.1.call-done = bf16[128,3072]{1,0:T(8,128)(2,1)} async-done(((bf16[512,3072]{1,0:T(8,128)(2,1)}), bf16[128,3072]{1,0:T(8,128)(2,1)}) %reduce-scatter.15.cloned.1.call-update) | async-done | bytes 786448 | tf_op jit(solution)/shard_map/reduce_scatter | solution.py:71
  502.4 8.8 %bitcast_convert_fusion.2 = bf16[2,256,3072]{2,1,0:T(8,128)(2,1)} fusion(bf16[1,3072,3,4,96]{1,4,3,2,0:T(8,128)(2,1)} %param.10, bf16[2,256,1,4,96]{1,4,3,0,2:T(8,128)(2,1)S(1)} %fusion.381, bf16[2,256,1,4,96]{1,4,3,0,2:T(8,128)(2,1)S(1)} %copy-done.20, bf16[2,256,1,4,96]{1,4,3,0,2:T(8,128)(2,1)S(1)} %copy-done.18), kind=kOutput, calls=%fused_computation.128 | convolution fusion | flops 3626631168 | bytes 11403264 | tf_op jit(solution)/shard_map/bscne,dcne->bsd/dot_general | solution.py:15
  512.2 10.1 %all-gather.25.cloned.1.call-done = bf16[512,3072]{1,0:T(8,128)(2,1)} async-done(((bf16[128,3072]{1,0:T(8,128)(2,1)}), bf16[512,3072]{1,0:T(8,128)(2,1)}) %all-gather.25.cloned.1.call-update) | async-done | bytes 3145744 | tf_op jit(solution)/shard_map/all_gather | solution.py:74
  539.0 9.3 %fusion.116 = bf16[2,256,3072]{2,1,0:T(8,128)(2,1)} fusion(bf16[2,256,3072]{2,1,0:T(8,128)(2,1)} %collective-permute-done.8, bf16[1,3072,3,4,96]{1,4,3,2,0:T(8,128)(2,1)} %param.10, bf16[2,256,1,4,96]{1,4,3,0,2:T(8,128)(2,1)S(1)} %fusion.380, bf16[2,256,1,4,96]{1,4,3,0,2:T(8,128)(2,1)S(1)} %copy-done.26, bf16[2,256,1,4,96]{1,4,3,0,2:T(8,128)(2,1)S(1)} %copy-done.24), kind=kOutput, calls=%fused_computation.130 | convolution fusion | flops 3629776896 | bytes 14548992 | tf_op jit(solution)/shard_map/bscne,dcne->bsd/dot_general | solution.py:15
  564.7 8.8 %bitcast_convert_fusion.1 = bf16[2,256,3072]{2,1,0:T(8,128)(2,1)} fusion(bf16[1,3072,3,4,96]{1,4,3,2,0:T(8,128)(2,1)} %param.10, bf16[2,256,1,4,96]{1,4,3,0,2:T(8,128)(2,1)S(1)} %fusion.383, bf16[2,256,1,4,96]{1,4,3,0,2:T(8,128)(2,1)S(1)} %copy-done.31, bf16[2,256,1,4,96]{1,4,3,0,2:T(8,128)(2,1)S(1)} %copy-done.30), kind=kOutput, calls=%fused_computation.125 | convolution fusion | flops 3626631168 | bytes 11403264 | tf_op jit(solution)/shard_map/bscne,dcne->bsd/dot_general | solution.py:15
  586.4 9.3 %fusion.115 = bf16[2,256,3072]{2,1,0:T(8,128)(2,1)} fusion(bf16[2,256,3072]{2,1,0:T(8,128)(2,1)} %collective-permute-done.11, bf16[1,3072,3,4,96]{1,4,3,2,0:T(8,128)(2,1)} %param.10, bf16[2,256,1,4,96]{1,4,3,0,2:T(8,128)(2,1)S(1)} %fusion.382, bf16[2,256,1,4,96]{1,4,3,0,2:T(8,128)(2,1)S(1)} %fusion.388, bf16[2,256,1,4,96]{1,4,3,0,2:T(8,128)(2,1)S(1)} %fusion.389), kind=kOutput, calls=%fused_computation.127 | convolution fusion | flops 3629776896 | bytes 14548992 | tf_op jit(solution)/shard_map/bscne,dcne->bsd/dot_general | solution.py:15
  598.6 32.4 %reduce-scatter.23.cloned.1.call-done = bf16[128,3072]{1,0:T(8,128)(2,1)} async-done(((bf16[512,3072]{1,0:T(8,128)(2,1)}), bf16[128,3072]{1,0:T(8,128)(2,1)}) %reduce-scatter.23.cloned.1.call-update) | async-done | bytes 786448 | tf_op jit(solution)/shard_map/reduce_scatter | solution.py:71
  640.1 28.3 %all-gather.13.cloned.1.call-done = bf16[512,3072]{1,0:T(8,128)(2,1)} async-done(((bf16[128,3072]{1,0:T(8,128)(2,1)}), bf16[512,3072]{1,0:T(8,128)(2,1)}) %all-gather.13.cloned.1.call-update) | async-done | bytes 3145744 | tf_op jit(solution)/shard_map/all_gather | solution.py:156
  668.4 37.8 %all-gather.17.cloned.1.call-done = bf16[512,3072]{1,0:T(8,128)(2,1)} async-done(((bf16[128,3072]{1,0:T(8,128)(2,1)}), bf16[512,3072]{1,0:T(8,128)(2,1)}) %all-gather.17.cloned.1.call-update) | async-done | bytes 3145744 | tf_op jit(solution)/shard_map/all_gather | solution.py:156
  706.2 6.0 pad_maximum_fusion.2
  712.4 7.5 pad_maximum_fusion.1
  719.9 22.7 %fusion.28 = bf16[1,1536,3072]{2,1,0:T(8,128)(2,1)} fusion(bf16[2048,3072]{1,0:T(8,128)(2,1)S(1)} %bitcast.498, bf16[512,1536]{1,0:T(8,128)(2,1)S(1)} %copy-done.73, bf16[512,1536]{1,0:T(8,128)(2,1)S(1)} %copy-done.79, bf16[512,1536]{1,0:T(8,128)(2,1)S(1)} %copy-done.71, bf16[512,1536]{1,0:T(8,128)(2,1)S(1)} %copy-done.78), kind=kOutput, calls=%fused_computation.30 | convolution fusion | flops 19357237248 | bytes 28311552 | tf_op jit(solution)/shard_map/tf,td->fd/dot_general | solution.py:15
  742.6 26.2 %fusion.29 = bf16[1,3072,1536]{2,1,0:T(8,128)(2,1)} fusion(bf16[512,3072]{1,0:T(8,128)(2,1)} %all-gather.15.cloned.1.call-done, bf16[512,3072]{1,0:T(8,128)(2,1)} %collective-permute-done.4, bf16[512,3072]{1,0:T(8,128)(2,1)} %all-gather.11.cloned.1.call-done, bf16[512,3072]{1,0:T(8,128)(2,1)} %collective-permute-done.1, bf16[512,1536]{1,0:T(8,128)(2,1)} %copy-done.75, ...), kind=kOutput, calls=%fused_computation.31 | convolution fusion | flops 19407568896 | bytes 28311552 | tf_op jit(solution)/shard_map/td,tf->df/dot_general | solution.py:15
  769.5 6.6 pad_maximum_fusion
  776.3 6.5 fusion.164
  786.3 6.0 pad_maximum_fusion.3
  792.4 20.3 %fusion.72 = bf16[1,3072,3,4,96]{1,4,3,2,0:T(8,128)(2,1)} fusion(bf16[2,256,3072]{2,1,0:T(8,128)(2,1)} %get-tuple-element.57, bf16[2,256,3072]{2,1,0:T(8,128)(2,1)} %get-tuple-element.33, bf16[2,256,3072]{2,1,0:T(8,128)(2,1)} %get-tuple-element.56, bf16[2,256,3072]{2,1,0:T(8,128)(2,1)} %copy-done.16, bf16[8,256,3,4,96]{1,4,3,0,2:T(8,128)(2,1)} %fusion.523), kind=kOutput, calls=%fused_computation.80 | convolution fusion | flops 14549385216 | bytes 24379392 | tf_op jit(solution)/shard_map/bsd,bscne->dcne/dot_general | solution.py:15
  812.8 21.1 %psum.7 = f32[2,3072]{1,0:T(2,128)S(1)} all-reduce(f32[2,3072]{1,0:T(2,128)S(1)} %pad_maximum_fusion.4), channel_id=1, replica_groups=mesh['dp'=4,'chip'=4,'core'=2] {'chip','core'}, use_global_device_ids=true, to_apply=%region_48.49 | all-reduce | flops 6144 | bytes 49152 | tf_op jit(solution)/shard_map/psum | solution.py:161
  839.1 11.1 %copy.81 = bf16[8,256,3072]{2,1,0:T(8,128)(2,1)} copy(bf16[8,256,3072]{2,1,0:T(8,128)(2,1)} %bitcast.496) | data formatting | bytes 25165824
  (342 shorter events, 189.8 us)
Async XLA Ops:
  7.2 38.1 %copy-start = (bf16[1,4,96,3072]{3,2,1,0:T(8,128)(2,1)S(1)}, bf16[1,4,96,3072]{3,2,1,0:T(8,128)(2,1)}, u32[]{:S(2)}) copy-start(bf16[1,4,96,3072]{3,2,1,0:T(8,128)(2,1)} %param.11) | copy-start | bytes 7077892
  7.2 98.8 %reduce-scatter.9.cloned.1.call-start = ((), (), s32[]{:S(2)}) async-start(), calls=%async_computation.8 | async-start | bytes 3932160 | tf_op jit(solution)/shard_map/reduce_scatter | solution.py:71
  48.8 14.0 %collective-permute-start = (bf16[2,256,3072]{2,1,0:T(8,128)(2,1)}, bf16[2,256,3072]{2,1,0:T(8,128)(2,1)}, u32[]{:S(2)}, u32[]{:S(2)}) collective-permute-start(bf16[2,256,3072]{2,1,0:T(8,128)(2,1)} %bitcast_convert_fusion.4), channel_id=1, source_target_pairs={{0,1},{1,0},{2,3},{3,2},{4,5},{5,4},{6,7},{7,6},{8,9},{9,8},{10,11... | collective-permute-start | bytes 9437192 | tf_op jit(solution)/shard_map/ppermute | solution.py:48
  68.6 40.3 %copy-start.42 = (f32[1,3072]{1,0:T(1,128)S(1)}, f32[1,3072]{1,0:T(1,128)}, u32[]{:S(2)}) copy-start(f32[1,3072]{1,0:T(1,128)} %param.12) | copy-start | bytes 36868
  68.6 77.4 %all-gather.11.cloned.1.call-start = ((), (), s32[]{:S(2)}) async-start(), calls=%async_computation.9 | async-start | bytes 3932160 | tf_op jit(solution)/shard_map/all_gather | solution.py:74
  70.1 40.1 %copy-start.53 = (f32[128]{0:T(128)}, f32[128]{0:T(128)S(1)}, u32[]{:S(2)}) copy-start(f32[128]{0:T(128)S(1)} %broadcast_multiply_fusion.11) | copy-start | bytes 1540
  110.1 149.3 %reduce-scatter.13.cloned.1.call-start = ((), (), s32[]{:S(2)}) async-start(), calls=%async_computation.12 | async-start | bytes 3932160 | tf_op jit(solution)/shard_map/reduce_scatter | solution.py:71
  128.0 43.0 %collective-permute-start.3 = (bf16[2,256,3072]{2,1,0:T(8,128)(2,1)}, bf16[2,256,3072]{2,1,0:T(8,128)(2,1)}, u32[]{:S(2)}, u32[]{:S(2)}) collective-permute-start(bf16[2,256,3072]{2,1,0:T(8,128)(2,1)} %bitcast_convert_fusion.3), channel_id=1, source_target_pairs={{0,1},{1,0},{2,3},{3,2},{4,5},{5,4},{6,7},{7,6},{8,9},{9,8},{10,11... | collective-permute-start | bytes 9437192 | tf_op jit(solution)/shard_map/ppermute | solution.py:48
  146.1 30.4 %collective-permute-start.1 = (bf16[512,3072]{1,0:T(8,128)(2,1)}, bf16[512,3072]{1,0:T(8,128)(2,1)}, u32[]{:S(2)}, u32[]{:S(2)}) collective-permute-start(bf16[512,3072]{1,0:T(8,128)(2,1)} %all-gather.11.cloned.1.call-done), channel_id=1, source_target_pairs={{0,1},{1,0},{2,3},{3,2},{4,5},{5,4},{6,7},{7,6},{8,9},{9,8},{10,11... | collective-permute-start | bytes 9437192 | tf_op jit(solution)/shard_map/ppermute | solution.py:48
  176.4 92.1 %reduce-scatter.17.cloned.1.call-start = ((), (), s32[]{:S(2)}) async-start(), calls=%async_computation.17 | async-start | bytes 3932160 | tf_op jit(solution)/shard_map/reduce_scatter | solution.py:71
  176.5 22.7 %slice-start.3 = ((s8[9437184]{0:T(1024)(128)(4,1)}), s8[4194304]{0:T(1024)(128)(4,1)S(1)}, s32[]{:S(2)}) async-start(s8[9437184]{0:T(1024)(128)(4,1)} %bitcast.516), calls=%async_computation.29 | async-start | bytes 8388608
  176.5 22.7 %slice-start.4 = ((s8[9437184]{0:T(1024)(128)(4,1)}), s8[4194304]{0:T(1024)(128)(4,1)S(1)}, s32[]{:S(2)}) async-start(s8[9437184]{0:T(1024)(128)(4,1)} %bitcast.516), calls=%async_computation.30 | async-start | bytes 8388608
  205.7 18.6 %collective-permute-start.6 = (bf16[512,3072]{1,0:T(8,128)(2,1)}, bf16[512,3072]{1,0:T(8,128)(2,1)}, u32[]{:S(2)}, u32[]{:S(2)}) collective-permute-start(bf16[512,3072]{1,0:T(8,128)(2,1)} %fusion.152), channel_id=1, source_target_pairs={{0,1},{1,0},{2,3},{3,2},{4,5},{5,4},{6,7},{7,6},{8,9},{9,8},{10,11... | collective-permute-start | bytes 9437192 | tf_op jit(solution)/shard_map/ppermute | solution.py:48
  233.4 72.2 %reduce-scatter.11.cloned.1.call-start = ((), (), s32[]{:S(2)}) async-start(), calls=%async_computation.10 | async-start | bytes 3932160 | tf_op jit(solution)/shard_map/reduce_scatter | solution.py:71
  241.6 5.9 collective-permute-start.2
  258.0 88.1 %all-gather.15.cloned.1.call-start = ((), (), s32[]{:S(2)}) async-start(), calls=%async_computation.13 | async-start | bytes 3932160 | tf_op jit(solution)/shard_map/all_gather | solution.py:74
  310.1 124.2 %all-gather.21.cloned.1.call-start = ((), (), s32[]{:S(2)}) async-start(), calls=%async_computation.18 | async-start | bytes 3932160 | tf_op jit(solution)/shard_map/all_gather | solution.py:74
  346.1 6.2 collective-permute-start.4
  347.1 97.5 %reduce-scatter.21.cloned.1.call-start = ((), (), s32[]{:S(2)}) async-start(), calls=%async_computation.21 | async-start | bytes 3932160 | tf_op jit(solution)/shard_map/reduce_scatter | solution.py:71
  347.2 16.4 %copy-start.9 = (bf16[2,256,3072]{2,1,0:T(8,128)(2,1)S(1)}, bf16[2,256,3072]{2,1,0:T(8,128)(2,1)}, u32[]{:S(2)}) copy-start(bf16[2,256,3072]{2,1,0:T(8,128)(2,1)} %get-tuple-element.36) | copy-start | bytes 9437188
  352.4 22.7 %slice-start.6 = ((s8[9437184]{0:T(1024)(128)(4,1)}), s8[4194304]{0:T(1024)(128)(4,1)S(1)}, s32[]{:S(2)}) async-start(s8[9437184]{0:T(1024)(128)(4,1)} %bitcast.518), calls=%async_computation.32 | async-start | bytes 8388608
  352.4 22.7 %slice-start.7 = ((s8[9437184]{0:T(1024)(128)(4,1)}), s8[4194304]{0:T(1024)(128)(4,1)S(1)}, s32[]{:S(2)}) async-start(s8[9437184]{0:T(1024)(128)(4,1)} %bitcast.518), calls=%async_computation.33 | async-start | bytes 8388608
  381.5 19.1 %collective-permute-start.9 = (bf16[512,3072]{1,0:T(8,128)(2,1)}, bf16[512,3072]{1,0:T(8,128)(2,1)}, u32[]{:S(2)}, u32[]{:S(2)}) collective-permute-start(bf16[512,3072]{1,0:T(8,128)(2,1)} %fusion.155), channel_id=1, source_target_pairs={{0,1},{1,0},{2,3},{3,2},{4,5},{5,4},{6,7},{7,6},{8,9},{9,8},{10,11... | collective-permute-start | bytes 9437192 | tf_op jit(solution)/shard_map/ppermute | solution.py:48
  409.7 72.7 %reduce-scatter.15.cloned.1.call-start = ((), (), s32[]{:S(2)}) async-start(), calls=%async_computation.14 | async-start | bytes 3932160 | tf_op jit(solution)/shard_map/reduce_scatter | solution.py:71
  418.0 5.8 collective-permute-start.5
  434.3 88.0 %all-gather.25.cloned.1.call-start = ((), (), s32[]{:S(2)}) async-start(), calls=%async_computation.22 | async-start | bytes 3932160 | tf_op jit(solution)/shard_map/all_gather | solution.py:74
  434.4 52.1 %collective-permute-start.7 = (bf16[512,3072]{1,0:T(8,128)(2,1)}, bf16[512,3072]{1,0:T(8,128)(2,1)}, u32[]{:S(2)}, u32[]{:S(2)}) collective-permute-start(bf16[512,3072]{1,0:T(8,128)(2,1)} %all-gather.21.cloned.1.call-done), channel_id=1, source_target_pairs={{0,1},{1,0},{2,3},{3,2},{4,5},{5,4},{6,7},{7,6},{8,9},{9,8},{10,11... | collective-permute-start | bytes 9437192 | tf_op jit(solution)/shard_map/ppermute | solution.py:48
  486.2 112.3 %reduce-scatter.19.cloned.1.call-start = ((), (), s32[]{:S(2)}) async-start(), calls=%async_computation.19 | async-start | bytes 3932160 | tf_op jit(solution)/shard_map/reduce_scatter | solution.py:71
  511.2 27.7 %collective-permute-start.8 = (bf16[2,256,3072]{2,1,0:T(8,128)(2,1)}, bf16[2,256,3072]{2,1,0:T(8,128)(2,1)}, u32[]{:S(2)}, u32[]{:S(2)}) collective-permute-start(bf16[2,256,3072]{2,1,0:T(8,128)(2,1)} %bitcast_convert_fusion.2), channel_id=1, source_target_pairs={{0,1},{1,0},{2,3},{3,2},{4,5},{5,4},{6,7},{7,6},{8,9},{9,8},{10,11... | collective-permute-start | bytes 9437192 | tf_op jit(solution)/shard_map/ppermute | solution.py:48
  522.2 26.6 %collective-permute-start.10 = (bf16[512,3072]{1,0:T(8,128)(2,1)}, bf16[512,3072]{1,0:T(8,128)(2,1)}, u32[]{:S(2)}, u32[]{:S(2)}) collective-permute-start(bf16[512,3072]{1,0:T(8,128)(2,1)} %all-gather.25.cloned.1.call-done), channel_id=1, source_target_pairs={{0,1},{1,0},{2,3},{3,2},{4,5},{5,4},{6,7},{7,6},{8,9},{9,8},{10,11... | collective-permute-start | bytes 9437192 | tf_op jit(solution)/shard_map/ppermute | solution.py:48
  548.4 82.6 %reduce-scatter.23.cloned.1.call-start = ((), (), s32[]{:S(2)}) async-start(), calls=%async_computation.23 | async-start | bytes 3932160 | tf_op jit(solution)/shard_map/reduce_scatter | solution.py:71
  573.6 12.8 %collective-permute-start.11 = (bf16[2,256,3072]{2,1,0:T(8,128)(2,1)}, bf16[2,256,3072]{2,1,0:T(8,128)(2,1)}, u32[]{:S(2)}, u32[]{:S(2)}) collective-permute-start(bf16[2,256,3072]{2,1,0:T(8,128)(2,1)} %bitcast_convert_fusion.1), channel_id=1, source_target_pairs={{0,1},{1,0},{2,3},{3,2},{4,5},{5,4},{6,7},{7,6},{8,9},{9,8},{10,11... | collective-permute-start | bytes 9437192 | tf_op jit(solution)/shard_map/ppermute | solution.py:48
  595.7 35.3 %copy-start.46 = (f32[1,3072]{1,0:T(1,128)S(1)}, f32[1,3072]{1,0:T(1,128)}, u32[]{:S(2)}) copy-start(f32[1,3072]{1,0:T(1,128)} %param.9) | copy-start | bytes 36868
  595.7 35.3 %copy-start.54 = (f32[128]{0:T(128)S(1)}, f32[128]{0:T(128)}, u32[]{:S(2)}) copy-start(f32[128]{0:T(128)} %copy-done.53) | copy-start | bytes 1540
  595.8 39.2 %copy-start.11 = (bf16[128,3072]{1,0:T(8,128)(2,1)S(1)}, bf16[128,3072]{1,0:T(8,128)(2,1)}, u32[]{:S(2)}) copy-start(bf16[128,3072]{1,0:T(8,128)(2,1)} %get-tuple-element.44) | copy-start | bytes 2359300
  595.8 39.2 %copy-start.12 = (bf16[128,3072]{1,0:T(8,128)(2,1)S(1)}, bf16[128,3072]{1,0:T(8,128)(2,1)}, u32[]{:S(2)}) copy-start(bf16[128,3072]{1,0:T(8,128)(2,1)} %get-tuple-element.46) | copy-start | bytes 2359300
  595.8 72.6 %all-gather.13.cloned.1.call-start = ((), (), s32[]{:S(2)}) async-start(), calls=%async_computation.11 | async-start | bytes 3932160 | tf_op jit(solution)/shard_map/all_gather | solution.py:156
  596.6 109.6 %all-gather.17.cloned.1.call-start = ((), (), s32[]{:S(2)}) async-start(), calls=%async_computation.15 | async-start | bytes 3932160 | tf_op jit(solution)/shard_map/all_gather | solution.py:156
  597.3 189.1 %all-gather.23.cloned.1.call-start = ((), (), s32[]{:S(2)}) async-start(), calls=%async_computation.20 | async-start | bytes 3932160 | tf_op jit(solution)/shard_map/all_gather | solution.py:156
  598.6 36.5 %copy-start.14 = (bf16[128,3072]{1,0:T(8,128)(2,1)S(1)}, bf16[128,3072]{1,0:T(8,128)(2,1)}, u32[]{:S(2)}) copy-start(bf16[128,3072]{1,0:T(8,128)(2,1)} %reduce-scatter.19.cloned.1.call-done) | copy-start | bytes 2359300
  639.4 146.9 %all-gather.27.cloned.1.call-start = ((), (), s32[]{:S(2)}) async-start(), calls=%async_computation.24 | async-start | bytes 3932160 | tf_op jit(solution)/shard_map/all_gather | solution.py:156
  640.0 172.7 %all-gather.19.cloned.1.call-start = ((), (), s32[]{:S(2)}) async-start(), calls=%async_computation.16 | async-start | bytes 18874368 | tf_op jit(solution)/shard_map/all_gather | solution.py:157
  712.3 126.8 %all-gather.29.cloned.1.call-start = ((), (), s32[]{:S(2)}) async-start(), calls=%async_computation.25 | async-start | bytes 18874368 | tf_op jit(solution)/shard_map/all_gather | solution.py:157
  742.6 26.2 %copy-start.48 = (f32[3072]{0:T(1024)S(1)}, f32[3072]{0:T(1024)}, u32[]{:S(2)}) copy-start(f32[3072]{0:T(1024)} %get-tuple-element.18) | copy-start | bytes 36868
  742.6 26.2 %copy-start.49 = (f32[3072]{0:T(1024)S(1)}, f32[3072]{0:T(1024)}, u32[]{:S(2)}) copy-start(f32[3072]{0:T(1024)} %get-tuple-element.16) | copy-start | bytes 36868
  792.4 20.4 %copy-start.50 = (f32[3072]{0:T(1024)S(1)}, f32[3072]{0:T(1024)}, u32[]{:S(2)}) copy-start(f32[3072]{0:T(1024)} %get-tuple-element.14) | copy-start | bytes 36868
  792.4 20.4 %copy-start.51 = (f32[3072]{0:T(1024)S(1)}, f32[3072]{0:T(1024)}, u32[]{:S(2)}) copy-start(f32[3072]{0:T(1024)} %get-tuple-element.54) | copy-start | bytes 36868
  792.4 20.4 %copy-start.52 = (f32[3072]{0:T(1024)S(1)}, f32[3072]{0:T(1024)}, u32[]{:S(2)}) copy-start(f32[3072]{0:T(1024)} %add.276) | copy-start | bytes 36868
  (79 other events, 447.2 us)
Sparse Core Ops, SparseCore 0:
  68.8 37.1 reduce-scatter.8
  110.2 35.8 all-gather.10
  176.5 34.6 reduce-scatter.12
  233.5 34.9 reduce-scatter.16
  270.7 34.8 reduce-scatter.10
  310.3 35.8 all-gather.14
  347.7 36.3 all-gather.20
  409.8 34.7 reduce-scatter.20
  447.5 34.8 reduce-scatter.14
  486.4 35.8 all-gather.24
  548.5 34.6 reduce-scatter.18
  595.9 35.0 reduce-scatter.22
  632.5 35.8 all-gather.12
  669.8 36.3 all-gather.16
  708.2 36.3 all-gather.22
  746.1 36.3 all-gather.26
  784.5 25.9 all-gather.18
  812.5 26.5 all-gather.28

commit v2 on v0

v2 whole, which is shorter than its diff:
```python
import functools

import jax
import jax.numpy as jnp
from jax import lax
from jax.experimental import pallas as pl
from jax.experimental.pallas import tpu as pltpu
from jax.sharding import PartitionSpec as P

LN_EPS = 1e-5
CORES = 2
CHIPS = 4
BF = jnp.bfloat16
F32 = jnp.float32
MESH = pl.DeviceIdType.MESH
VMEM_BYTES = 67043328
GELU_C = 0.7978845608028654
GELU_K = 0.044715
SLOTS = 3

ORDER = (
    ('d1', 4), ('f4', 22), ('b3', 8), ('c3', 9), ('f1', 6), ('c4', 17), ('a4', 15), ('F1', 0), ('MY', 7),
    ('e3', 12), ('d4', 18), ('a3', 7), ('d3', 10), ('MU', 6), ('e1', 5), ('c1', 2), ('b1', 1), ('a1', 0),
    ('B2', 14), ('MD', 6), ('e4', 20), ('f3', 13), ('b4', 15),
)


def dg(a, b, ca, cb):
    return lax.dot_general(a, b, (((ca,), (cb,)), ((), ())), preferred_element_type=F32)


def ln_parts(z):
    mu = jnp.mean(z, axis=-1, keepdims=True)
    c = z - mu
    var = jnp.mean(c * c, axis=-1, keepdims=True)
    r = lax.rsqrt(var + LN_EPS)
    return c * r, r


def ln_bwd(z, gain, d):
    xhat, r = ln_parts(z)
    h = d * gain
    m1 = jnp.mean(h, axis=-1, keepdims=True)
    m2 = jnp.mean(h * xhat, axis=-1, keepdims=True)
    return r * (h - m1 - xhat * m2), jnp.sum(d * xhat, axis=0, keepdims=True)


def gelu_both(z):
    z2 = z * z
    t = jnp.tanh(GELU_C * (z + GELU_K * (z2 * z)))
    cdf = 0.5 * (1.0 + t)
    d = cdf + z * (0.5 * (1.0 - t * t)) * (GELU_C * (1.0 + (3.0 * GELU_K) * z2))
    return z * cdf, d


def tile_of(n, want):
    t = min(n, want)
    while n % t:
        t //= 2
    return t


def body(heads, x, dy, wqkv_h, wo_h, wu_h, wd_h, ga, gm,
         nm_o, g_o, dx_o, a_o, o_o, qkv_o, h_o, dp_o, dq_o, py_o, xm_o, dgain_o,
         wqkv, wo, wu, wd, S, RD, R1, R2, xb, ab, nb, dyb, gb, qb, qb2, dqb, dqt, ob, obt, hb_, dpb, pyb,
         xs, xm, gs, own, dgb, lsem, ssem, rsem):
    nseq, slen, dm = x.shape
    half = slen // CORES
    blk = half // CHIPS
    hb = blk // 2
    he = wo.shape[0]
    e = he // heads
    ff = wu.shape[1]
    scale = e ** -0.5
    tp = lax.axis_index('tp')
    chip = tp // CORES
    core = tp % CORES
    sib = chip * CORES + (1 - core)
    rchip = (chip + 1) % CHIPS
    lchip = (chip + CHIPS - 1) % CHIPS
    ochip = (chip + 2) % CHIPS
    right = rchip * CORES + core
    left = lchip * CORES + core

    def off(ch, co):
        return pl.multiple_of(co * half + ch * blk, blk)

    myoff = off(chip, core)

    def lc(src, dst, k):
        return pltpu.make_async_copy(src, dst, lsem.at[k])

    w1 = (lc(wqkv_h, wqkv, 0), lc(wo_h, wo, 1))
    w2 = (lc(wu_h, wu, 2), lc(wd_h, wd, 3))

    def ld_x(c):
        return lc(x.at[c], xb, 4)

    def ld_dy(c):
        return lc(dy.at[c], dyb, 5)

    def ld_nm(c):
        return lc(nm_o.at[c], nb, 6)

    def ld_g(c):
        return lc(g_o.at[c], gb, 7)

    def ld_q(c):
        return lc(qkv_o.at[c], qb2, 8)

    def st_a(c):
        return lc(ab, a_o.at[c], 9)

    def st_q(c):
        return lc(qb, qkv_o.at[c], 10)

    def st_o(c):
        return lc(ob, o_o.at[c], 11)

    def st_h(c):
        return lc(hb_, h_o.at[c], 12)

    def st_dp(c):
        return lc(dpb, dp_o.at[c], 13)

    def st_py(c):
        return lc(pyb, py_o.at[c], 14)

    def st_dq(c):
        return lc(dqb, dq_o.at[c], 15)

    xs_ld = lc(x.at[:, pl.ds(myoff, blk), :], xs, 16)
    dys_ld = lc(dy.at[:, pl.ds(myoff, blk), :], gs, 17)
    out_ref = {1: nm_o, 3: g_o, 4: dx_o}
    fset = {1: 0, 3: 1, 4: 0}

    def st_own(fl, c):
        return lc(own.at[fset[fl], c % 2], out_ref[fl].at[c, pl.ds(myoff, blk)], 19 + (fl // 2) * nseq + c)

    def rc(kind, fl, c, src, dst, dev):
        f = fl // 2
        return pltpu.make_async_remote_copy(
            src_ref=src, dst_ref=dst, send_sem=ssem.at[f, kind, c], recv_sem=rsem.at[f, kind, c],
            device_id={'tp': dev}, device_id_type=MESH)

    def c_pair(fl, c):
        f = fset[fl]
        return rc(0, fl, c, S.at[f, SLOTS], RD.at[f, c % SLOTS], sib)

    def rows(f, s, ch, second):
        return S.at[f, s, pl.ds(pl.multiple_of(ch * blk + second * hb, hb), hb)]

    def c_relay(fl, c, d):
        f, s = fset[fl], c % SLOTS
        return rc(1 + d, fl, c, rows(f, s, ochip, d), R1.at[f, s, d, 0], left if d else right)

    def c_direct(fl, c, d):
        f, s = fset[fl], c % SLOTS
        return rc(3 + d, fl, c, rows(f, s, lchip if d else rchip, 1 - d), R1.at[f, s, d, 1], left if d else right)

    def c_second(fl, c, d):
        f, s = fset[fl], c % SLOTS
        return rc(5 + d, fl, c, rows(f, s, lchip if d else rchip, d), R2.at[f, s, d], left if d else right)

    def c_own(fl, c, d):
        dev = (right, left, sib)[d]
        return rc(7 + d, fl, c, own.at[fset[fl], c % 2], out_ref[fl].at[c, pl.ds(myoff, blk)], dev)

    def c_fwd(fl, c, d):
        o = pl.multiple_of(off(rchip if d else lchip, core) + d * hb, hb)
        r = out_ref[fl].at[c, pl.ds(o, hb)]
        return rc(10 + d, fl, c, r, r, left if d else right)

    def c_cross(fl, c, d):
        o = off((lchip, rchip, ochip)[d], core)
        r = out_ref[fl].at[c, pl.ds(o, blk)]
        return rc(12 + d, fl, c, r, r, sib)

    def store_part(f, c, col, n, val):
        v = val.astype(BF)
        s = c % SLOTS
        i0 = s * (1 - core) + SLOTS * core
        i1 = s * core + SLOTS * (1 - core)
        S[f, i0, :, pl.ds(col, n)] = v[:half]
        S[f, i1, :, pl.ds(col, n)] = v[half:]

    def stage_a(fl, c):
        f, s = fset[fl], c % SLOTS
        c_pair(fl, c).wait_recv()
        c_pair(fl, c).wait_send()

        for st in {1: (st_a, st_q, st_o), 3: (st_h, st_dp), 4: (st_dq,)}[fl]:
            st(c).wait()

        def add(t, _):
            r = pl.ds(pl.multiple_of(t * hb, hb), hb)
            S[f, s, r] = (S[f, s, r].astype(F32) + RD[f, s, r].astype(F32)).astype(BF)
            return 0

        lax.fori_loop(0, half // hb, add, 0)
        for d in (0, 1):
            c_relay(fl, c, d).start()
        for d in (0, 1):
            c_direct(fl, c, d).start()

    def stage_b(fl, c):
        f, s = fset[fl], c % SLOTS
        for d in (0, 1):
            c_relay(fl, c, d).wait_recv()
        for d in (0, 1):
            o = pl.ds(pl.multiple_of((lchip if d else rchip) * blk + d * hb, hb), hb)
            S[f, s, o] = (S[f, s, o].astype(F32) + R1[f, s, d, 0].astype(F32)).astype(BF)
            c_second(fl, c, d).start()

    def stage_c(fl, c):
        f, s = fset[fl], c % SLOTS
        for d in (0, 1):
            c_direct(fl, c, d).wait_recv()
            c_second(fl, c, d).wait_recv()

        for k in (0, 1):
            q = pl.ds(k * hb, hb)
            o = pl.ds(pl.multiple_of(chip * blk + k * hb, hb), hb)
            tot = S[f, s, o].astype(F32) + R1[f, s, 1 - k, 1].astype(F32) + R2[f, s, k].astype(F32)
            if fl == 1:
                z = (xs[c, q].astype(F32) + tot).astype(BF)
                xm[c, q] = z
                xh, _ = ln_parts(z.astype(F32))
                own[f, c % 2, q] = (xh * gm[...]).astype(BF)
            elif fl == 3:
                dr, dgn = ln_bwd(xm[c, q].astype(F32), gm[...], tot)
                v = (gs[c, q].astype(F32) + dr).astype(BF)
                gs[c, q] = v
                own[f, c % 2, q] = v
                dgb[1:2] += dgn
            else:
                dr, dgn = ln_bwd(xs[c, q].astype(F32), ga[...], tot)
                own[f, c % 2, q] = (gs[c, q].astype(F32) + dr).astype(BF)
                dgb[0:1] += dgn
        for d in (0, 1, 2):
            c_own(fl, c, d).start()
        st_own(fl, c).start()
        for d in (0, 1):
            c_relay(fl, c, d).wait_send()
            c_direct(fl, c, d).wait_send()
            c_second(fl, c, d).wait_send()

    def stage_d(fl, c):
        for d in (1, 0):
            c_own(fl, c, 1 - d).wait_recv()
            c_fwd(fl, c, 1 - d).start()
        for d in (0, 1):
            c_cross(fl, c, d).start()
        for d in (0, 1, 2):
            c_own(fl, c, d).wait_send()
        st_own(fl, c).wait()

    def stage_e(fl, c):
        for d in (0, 1):
            c_fwd(fl, c, d).wait_recv()
        c_cross(fl, c, 2).start()

    def stage_f(fl, c):
        c_own(fl, c, 2).wait_recv()
        for d in (0, 1, 2):
            c_cross(fl, c, d).wait_recv()
        for d in (0, 1):
            c_fwd(fl, c, d).wait_send()
        for d in (0, 1, 2):
            c_cross(fl, c, d).wait_send()
        if fl == 1:
            ld_nm(c).start()
        if fl == 3:
            ld_g(c).start()

    def probs_t(q_ref, hd):
        qt = q_ref[pl.ds(pl.multiple_of(hd * e, e), e)]
        kt = q_ref[pl.ds(pl.multiple_of(he + hd * e, e), e)]
        vt = q_ref[pl.ds(pl.multiple_of(2 * he + hd * e, e), e)]
        s = dg(kt, qt, 0, 0) * scale
        keep = lax.broadcasted_iota(jnp.int32, (slen, slen), 0) <= lax.broadcasted_iota(jnp.int32, (slen, slen), 1)
        s = jnp.where(keep, s, -1e30)
        ex = jnp.exp(s - jnp.max(s, axis=0, keepdims=True))
        return qt, kt, vt, ex / jnp.sum(ex, axis=0, keepdims=True)

    def stage_F1(c):
        @pl.when(c == 0)
        def _():
            for w in w1:
                w.wait()
            xs_ld.wait()

        ld_x(c).wait()

        def ln(t, _):
            r = pl.ds(pl.multiple_of(t * hb, hb), hb)
            xh, _r = ln_parts(xb[r].astype(F32))
            ab[r] = (xh * ga[...]).astype(BF)
            return 0

        lax.fori_loop(0, slen // hb, ln, 0)
        st_a(c).start()

        @pl.when(c + 1 < nseq)
        def _():
            ld_x(c + 1).start()

        qt = tile_of(3 * he, 3 * he // 2)

        def qkv(t, _):
            r = pl.ds(pl.multiple_of(t * qt, qt), qt)
            qb[r] = dg(wqkv[r], ab[...], 1, 1).astype(BF)
            return 0

        lax.fori_loop(0, 3 * he // qt, qkv, 0)
        st_q(c).start()

        def head(hd, _):
            _q, _k, vt, p = probs_t(qb, hd)
            obt[pl.ds(pl.multiple_of(hd * e, e), e)] = dg(vt, p.astype(BF), 1, 0).astype(BF)
            return 0

        lax.fori_loop(0, heads, head, 0)
        tr = tile_of(he, 128)
        for t in range(he // tr):
            ob[:, t * tr:(t + 1) * tr] = obt[t * tr:(t + 1) * tr].T
        st_o(c).start()
        n = tile_of(dm, 1024)

        def proj(t, _):
            col = pl.multiple_of(t * n, n)
            store_part(0, c, col, n, dg(ob[...], wo[:, pl.ds(col, n)], 1, 0))
            return 0

        lax.fori_loop(0, dm // n, proj, 0)
        c_pair(1, c).start()

    def stage_MU(c):
        @pl.when(c == 0)
        def _():
            for w in w2:
                w.wait()
            dys_ld.wait()

        ld_nm(c).wait()
        ld_dy(c).wait()
        n = tile_of(ff, 512)

        def up(t, _):
            col = pl.ds(pl.multiple_of(t * n, n), n)
            pre = dg(nb[...], wu[:, col], 1, 0)
            dh = dg(dyb[...], wd[col], 1, 1)
            act, der = gelu_both(pre)
            hb_[:, col] = act.astype(BF)
            dpb[:, col] = (dh.astype(BF).astype(F32) * der).astype(BF)
            return 0

        lax.fori_loop(0, ff // n, up, 0)
        st_h(c).start()
        st_dp(c).start()

        @pl.when(c + 1 < nseq)
        def _():
            ld_dy(c + 1).start()

    m = tile_of(dm, 512)

    def stage_MD(c):
        def down(t, _):
            col = pl.multiple_of(t * m, m)
            store_part(1, c, col, m, dg(dpb[...], wu[pl.ds(col, m)], 1, 1))
            return 0

        lax.fori_loop(0, dm // m, down, 0)
        c_pair(3, c).start()

    def stage_MY(c):
        @pl.when(c > 0)
        def _():
            st_py(c - 1).wait()

        def outp(t, _):
            col = pl.multiple_of(t * m, m)
            pyb[:, pl.ds(col, m)] = dg(hb_[...], wd[:, pl.ds(col, m)], 1, 0).astype(BF)
            return 0

        lax.fori_loop(0, dm // m, outp, 0)
        st_py(c).start()

    def stage_B2(c):
        ld_q(c).start()
        ld_g(c).wait()
        obt[...] = dg(wo[...], gb[...], 1, 1).astype(BF)
        ld_q(c).wait()

        def head(hd, _):
            qt, kt, vt, p = probs_t(qb2, hd)
            do = obt[pl.ds(pl.multiple_of(hd * e, e), e)]
            dqt[pl.ds(pl.multiple_of(2 * he + hd * e, e), e)] = dg(do, p.astype(BF), 1, 1).astype(BF)
            dpr = dg(vt, do, 0, 0).astype(BF).astype(F32)
            ds = p * (dpr - jnp.sum(dpr * p, axis=0, keepdims=True))
            ds = (ds * scale).astype(BF)
            dqt[pl.ds(pl.multiple_of(hd * e, e), e)] = dg(kt, ds, 1, 0).astype(BF)
            dqt[pl.ds(pl.multiple_of(he + hd * e, e), e)] = dg(qt, ds, 1, 1).astype(BF)
            return 0

        lax.fori_loop(0, heads, head, 0)
        tr = tile_of(3 * he, 128)
        for t in range(3 * he // tr):
            dqb[:, t * tr:(t + 1) * tr] = dqt[t * tr:(t + 1) * tr].T
        st_dq(c).start()
        n = tile_of(dm, 512)

        def proj(t, _):
            col = pl.multiple_of(t * n, n)
            store_part(0, c, col, n, dg(dqb[...], wqkv[:, pl.ds(col, n)], 1, 0))
            return 0

        lax.fori_loop(0, dm // n, proj, 0)
        c_pair(4, c).start()

    barrier = pltpu.get_barrier_semaphore()
    for dev in (sib, left, right):
        pl.semaphore_signal(barrier, inc=1, device_id={'tp': dev}, device_id_type=MESH)
    ld_x(0).start()
    for w in w1:
        w.start()
    xs_ld.start()
    for w in w2:
        w.start()
    dys_ld.start()
    ld_dy(0).start()
    dgb[...] = jnp.zeros_like(dgb)
    pl.semaphore_wait(barrier, 3)

    run = {'F1': stage_F1, 'MU': stage_MU, 'MD': stage_MD, 'MY': stage_MY, 'B2': stage_B2}
    hops = {'a': stage_a, 'b': stage_b, 'c': stage_c, 'd': stage_d, 'e': stage_e, 'f': stage_f}
    order = ORDER

    def step(i, _):
        for name, lag in order:
            c = i - lag

            @pl.when((c >= 0) & (c < nseq))
            def _():
                if name in run:
                    run[name](c)
                else:
                    hops[name[0]](int(name[1]), c)
        return 0

    lax.fori_loop(0, nseq + max(l for _, l in order), step, 0)

    last = nseq - 1
    st_py(last).wait()
    xo = lc(xm, xm_o, 18)
    xo.start()
    dgain_o[...] = dgb[...]
    xo.wait()


def mega(x, dy, wqkv, wo, wu, wd, ga, gm, heads):
    nseq, slen, dm = x.shape
    he, ff = wo.shape[0], wu.shape[1]
    half = slen // CORES
    blk = half // CHIPS
    hb = blk // 2
    act = jax.ShapeDtypeStruct((nseq, slen, dm), BF)

    def arr(n, dt=BF):
        return jax.ShapeDtypeStruct((nseq, n, slen) if dt is None else (nseq, slen, n), BF)

    outs = (act, act, act, act, arr(he), jax.ShapeDtypeStruct((nseq, 3 * he, slen), BF), arr(ff), arr(ff), arr(3 * he), act,
            jax.ShapeDtypeStruct((nseq, blk, dm), BF), jax.ShapeDtypeStruct((2, dm), F32))
    hbm = pl.BlockSpec(memory_space=pl.ANY)
    vm = pl.BlockSpec(memory_space=pltpu.VMEM)
    V = pltpu.VMEM
    scratch = [
        V(wqkv.shape, BF), V(wo.shape, BF), V(wu.shape, BF), V(wd.shape, BF),
        V((2, SLOTS + 1, half, dm), BF), V((2, SLOTS, half, dm), BF),
        V((2, SLOTS, 2, 2, hb, dm), BF), V((2, SLOTS, 2, hb, dm), BF),
        V((slen, dm), BF), V((slen, dm), BF), V((slen, dm), BF), V((slen, dm), BF), V((slen, dm), BF),
        V((3 * he, slen), BF), V((3 * he, slen), BF), V((slen, 3 * he), BF), V((3 * he, slen), BF),
        V((slen, he), BF), V((he, slen), BF), V((slen, ff), BF), V((slen, ff), BF), V((slen, dm), BF),
        V((nseq, blk, dm), BF), V((nseq, blk, dm), BF), V((nseq, blk, dm), BF), V((2, 2, blk, dm), BF), V((2, dm), F32),
        pltpu.SemaphoreType.DMA((19 + 3 * nseq,)), pltpu.SemaphoreType.DMA((3, 15, nseq)), pltpu.SemaphoreType.DMA((3, 15, nseq)),
    ]
    flops = 2 * nseq * slen * dm * (4 * he * 2 + ff * 4)
    return pl.pallas_call(
        functools.partial(body, heads),
        name='mega',
        out_shape=outs,
        in_specs=[hbm] * 6 + [vm] * 2,
        out_specs=(hbm,) * 11 + (vm,),
        scratch_shapes=scratch,
        compiler_params=pltpu.CompilerParams(collective_id=0, has_side_effects=True, vmem_limit_bytes=VMEM_BYTES),
        cost_estimate=pl.CostEstimate(flops=flops, bytes_accessed=12 * nseq * slen * dm * 2, transcendentals=0),
    )(x, dy, wqkv, wo, wu, wd, ga, gm)


def solution(mesh):
    tpn = mesh.shape['tp']

    def hop(v, chips_by, cores_by):
        perm = []
        for t in range(tpn):
            ch, co = t // CORES, t % CORES
            perm.append((t, ((ch + chips_by) % CHIPS) * CORES + (co + cores_by) % CORES))
        return lax.ppermute(v, 'tp', perm)

    def reduce_and_gather(py, xm, chip, core):
        nseq, slen, dm = py.shape
        half = slen // CORES
        blk = half // CHIPS
        hb = blk // 2
        rchip, lchip, ochip = (chip + 1) % CHIPS, (chip + CHIPS - 1) % CHIPS, (chip + 2) % CHIPS

        def half_of(co):
            return lax.dynamic_slice_in_dim(py, co * half, half, axis=1)

        got = hop(half_of(1 - core), 0, 1)
        s = (half_of(core).astype(F32) + got.astype(F32)).astype(BF)

        def rows(ch, k):
            return lax.dynamic_slice_in_dim(s, ch * blk + k * hb, hb, axis=1)

        rel_l = hop(rows(ochip, 0), 1, 0)
        rel_r = hop(rows(ochip, 1), -1, 0)
        dir_l = hop(rows(rchip, 1), 1, 0)
        dir_r = hop(rows(lchip, 0), -1, 0)
        sec_l = hop((rows(rchip, 0).astype(F32) + rel_l.astype(F32)).astype(BF), 1, 0)
        sec_r = hop((rows(lchip, 1).astype(F32) + rel_r.astype(F32)).astype(BF), -1, 0)
        tot0 = rows(chip, 0).astype(F32) + dir_r.astype(F32) + sec_l.astype(F32)
        tot1 = rows(chip, 1).astype(F32) + dir_l.astype(F32) + sec_r.astype(F32)
        y = (xm.astype(F32) + jnp.concatenate([tot0, tot1], axis=1)).astype(BF)
        y_l, y_r = hop(y, 1, 0), hop(y, -1, 0)
        y_o = jnp.concatenate([hop(y_l[:, :hb], 1, 0), hop(y_r[:, hb:], -1, 0)], axis=1)
        out = jnp.zeros((nseq, half, dm), BF)
        for ch, v in ((chip, y), (lchip, y_l), (rchip, y_r), (ochip, y_o)):
            out = lax.dynamic_update_slice_in_dim(out, v, ch * blk, axis=1)
        other = hop(out, 0, 1)
        return jnp.where(core == 0, jnp.concatenate([out, other], axis=1), jnp.concatenate([other, out], axis=1))

    def step(x_in, gain_attn, w_qkv, w_out, gain_mlp, w_up, w_down, dy_out):
        nseq, slen, dm = x_in.shape
        heads, e = w_qkv.shape[3:]
        he = heads * e
        tp = lax.axis_index('tp')
        wqkv = jnp.transpose(w_qkv[0], (1, 2, 3, 0)).reshape(3 * he, dm)
        wo = w_out[0].reshape(he, dm)
        nm, g, dx, a, o, _qkv, h, dp, dq, py, xm, dgain = mega(
            x_in, dy_out, wqkv, wo, w_up[0], w_down[0], gain_attn, gain_mlp, heads)
        tok = nseq * slen

        def wg(p, q):
            return lax.dot_general(p.reshape(tok, -1), q.reshape(tok, -1), (((0,), (0,)), ((), ())),
                                   preferred_element_type=F32).astype(BF)

        y = reduce_and_gather(py, xm, tp // CORES, tp % CORES)
        dw_down = wg(h, dy_out)
        dw_up = wg(nm, dp)
        dw_out = wg(o, g)
        dw_qkv = wg(dq, a)
        dw_qkv = jnp.transpose(dw_qkv.reshape(3, heads, e, dm), (3, 0, 1, 2))
        dgain = lax.psum(dgain, 'tp')
        return (y, dx, dgain[0:1], dw_qkv[None], dw_out.reshape(1, heads, e, dm), dgain[1:2], dw_up[None], dw_down[None])

    act = P('dp', None, None)
    in_specs = (act, P(None, None), P(None, None, None, 'tp', None), P(None, 'tp', None, None), P(None, None),
                P(None, None, 'tp'), P(None, 'tp', None), act)
    out_specs = (act, act, P('dp', None), P('dp', None, None, 'tp', None), P('dp', 'tp', None, None), P('dp', None),
                 P('dp', None, 'tp'), P('dp', 'tp', None))
    return jax.shard_map(step, mesh=mesh, in_specs=in_specs, out_specs=out_specs, check_vma=False)
```

time: 891 us -> 599 us (0.67)
  Pallas kernels: 0 us -> 360 us
  waiting for transfers between devices: 409 us -> 72.2 us
  matrix products: 313 us -> 75.8 us
  other arithmetic: 145 us -> 25.8 us
  blocking collectives: 0 us -> 29.2 us
  local copies, waits for them, and re-layouts: 5.15 us -> 21.1 us
  between operations: 14.3 us -> 0.9 us
  starting transfers between devices: 0.19 us -> 13.1 us
    psum x3 -> x0, waiting for transfers between devices: 409 us -> none  [the longest x1 221 us: layer_forward(): mlp_sum = lax.psum(mlp_part, 'tp')]
    pallas_call x0 -> x1, Pallas kernels: none -> 360 us  [mega(): pl.pallas_call(functools.partial(body, heads), name='mega', out_shape=out...]
    dot_general x18 -> x4, matrix products: 313 us -> 75.8 us  [wg(): lax.dot_general(p.reshape(tok, -1), q.reshape(tok, -1), (((0,), (0,)), ((...]
    reduce_sum x8 -> x0, other arithmetic: 102 us -> none  [the longest x4 64.6 us: layer_norm(): return centered * lax.rsqrt(variance + LN_EPS) * gain_vec]
    ppermute x0 -> x12, waiting for transfers between devices: none -> 72.2 us  [hop(): return lax.ppermute(v, 'tp', perm)]
    convert_element_type x2, other arithmetic: 38.4 us -> 8.75 us  [the longest x1 7.43 us: reduce_and_gather(): s = (half_of(core).astype(F32) + got.astype(F32)).astype(BF)]
    psum x0 -> x1, blocking collectives: none -> 29.2 us  [step(): dgain = lax.psum(dgain, 'tp')]
    ppermute x0 -> x12, starting transfers between devices: none -> 13.1 us  [hop(): return lax.ppermute(v, 'tp', perm)]
  transfers between devices with their start and end apart: 3 -> 12, of which waited for: 3 -> 7; matrix products, arithmetic and copies ran while one was open for 14% -> 14% of each run, Pallas kernels for 0% -> 0%
where the time goes in v2:
time: 599 us; the launch traced here: 598 us
  Pallas kernels  360 us (60%)
  matrix products  75.8 us (13%)
  waiting for transfers between devices  72.2 us (12%)
  blocking collectives  29.2 us (5%)
  other arithmetic  25.8 us (4%)
  local copies, waits for them, and re-layouts  21.1 us (4%)
  starting transfers between devices  13.1 us (2%)
    pallas_call x1, Pallas kernels, mega(): pl.pallas_call(functools.partial(body, heads), name='mega', out_shape=out...  360 us
    dot_general x4, matrix products, wg(): lax.dot_general(p.reshape(tok, -1), q.reshape(tok, -1), (((0,), (0,)), ((...  75.8 us
    ppermute x12, waiting for transfers between devices, hop(): return lax.ppermute(v, 'tp', perm)  72.2 us
    psum x1, blocking collectives, step(): dgain = lax.psum(dgain, 'tp')  29.2 us
    ppermute x12, starting transfers between devices, hop(): return lax.ppermute(v, 'tp', perm)  13.1 us
  transfers between devices with their start and end apart: 12, of which 7 were waited for; matrix products, arithmetic and copies ran while one was open for 14% of the time, Pallas kernels for 0%

profile of v2, /device:TPU:81, one launch (start us, length us, event | category | flops | bytes accessed | tf_op | source)
XLA Modules:
  0.0 598.5 jit_solution(15034216125286993854)
XLA Ops:
  0.7 360.3 %mega.1 = (bf16[8,256,3072]{2,1,0:T(8,128)(2,1)}, bf16[8,256,3072]{2,1,0:T(8,128)(2,1)}, bf16[8,256,3072]{2,1,0:T(8,128)(2,1)}, bf16[8,256,3072]{2,1,0:T(8,128)(...) custom-call(bf16[8,256,3072]{2,1,0:T(8,128)(2,1)} %x.1, ...), custom_call_target="tpu_custom_call" | custom-call | flops 115964116992 | bytes 150994944 | tf_op jit(solution)/shard_map/mega/pallas_call | solution.py:489
  361.0 5.9 constant_dynamic-slice_fusion.4
  366.9 0.2 collective-permute-start
  367.1 9.9 %collective-permute-done = bf16[8,128,3072]{2,1,0:T(8,128)(2,1)} collective-permute-done((bf16[8,128,3072]{2,1,0:T(8,128)(2,1)}, bf16[8,128,3072]{2,1,0:T(8,128)(2,1)}, u32[]{:S(2)}, u32[]{:S(2)}) %collective-permute-start) | collective-permute-done | bytes 6291488 | tf_op jit(solution)/shard_map/ppermute | solution.py:509
  377.0 7.4 %add_convert_fusion = bf16[8,128,3072]{2,1,0:T(8,128)(2,1)S(1)} fusion(bf16[8,128,3072]{2,1,0:T(8,128)(2,1)} %collective-permute-done, bf16[8,256,3072]{2,1,0:T(8,128)(2,1)} %get-tuple-element.20, s32[]{:T(128)S(6)} %select_n.67), kind=kLoop, calls=%fused_computation.4 | loop fusion | flops 12582912 | bytes 18874372 | tf_op jit(solution)/shard_map/convert_element_type | solution.py:522
  384.5 0.0 copy-start.1
  384.5 2.7 copy-done.1
  387.2 1.7 constant_dynamic-slice_fusion.3
  388.9 0.3 collective-permute-start.2
  389.2 2.4 collective-permute-start.1
  391.6 0.3 collective-permute-start.5
  391.9 17.1 %collective-permute-done.2 = bf16[8,16,3072]{2,1,0:T(8,128)(2,1)S(1)} collective-permute-done((bf16[8,16,3072]{2,1,0:T(8,128)(2,1)}, bf16[8,16,3072]{2,1,0:T(8,128)(2,1)S(1)}, u32[]{:S(2)}, u32[]{:S(2)}) %collective-permute-start.2) | collective-permute-done | bytes 786464 | tf_op jit(solution)/shard_map/ppermute | solution.py:509
  409.0 1.3 add_convert_fusion.2
  410.3 0.1 collective-permute-start.3
  410.5 0.8 collective-permute-start.4
  411.3 0.0 collective-permute-done.1
  411.3 14.1 %collective-permute-done.5 = bf16[8,16,3072]{2,1,0:T(8,128)(2,1)S(1)} collective-permute-done((bf16[8,16,3072]{2,1,0:T(8,128)(2,1)}, bf16[8,16,3072]{2,1,0:T(8,128)(2,1)S(1)}, u32[]{:S(2)}, u32[]{:S(2)}) %collective-permute-start.5) | collective-permute-done | bytes 786464 | tf_op jit(solution)/shard_map/ppermute | solution.py:509
  425.4 4.4 collective-permute-done.3
  429.8 3.1 convert_add_fusion.1
  432.9 13.7 %collective-permute-done.4 = bf16[8,16,3072]{2,1,0:T(8,128)(2,1)} collective-permute-done((bf16[8,16,3072]{2,1,0:T(8,128)(2,1)}, bf16[8,16,3072]{2,1,0:T(8,128)(2,1)}, u32[]{:S(2)}, u32[]{:S(2)}) %collective-permute-start.4) | collective-permute-done | bytes 786464 | tf_op jit(solution)/shard_map/ppermute | solution.py:509
  446.6 2.2 collective-permute-done.6
  448.8 2.1 convert_add_fusion
  450.9 0.8 broadcast_in_dim.12
  451.7 0.6 constant_dynamic-update-slice_fusion.2
  452.3 0.0 copy-start
  452.3 0.1 collective-permute-start.7
  452.4 2.6 collective-permute-start.8
  455.1 0.0 slice-start.7
  455.1 19.6 %bitcast_convert_fusion.2 = bf16[1152,3072]{1,0:T(8,128)(2,1)} fusion(bf16[8,256,1152]{2,1,0:T(8,128)(2,1)S(1)} %bitcast.51, bf16[8,256,3072]{2,1,0:T(8,128)(2,1)} %get-tuple-element.24), kind=kOutput, calls=%fused_computation.2 | convolution fusion | flops 14499053568 | bytes 24379392 | tf_op jit(solution)/shard_map/dot_general | solution.py:556
  474.8 10.8 %collective-permute-done.7 = bf16[8,32,3072]{2,1,0:T(8,128)(2,1)S(1)} collective-permute-done((bf16[8,32,3072]{2,1,0:T(8,128)(2,1)S(1)}, bf16[8,32,3072]{2,1,0:T(8,128)(2,1)S(1)}, u32[]{:S(2)}, u32[]{:S(2)}) %collective-permute-start.7) | collective-permute-done | bytes 1572896 | tf_op jit(solution)/shard_map/ppermute | solution.py:509
  485.5 1.0 slice.16
  486.5 1.0 slice.17
  487.4 2.7 collective-permute-start.10
  490.1 6.4 %bitcast_convert_fusion.3 = bf16[384,3072]{1,0:T(8,128)(2,1)} fusion(bf16[8,256,384]{2,1,0:T(8,128)(2,1)S(1)} %copy-done.4, bf16[8,256,3072]{2,1,0:T(8,128)(2,1)S(1)} %bitcast.49), kind=kOutput, calls=%fused_computation.7 | convolution fusion | flops 4833017856 | bytes 16515072 | tf_op jit(solution)/shard_map/dot_general | solution.py:556
  496.5 29.2 %psum.7 = f32[2,3072]{1,0:T(2,128)S(1)} all-reduce(f32[2,3072]{1,0:T(2,128)S(1)} %copy-done.3), channel_id=1, replica_groups=mesh['dp'=4,'tp'=8] {'tp'}, use_global_device_ids=true, to_apply=%region_0.1 | all-reduce | flops 6144 | bytes 49152 | tf_op jit(solution)/shard_map/psum | solution.py:565
  525.7 1.3 constant_dynamic-update-slice_fusion.1
  527.0 1.3 constant_dynamic-update-slice_fusion
  528.3 2.8 maximum_dynamic-update-slice_fusion
  531.1 3.5 collective-permute-start.11
  534.7 0.6 fusion.4
  535.3 25.9 %fusion.1 = bf16[1,1536,3072]{2,1,0:T(8,128)(2,1)} fusion(bf16[8,256,1536]{2,1,0:T(8,128)(2,1)} %get-tuple-element.29, bf16[8,256,3072]{2,1,0:T(8,128)(2,1)} %dy.1), kind=kOutput, calls=%fused_computation.6 | convolution fusion | flops 19332071424 | bytes 28311552 | tf_op jit(solution)/shard_map/dot_general | solution.py:556
  561.2 0.0 slice-start.1
  561.2 0.0 slice-start.3
  561.2 0.0 slice-start.4
  561.2 23.9 %fusion = bf16[1,3072,1536]{2,1,0:T(8,128)(2,1)} fusion(bf16[8,256,3072]{2,1,0:T(8,128)(2,1)} %get-tuple-element.27, bf16[8,256,1536]{2,1,0:T(8,128)(2,1)S(1)} %bitcast.53), kind=kOutput, calls=%fused_computation.5 | convolution fusion | flops 19332071424 | bytes 28311552 | tf_op jit(solution)/shard_map/dot_general | solution.py:556
  585.1 0.0 collective-permute-done.11
  585.1 8.5 %maximum_select_fusion = bf16[8,256,3072]{2,1,0:T(8,128)(2,1)} fusion(bf16[8,128,3072]{2,1,0:T(8,128)(2,1)S(1)} %collective-permute-done.11, bf16[8,128,3072]{2,1,0:T(8,128)(2,1)S(1)} %bitcast.39, pred[]{:T(512)S(6)} %eq.8), kind=kLoop, calls=%fused_computation.3 | loop fusion | flops 56623104 | bytes 25165824 | tf_op jit(solution)/shard_map/jit(_where)/select_n | solution.py:542
  593.7 4.8 copy.29
  (37 shorter events, 0.1 us)
Async XLA Ops:
  366.9 10.1 %collective-permute-start = (bf16[8,128,3072]{2,1,0:T(8,128)(2,1)}, bf16[8,128,3072]{2,1,0:T(8,128)(2,1)}, u32[]{:S(2)}, u32[]{:S(2)}) collective-permute-start(bf16[8,128,3072]{2,1,0:T(8,128)(2,1)} %constant_dynamic-slice_fusion.4), channel_id=1, source_target_pairs={{0,1},{1,0},{2,3},{3,2},{4,5},{5,4},{6,7},{7,6},{8,9},{9,8},{10,11... | collective-permute-start | bytes 18874376 | tf_op jit(solution)/shard_map/ppermute | solution.py:509
  384.5 2.7 copy-start.1
  388.9 20.1 %collective-permute-start.2 = (bf16[8,16,3072]{2,1,0:T(8,128)(2,1)}, bf16[8,16,3072]{2,1,0:T(8,128)(2,1)S(1)}, u32[]{:S(2)}, u32[]{:S(2)}) collective-permute-start(bf16[8,16,3072]{2,1,0:T(8,128)(2,1)} %get-tuple-element.37), channel_id=1, source_target_pairs={{0,2},{1,3},{2,4},{3,5},{4,6},{5,7},{6,0},{7,1},{8,10},{9,11},{10,... | collective-permute-start | bytes 2359304 | tf_op jit(solution)/shard_map/ppermute | solution.py:509
  389.2 22.1 %collective-permute-start.1 = (bf16[8,16,3072]{2,1,0:T(8,128)(2,1)}, bf16[8,16,3072]{2,1,0:T(8,128)(2,1)S(1)}, u32[]{:S(2)}, u32[]{:S(2)}) collective-permute-start(bf16[8,16,3072]{2,1,0:T(8,128)(2,1)} %get-tuple-element.34), channel_id=1, source_target_pairs={{0,6},{1,7},{2,0},{3,1},{4,2},{5,3},{6,4},{7,5},{8,14},{9,15},{10,... | collective-permute-start | bytes 2359304 | tf_op jit(solution)/shard_map/ppermute | solution.py:509
  391.6 33.8 %collective-permute-start.5 = (bf16[8,16,3072]{2,1,0:T(8,128)(2,1)}, bf16[8,16,3072]{2,1,0:T(8,128)(2,1)S(1)}, u32[]{:S(2)}, u32[]{:S(2)}) collective-permute-start(bf16[8,16,3072]{2,1,0:T(8,128)(2,1)} %get-tuple-element.35), channel_id=1, source_target_pairs={{0,6},{1,7},{2,0},{3,1},{4,2},{5,3},{6,4},{7,5},{8,14},{9,15},{10,... | collective-permute-start | bytes 2359304 | tf_op jit(solution)/shard_map/ppermute | solution.py:509
  410.3 19.5 %collective-permute-start.3 = (bf16[8,16,3072]{2,1,0:T(8,128)(2,1)S(1)}, bf16[8,16,3072]{2,1,0:T(8,128)(2,1)}, u32[]{:S(2)}, u32[]{:S(2)}) collective-permute-start(bf16[8,16,3072]{2,1,0:T(8,128)(2,1)S(1)} %add_convert_fusion.2), channel_id=1, source_target_pairs={{0,2},{1,3},{2,4},{3,5},{4,6},{5,7},{6,0},{7,1},{8,10},{9,11},{10,... | collective-permute-start | bytes 2359304 | tf_op jit(solution)/shard_map/ppermute | solution.py:509
  410.5 36.2 %collective-permute-start.4 = (bf16[8,16,3072]{2,1,0:T(8,128)(2,1)}, bf16[8,16,3072]{2,1,0:T(8,128)(2,1)}, u32[]{:S(2)}, u32[]{:S(2)}) collective-permute-start(bf16[8,16,3072]{2,1,0:T(8,128)(2,1)} %get-tuple-element.36), channel_id=1, source_target_pairs={{0,2},{1,3},{2,4},{3,5},{4,6},{5,7},{6,0},{7,1},{8,10},{9,11},{10,... | collective-permute-start | bytes 2359304 | tf_op jit(solution)/shard_map/ppermute | solution.py:509
  432.9 18.8 %copy-start.2 = (bf16[8,32,3072]{2,1,0:T(8,128)(2,1)S(1)}, bf16[8,32,3072]{2,1,0:T(8,128)(2,1)}, u32[]{:S(2)}) copy-start(bf16[8,32,3072]{2,1,0:T(8,128)(2,1)} %get-tuple-element.19) | copy-start | bytes 4718596
  432.9 15.9 %collective-permute-start.6 = (bf16[8,16,3072]{2,1,0:T(8,128)(2,1)}, bf16[8,16,3072]{2,1,0:T(8,128)(2,1)}, u32[]{:S(2)}, u32[]{:S(2)}) collective-permute-start(bf16[8,16,3072]{2,1,0:T(8,128)(2,1)} %get-tuple-element.33), channel_id=1, source_target_pairs={{0,6},{1,7},{2,0},{3,1},{4,2},{5,3},{6,4},{7,5},{8,14},{9,15},{10,... | collective-permute-start | bytes 2359304 | tf_op jit(solution)/shard_map/ppermute | solution.py:509
  448.8 6.3 %slice-start.8 = ((s8[4718592]{0:T(1024)(128)(4,1)}), s8[4194304]{0:T(1024)(128)(4,1)S(1)}, s32[]{:S(2)}) async-start(s8[4718592]{0:T(1024)(128)(4,1)} %bitcast.50), calls=%async_computation.8 | async-start | bytes 8388608
  450.9 4.2 slice-start.9
  451.7 38.4 %slice-start.5 = ((s8[12582912]{0:T(1024)(128)(4,1)}), s8[4194304]{0:T(1024)(128)(4,1)S(1)}, s32[]{:S(2)}) async-start(s8[12582912]{0:T(1024)(128)(4,1)} %bitcast.48), calls=%async_computation.5 | async-start | bytes 8388608
  452.3 22.5 %copy-start = (bf16[8,128,3072]{2,1,0:T(8,128)(2,1)}, bf16[8,128,3072]{2,1,0:T(8,128)(2,1)S(1)}, u32[]{:S(2)}) copy-start(bf16[8,128,3072]{2,1,0:T(8,128)(2,1)S(1)} %get-tuple-element.30) | copy-start | bytes 18874372
  452.3 33.2 %collective-permute-start.7 = (bf16[8,32,3072]{2,1,0:T(8,128)(2,1)S(1)}, bf16[8,32,3072]{2,1,0:T(8,128)(2,1)S(1)}, u32[]{:S(2)}, u32[]{:S(2)}) collective-permute-start(bf16[8,32,3072]{2,1,0:T(8,128)(2,1)S(1)} %get-tuple-element.31), channel_id=1, source_target_pairs={{0,2},{1,3},{2,4},{3,5},{4,6},{5,7},{6,0},{7,1},{8,10},{9,11},{10,... | collective-permute-start | bytes 4718600 | tf_op jit(solution)/shard_map/ppermute | solution.py:509
  452.4 34.1 %collective-permute-start.8 = (bf16[8,32,3072]{2,1,0:T(8,128)(2,1)S(1)}, bf16[8,32,3072]{2,1,0:T(8,128)(2,1)S(1)}, u32[]{:S(2)}, u32[]{:S(2)}) collective-permute-start(bf16[8,32,3072]{2,1,0:T(8,128)(2,1)S(1)} %get-tuple-element.31), channel_id=1, source_target_pairs={{0,6},{1,7},{2,0},{3,1},{4,2},{5,3},{6,4},{7,5},{8,14},{9,15},{10,... | collective-permute-start | bytes 4718600 | tf_op jit(solution)/shard_map/ppermute | solution.py:509
  455.1 35.0 %slice-start.6 = ((s8[12582912]{0:T(1024)(128)(4,1)}), s8[4194304]{0:T(1024)(128)(4,1)S(1)}, s32[]{:S(2)}) async-start(s8[12582912]{0:T(1024)(128)(4,1)} %bitcast.48), calls=%async_computation.6 | async-start | bytes 8388608
  455.1 35.0 %slice-start.7 = ((s8[12582912]{0:T(1024)(128)(4,1)}), s8[4194304]{0:T(1024)(128)(4,1)S(1)}, s32[]{:S(2)}) async-start(s8[12582912]{0:T(1024)(128)(4,1)} %bitcast.48), calls=%async_computation.7 | async-start | bytes 8388608
  455.1 35.0 %copy-start.4 = (bf16[8,256,384]{2,1,0:T(8,128)(2,1)S(1)}, bf16[8,256,384]{2,1,0:T(8,128)(2,1)}, u32[]{:S(2)}) copy-start(bf16[8,256,384]{2,1,0:T(8,128)(2,1)} %get-tuple-element.25) | copy-start | bytes 4718596
  486.5 41.9 %collective-permute-start.9 = (bf16[8,16,3072]{2,1,0:T(8,128)(2,1)}, bf16[8,16,3072]{2,1,0:T(8,128)(2,1)}, u32[]{:S(2)}, u32[]{:S(2)}) collective-permute-start(bf16[8,16,3072]{2,1,0:T(8,128)(2,1)} %slice.16), channel_id=1, source_target_pairs={{0,2},{1,3},{2,4},{3,5},{4,6},{5,7},{6,0},{7,1},{8,10},{9,11},{10,... | collective-permute-start | bytes 2359304 | tf_op jit(solution)/shard_map/ppermute | solution.py:509
  487.4 40.9 %collective-permute-start.10 = (bf16[8,16,3072]{2,1,0:T(8,128)(2,1)}, bf16[8,16,3072]{2,1,0:T(8,128)(2,1)}, u32[]{:S(2)}, u32[]{:S(2)}) collective-permute-start(bf16[8,16,3072]{2,1,0:T(8,128)(2,1)} %slice.17), channel_id=1, source_target_pairs={{0,6},{1,7},{2,0},{3,1},{4,2},{5,3},{6,4},{7,5},{8,14},{9,15},{10,... | collective-permute-start | bytes 2359304 | tf_op jit(solution)/shard_map/ppermute | solution.py:509
  490.1 6.4 %copy-start.3 = (f32[2,3072]{1,0:T(2,128)S(1)}, f32[2,3072]{1,0:T(2,128)}, u32[]{:S(2)}) copy-start(f32[2,3072]{1,0:T(2,128)} %get-tuple-element.22) | copy-start | bytes 73732
  528.3 32.9 %slice-start.10 = ((s8[6291456]{0:T(1024)(128)(4,1)}), s8[4194304]{0:T(1024)(128)(4,1)S(1)}, s32[]{:S(2)}) async-start(s8[6291456]{0:T(1024)(128)(4,1)} %bitcast.52), calls=%async_computation.10 | async-start | bytes 8388608
  531.1 54.0 %collective-permute-start.11 = (bf16[8,128,3072]{2,1,0:T(8,128)(2,1)}, bf16[8,128,3072]{2,1,0:T(8,128)(2,1)S(1)}, u32[]{:S(2)}, u32[]{:S(2)}) collective-permute-start(bf16[8,128,3072]{2,1,0:T(8,128)(2,1)} %maximum_dynamic-update-slice_fusion), channel_id=1, source_target_pairs={{0,1},{1,0},{2,3},{3,2},{4,5},{5,4},{6,7},{7,6},{8,9},{9,8},{10,11... | collective-permute-start | bytes 18874376 | tf_op jit(solution)/shard_map/ppermute | solution.py:509
  535.3 25.9 %slice-start.11 = ((s8[6291456]{0:T(1024)(128)(4,1)}), s8[2097152]{0:T(1024)(128)(4,1)S(1)}, s32[]{:S(2)}) async-start(s8[6291456]{0:T(1024)(128)(4,1)} %bitcast.52), calls=%async_computation.11 | async-start | bytes 4194304
  535.3 49.8 %slice-start = ((s8[6291456]{0:T(1024)(128)(4,1)}), s8[4194304]{0:T(1024)(128)(4,1)S(1)}, s32[]{:S(2)}) async-start(s8[6291456]{0:T(1024)(128)(4,1)} %bitcast.38), calls=%async_computation | async-start | bytes 8388608
  561.2 32.5 %slice-start.2 = ((s8[12582912]{0:T(1024)(128)(4,1)}), s8[4194304]{0:T(1024)(128)(4,1)S(1)}, s32[]{:S(2)}) async-start(s8[12582912]{0:T(1024)(128)(4,1)} %bitcast.40), calls=%async_computation.2 | async-start | bytes 8388608
  561.2 23.9 %slice-start.1 = ((s8[6291456]{0:T(1024)(128)(4,1)}), s8[2097152]{0:T(1024)(128)(4,1)S(1)}, s32[]{:S(2)}) async-start(s8[6291456]{0:T(1024)(128)(4,1)} %bitcast.38), calls=%async_computation.1 | async-start | bytes 4194304
  561.2 32.4 %slice-start.3 = ((s8[12582912]{0:T(1024)(128)(4,1)}), s8[4194304]{0:T(1024)(128)(4,1)S(1)}, s32[]{:S(2)}) async-start(s8[12582912]{0:T(1024)(128)(4,1)} %bitcast.40), calls=%async_computation.3 | async-start | bytes 8388608
  561.2 32.4 %slice-start.4 = ((s8[12582912]{0:T(1024)(128)(4,1)}), s8[4194304]{0:T(1024)(128)(4,1)S(1)}, s32[]{:S(2)}) async-start(s8[12582912]{0:T(1024)(128)(4,1)} %bitcast.40), calls=%async_computation.4 | async-start | bytes 8388608

commit v3 on v2

--- a/solution.py
+++ b/solution.py
@@ -1,4 +1,5 @@
 import functools
+import math
 
 import jax
 import jax.numpy as jnp
@@ -19,9 +20,10 @@
 SLOTS = 3
 
 ORDER = (
-    ('d1', 4), ('f4', 22), ('b3', 8), ('c3', 9), ('f1', 6), ('c4', 17), ('a4', 15), ('F1', 0), ('MY', 7),
-    ('e3', 12), ('d4', 18), ('a3', 7), ('d3', 10), ('MU', 6), ('e1', 5), ('c1', 2), ('b1', 1), ('a1', 0),
-    ('B2', 14), ('MD', 6), ('e4', 20), ('f3', 13), ('b4', 15),
+    ('e5', 27), ('f1', 6), ('c3', 9), ('c1', 3), ('b5', 23), ('b1', 2), ('b3', 8), ('a3', 7), ('f3', 14),
+    ('e3', 13), ('d3', 10), ('MU', 6), ('a1', 1), ('c5', 24), ('a5', 22), ('d4', 19), ('c4', 17), ('YL', 21),
+    ('d5', 25), ('f5', 28), ('e4', 22), ('MD', 6), ('b4', 16), ('d1', 4), ('e1', 5), ('F1', 0), ('YS', 21),
+    ('a4', 15), ('WG', 22), ('MY', 6), ('f4', 23), ('B2', 14),
 )
 
 
@@ -60,11 +62,12 @@
     return t
 
 
-def body(heads, x, dy, wqkv_h, wo_h, wu_h, wd_h, ga, gm,
-         nm_o, g_o, dx_o, a_o, o_o, qkv_o, h_o, dp_o, dq_o, py_o, xm_o, dgain_o,
+def body(heads, x, dy, dyf, wqkv_h, wo_h, wu_h, wd_h, ga, gm,
+         y_o, dx_o, dwq_o, dwo_o, dwu_o, dwd_o, nm_o, g_o, a_o, o_o, qkv_o, h_o, dp_o, dq_o, py_o, dgain_o,
          wqkv, wo, wu, wd, S, RD, R1, R2, xb, ab, nb, dyb, gb, qb, qb2, dqb, dqt, ob, obt, hb_, dpb, pyb,
-         xs, xm, gs, own, dgb, lsem, ssem, rsem):
+         xs, xm, gs, own, dgb, dgs, lsem, wsem, dsem, ssem, rsem):
     nseq, slen, dm = x.shape
+    tok = nseq * slen
     half = slen // CORES
     blk = half // CHIPS
     hb = blk // 2
@@ -72,6 +75,7 @@
     e = he // heads
     ff = wu.shape[1]
     scale = e ** -0.5
+    tpn = CHIPS * CORES
     tp = lax.axis_index('tp')
     chip = tp // CORES
     core = tp % CORES
@@ -82,6 +86,9 @@
     right = rchip * CORES + core
     left = lchip * CORES + core
 
+    def seq(c):
+        return pl.ds(pl.multiple_of(c * slen, slen), slen)
+
     def off(ch, co):
         return pl.multiple_of(co * half + ch * blk, blk)
 
@@ -100,45 +107,49 @@
         return lc(dy.at[c], dyb, 5)
 
     def ld_nm(c):
-        return lc(nm_o.at[c], nb, 6)
+        return lc(nm_o.at[seq(c)], nb, 6)
 
     def ld_g(c):
-        return lc(g_o.at[c], gb, 7)
+        return lc(g_o.at[seq(c)], gb, 7)
 
     def ld_q(c):
         return lc(qkv_o.at[c], qb2, 8)
 
     def st_a(c):
-        return lc(ab, a_o.at[c], 9)
+        return lc(ab, a_o.at[seq(c)], 9)
 
     def st_q(c):
         return lc(qb, qkv_o.at[c], 10)
 
     def st_o(c):
-        return lc(ob, o_o.at[c], 11)
+        return lc(ob, o_o.at[seq(c)], 11)
 
     def st_h(c):
-        return lc(hb_, h_o.at[c], 12)
+        return lc(hb_, h_o.at[seq(c)], 12)
 
     def st_dp(c):
-        return lc(dpb, dp_o.at[c], 13)
+        return lc(dpb, dp_o.at[seq(c)], 13)
 
     def st_py(c):
-        return lc(pyb, py_o.at[c], 14)
+        return lc(pyb, py_o.at[seq(c)], 14)
 
     def st_dq(c):
-        return lc(dqb, dq_o.at[c], 15)
+        return lc(dqb, dq_o.at[seq(c)], 15)
 
     xs_ld = lc(x.at[:, pl.ds(myoff, blk), :], xs, 16)
     dys_ld = lc(dy.at[:, pl.ds(myoff, blk), :], gs, 17)
-    out_ref = {1: nm_o, 3: g_o, 4: dx_o}
-    fset = {1: 0, 3: 1, 4: 0}
+    out_ref = {1: nm_o, 3: g_o, 4: dx_o, 5: y_o}
+    fset = {1: 0, 3: 1, 4: 0, 5: 1}
+    semset = {1: 0, 3: 1, 4: 2, 5: 3}
+
+    def out_rows(fl, c, o, n):
+        return out_ref[fl].at[pl.ds(pl.multiple_of(c * slen + o, n), n)]
 
     def st_own(fl, c):
-        return lc(own.at[fset[fl], c % 2], out_ref[fl].at[c, pl.ds(myoff, blk)], 19 + (fl // 2) * nseq + c)
+        return lc(own.at[fset[fl], c % 2], out_rows(fl, c, myoff, blk), 21 + semset[fl] * nseq + c)
 
     def rc(kind, fl, c, src, dst, dev):
-        f = fl // 2
+        f = semset[fl]
         return pltpu.make_async_remote_copy(
             src_ref=src, dst_ref=dst, send_sem=ssem.at[f, kind, c], recv_sem=rsem.at[f, kind, c],
             device_id={'tp': dev}, device_id_type=MESH)
@@ -164,17 +175,20 @@
 
     def c_own(fl, c, d):
         dev = (right, left, sib)[d]
-        return rc(7 + d, fl, c, own.at[fset[fl], c % 2], out_ref[fl].at[c, pl.ds(myoff, blk)], dev)
+        return rc(7 + d, fl, c, own.at[fset[fl], c % 2], out_rows(fl, c, myoff, blk), dev)
 
     def c_fwd(fl, c, d):
-        o = pl.multiple_of(off(rchip if d else lchip, core) + d * hb, hb)
-        r = out_ref[fl].at[c, pl.ds(o, hb)]
+        r = out_rows(fl, c, off(rchip if d else lchip, core) + d * hb, hb)
         return rc(10 + d, fl, c, r, r, left if d else right)
 
     def c_cross(fl, c, d):
-        o = off((lchip, rchip, ochip)[d], core)
-        r = out_ref[fl].at[c, pl.ds(o, blk)]
+        r = out_rows(fl, c, off((lchip, rchip, ochip)[d], core), blk)
         return rc(12 + d, fl, c, r, r, sib)
+
+    def c_gain(k):
+        return pltpu.make_async_remote_copy(
+            src_ref=dgb, dst_ref=dgs.at[tp], send_sem=dsem.at[0, k], recv_sem=dsem.at[1, k],
+            device_id={'tp': (tp + k) % tpn}, device_id_type=MESH)
 
     def store_part(f, c, col, n, val):
         v = val.astype(BF)
@@ -189,7 +203,7 @@
         c_pair(fl, c).wait_recv()
         c_pair(fl, c).wait_send()
 
-        for st in {1: (st_a, st_q, st_o), 3: (st_h, st_dp), 4: (st_dq,)}[fl]:
+        for st in {1: (st_a, st_q, st_o), 3: (st_h, st_dp), 4: (st_dq,), 5: ()}[fl]:
             st(c).wait()
 
         def add(t, _):
@@ -233,6 +247,8 @@
                 gs[c, q] = v
                 own[f, c % 2, q] = v
                 dgb[1:2] += dgn
+            elif fl == 5:
+                own[f, c % 2, q] = (xm[c, q].astype(F32) + tot).astype(BF)
             else:
                 dr, dgn = ln_bwd(xs[c, q].astype(F32), ga[...], tot)
                 own[f, c % 2, q] = (gs[c, q].astype(F32) + dr).astype(BF)
@@ -244,6 +260,12 @@
             c_relay(fl, c, d).wait_send()
             c_direct(fl, c, d).wait_send()
             c_second(fl, c, d).wait_send()
+        if fl == 4:
+            @pl.when(c == nseq - 1)
+            def _():
+                dgs[tp] = dgb[...]
+                for k in range(1, tpn):
+                    c_gain(k).start()
 
     def stage_d(fl, c):
         for d in (1, 0):
@@ -388,6 +410,12 @@
         st_py(c).start()
 
     def stage_B2(c):
+        @pl.when(c == nseq - 1)
+        def _():
+            start_a(0)
+            for k in (0, 1):
+                b_load(0, k).start()
+
         ld_q(c).start()
         ld_g(c).wait()
         obt[...] = dg(wo[...], gb[...], 1, 1).astype(BF)
@@ -419,9 +447,112 @@
         lax.fori_loop(0, dm // n, proj, 0)
         c_pair(4, c).start()
 
+    def y_loads(c):
+        s = c % SLOTS
+
+        def part(co):
+            return py_o.at[pl.ds(pl.multiple_of(c * slen + co * half, half), half)]
+
+        return lc(part(1 - core), S.at[1, SLOTS], 19), lc(part(core), S.at[1, s], 20)
+
+    def stage_YL(c):
+        @pl.when(c == nseq - 1)
+        def _():
+            st_py(c).wait()
+
+        for cp in y_loads(c):
+            cp.start()
+
+    def stage_YS(c):
+        for cp in y_loads(c):
+            cp.wait()
+        c_pair(5, c).start()
+
+    kh = tok // 2
+    gemms = []
+    for lhs, rhs, res in ((nm_o, dp_o, dwu_o), (h_o, dyf, dwd_o), (dq_o, a_o, dwq_o), (o_o, g_o, dwo_o)):
+        for cb in range(rhs.shape[1] // ff):
+            gemms.append((lhs, rhs, res, lhs.shape[1] // he, cb * ff))
+    first = [sum(g[3] for g in gemms[:p]) for p in range(len(gemms) + 1)]
+    tiles = first[-1]
+
+    def a_buf(b, k):
+        return wd.at[pl.ds(0, kh), pl.ds(pl.multiple_of((2 * b + k) * he, he), he)]
+
+    def b_buf(p, k):
+        return wqkv.at[pl.ds(0, kh), pl.ds(k * ff, ff)] if p % 2 else wu.at[pl.ds(k * kh, kh)]
+
+    def o_buf(b):
+        return wu.at[pl.ds(pl.multiple_of(tok + b * he, math.gcd(tok, he)), he)]
+
+    def a_load(p, w, k):
+        col = pl.multiple_of((w - first[p]) * he, he)
+        return pltpu.make_async_copy(gemms[p][0].at[pl.ds(k * kh, kh), pl.ds(col, he)], a_buf(w % 2, k), wsem.at[k, w % 2])
+
+    def b_load(p, k):
+        return pltpu.make_async_copy(gemms[p][1].at[pl.ds(k * kh, kh), pl.ds(gemms[p][4], ff)], b_buf(p, k), wsem.at[2 + k, p % 2])
+
+    def o_store(p, w):
+        row = pl.multiple_of((w - first[p]) * he, he)
+        return pltpu.make_async_copy(o_buf(w % 2), gemms[p][2].at[pl.ds(row, he), pl.ds(gemms[p][4], ff)], wsem.at[4, w % 2])
+
+    def in_gemm(p, w):
+        return (w >= first[p]) & (w < first[p + 1])
+
+    def start_a(w):
+        for p in range(len(gemms)):
+            @pl.when(in_gemm(p, w))
+            def _():
+                for k in (0, 1):
+                    a_load(p, w, k).start()
+
+    def tile(w):
+        for k in (0, 1):
+            a_load(0, w % 2, k).wait()
+        start_a(w + 1)
+        for p in range(len(gemms)):
+            @pl.when(w == first[p])
+            def _():
+                for k in (0, 1):
+                    b_load(p, k).wait()
+                if p + 1 < len(gemms):
+                    for k in (0, 1):
+                        b_load(p + 1, k).start()
+
+        @pl.when(w >= 2)
+        def _():
+            o_store(0, w % 2).wait()
+
+        n = tile_of(ff, 512)
+        for odd in (0, 1):
+            sel = functools.reduce(lambda u, v: u | v, [in_gemm(p, w) for p in range(len(gemms)) if p % 2 == odd])
+
+            @pl.when(sel)
+            def _():
+                for j in range(ff // n):
+                    acc = None
+                    for k in (0, 1):
+                        t = dg(a_buf(w % 2, k)[...], b_buf(odd, k)[:, pl.ds(j * n, n)], 0, 0)
+                        acc = t if acc is None else acc + t
+                    o_buf(w % 2)[:, pl.ds(j * n, n)] = acc.astype(BF)
+
+        for p in range(len(gemms)):
+            @pl.when(in_gemm(p, w))
+            def _():
+                o_store(p, w).start()
+
+    def stage_WG(c):
+        per = tiles // nseq
+
+        def one(j, _):
+            tile(c * per + j)
+            return 0
+
+        lax.fori_loop(0, per, one, 0)
+
     barrier = pltpu.get_barrier_semaphore()
-    for dev in (sib, left, right):
-        pl.semaphore_signal(barrier, inc=1, device_id={'tp': dev}, device_id_type=MESH)
+    for k in range(1, tpn):
+        pl.semaphore_signal(barrier, inc=1, device_id={'tp': (tp + k) % tpn}, device_id_type=MESH)
     ld_x(0).start()
     for w in w1:
         w.start()
@@ -431,9 +562,10 @@
     dys_ld.start()
     ld_dy(0).start()
     dgb[...] = jnp.zeros_like(dgb)
-    pl.semaphore_wait(barrier, 3)
-
-    run = {'F1': stage_F1, 'MU': stage_MU, 'MD': stage_MD, 'MY': stage_MY, 'B2': stage_B2}
+    pl.semaphore_wait(barrier, tpn - 1)
+
+    run = {'F1': stage_F1, 'MU': stage_MU, 'MD': stage_MD, 'MY': stage_MY, 'B2': stage_B2,
+           'YL': stage_YL, 'YS': stage_YS, 'WG': stage_WG}
     hops = {'a': stage_a, 'b': stage_b, 'c': stage_c, 'd': stage_d, 'e': stage_e, 'f': stage_f}
     order = ORDER
 
@@ -451,12 +583,16 @@
 
     lax.fori_loop(0, nseq + max(l for _, l in order), step, 0)
 
-    last = nseq - 1
-    st_py(last).wait()
-    xo = lc(xm, xm_o, 18)
-    xo.start()
-    dgain_o[...] = dgb[...]
-    xo.wait()
+    for b in (0, 1):
+        o_store(0, b).wait()
+    for k in range(1, tpn):
+        c_gain(k).wait_recv()
+    tot = dgs[0]
+    for t in range(1, tpn):
+        tot = tot + dgs[t]
+    dgain_o[...] = tot
+    for k in range(1, tpn):
+        c_gain(k).wait_send()
 
 
 def mega(x, dy, wqkv, wo, wu, wd, ga, gm, heads):
@@ -465,13 +601,14 @@
     half = slen // CORES
     blk = half // CHIPS
     hb = blk // 2
-    act = jax.ShapeDtypeStruct((nseq, slen, dm), BF)
-
-    def arr(n, dt=BF):
-        return jax.ShapeDtypeStruct((nseq, n, slen) if dt is None else (nseq, slen, n), BF)
-
-    outs = (act, act, act, act, arr(he), jax.ShapeDtypeStruct((nseq, 3 * he, slen), BF), arr(ff), arr(ff), arr(3 * he), act,
-            jax.ShapeDtypeStruct((nseq, blk, dm), BF), jax.ShapeDtypeStruct((2, dm), F32))
+    tok = nseq * slen
+
+    def arr(*shape):
+        return jax.ShapeDtypeStruct(shape, BF)
+
+    act = arr(tok, dm)
+    outs = (act, act, arr(3 * he, dm), arr(he, dm), arr(dm, ff), arr(ff, dm), act, act, act, arr(tok, he),
+            arr(nseq, 3 * he, slen), arr(tok, ff), arr(tok, ff), arr(tok, 3 * he), act, jax.ShapeDtypeStruct((2, dm), F32))
     hbm = pl.BlockSpec(memory_space=pl.ANY)
     vm = pl.BlockSpec(memory_space=pltpu.VMEM)
     V = pltpu.VMEM
@@ -483,87 +620,38 @@
         V((3 * he, slen), BF), V((3 * he, slen), BF), V((slen, 3 * he), BF), V((3 * he, slen), BF),
         V((slen, he), BF), V((he, slen), BF), V((slen, ff), BF), V((slen, ff), BF), V((slen, dm), BF),
         V((nseq, blk, dm), BF), V((nseq, blk, dm), BF), V((nseq, blk, dm), BF), V((2, 2, blk, dm), BF), V((2, dm), F32),
-        pltpu.SemaphoreType.DMA((19 + 3 * nseq,)), pltpu.SemaphoreType.DMA((3, 15, nseq)), pltpu.SemaphoreType.DMA((3, 15, nseq)),
+        V((CHIPS * CORES, 2, dm), F32),
+        pltpu.SemaphoreType.DMA((21 + 4 * nseq,)), pltpu.SemaphoreType.DMA((5, 2)), pltpu.SemaphoreType.DMA((2, CHIPS * CORES)),
+        pltpu.SemaphoreType.DMA((4, 15, nseq)), pltpu.SemaphoreType.DMA((4, 15, nseq)),
     ]
     flops = 2 * nseq * slen * dm * (4 * he * 2 + ff * 4)
     return pl.pallas_call(
         functools.partial(body, heads),
         name='mega',
         out_shape=outs,
-        in_specs=[hbm] * 6 + [vm] * 2,
-        out_specs=(hbm,) * 11 + (vm,),
+        in_specs=[hbm] * 7 + [vm] * 2,
+        out_specs=(hbm,) * 15 + (vm,),
         scratch_shapes=scratch,
         compiler_params=pltpu.CompilerParams(collective_id=0, has_side_effects=True, vmem_limit_bytes=VMEM_BYTES),
         cost_estimate=pl.CostEstimate(flops=flops, bytes_accessed=12 * nseq * slen * dm * 2, transcendentals=0),
-    )(x, dy, wqkv, wo, wu, wd, ga, gm)
+    )(x, dy, dy.reshape(tok, dm), wqkv, wo, wu, wd, ga, gm)
 
 
 def solution(mesh):
-    tpn = mesh.shape['tp']
-
-    def hop(v, chips_by, cores_by):
-        perm = []
-        for t in range(tpn):
-            ch, co = t // CORES, t % CORES
-            perm.append((t, ((ch + chips_by) % CHIPS) * CORES + (co + cores_by) % CORES))
-        return lax.ppermute(v, 'tp', perm)
-
-    def reduce_and_gather(py, xm, chip, core):
-        nseq, slen, dm = py.shape
-        half = slen // CORES
-        blk = half // CHIPS
-        hb = blk // 2
-        rchip, lchip, ochip = (chip + 1) % CHIPS, (chip + CHIPS - 1) % CHIPS, (chip + 2) % CHIPS
-
-        def half_of(co):
-            return lax.dynamic_slice_in_dim(py, co * half, half, axis=1)
-
-        got = hop(half_of(1 - core), 0, 1)
-        s = (half_of(core).astype(F32) + got.astype(F32)).astype(BF)
-
-        def rows(ch, k):
-            return lax.dynamic_slice_in_dim(s, ch * blk + k * hb, hb, axis=1)
-
-        rel_l = hop(rows(ochip, 0), 1, 0)
-        rel_r = hop(rows(ochip, 1), -1, 0)
-        dir_l = hop(rows(rchip, 1), 1, 0)
-        dir_r = hop(rows(lchip, 0), -1, 0)
-        sec_l = hop((rows(rchip, 0).astype(F32) + rel_l.astype(F32)).astype(BF), 1, 0)
-        sec_r = hop((rows(lchip, 1).astype(F32) + rel_r.astype(F32)).astype(BF), -1, 0)
-        tot0 = rows(chip, 0).astype(F32) + dir_r.astype(F32) + sec_l.astype(F32)
-        tot1 = rows(chip, 1).astype(F32) + dir_l.astype(F32) + sec_r.astype(F32)
-        y = (xm.astype(F32) + jnp.concatenate([tot0, tot1], axis=1)).astype(BF)
-        y_l, y_r = hop(y, 1, 0), hop(y, -1, 0)
-        y_o = jnp.concatenate([hop(y_l[:, :hb], 1, 0), hop(y_r[:, hb:], -1, 0)], axis=1)
-        out = jnp.zeros((nseq, half, dm), BF)
-        for ch, v in ((chip, y), (lchip, y_l), (rchip, y_r), (ochip, y_o)):
-            out = lax.dynamic_update_slice_in_dim(out, v, ch * blk, axis=1)
-        other = hop(out, 0, 1)
-        return jnp.where(core == 0, jnp.concatenate([out, other], axis=1), jnp.concatenate([other, out], axis=1))
+    assert mesh.shape['tp'] == CHIPS * CORES
 
     def step(x_in, gain_attn, w_qkv, w_out, gain_mlp, w_up, w_down, dy_out):
-        nseq, slen, dm = x_in.shape
         heads, e = w_qkv.shape[3:]
+        dm = x_in.shape[2]
         he = heads * e
-        tp = lax.axis_index('tp')
         wqkv = jnp.transpose(w_qkv[0], (1, 2, 3, 0)).reshape(3 * he, dm)
         wo = w_out[0].reshape(he, dm)
-        nm, g, dx, a, o, _qkv, h, dp, dq, py, xm, dgain = mega(
-            x_in, dy_out, wqkv, wo, w_up[0], w_down[0], gain_attn, gain_mlp, heads)
-        tok = nseq * slen
-
-        def wg(p, q):
-            return lax.dot_general(p.reshape(tok, -1), q.reshape(tok, -1), (((0,), (0,)), ((), ())),
-                                   preferred_element_type=F32).astype(BF)
-
-        y = reduce_and_gather(py, xm, tp // CORES, tp % CORES)
-        dw_down = wg(h, dy_out)
-        dw_up = wg(nm, dp)
-        dw_out = wg(o, g)
-        dw_qkv = wg(dq, a)
-        dw_qkv = jnp.transpose(dw_qkv.reshape(3, heads, e, dm), (3, 0, 1, 2))
-        dgain = lax.psum(dgain, 'tp')
-        return (y, dx, dgain[0:1], dw_qkv[None], dw_out.reshape(1, heads, e, dm), dgain[1:2], dw_up[None], dw_down[None])
+        out = mega(x_in, dy_out, wqkv, wo, w_up[0], w_down[0], gain_attn, gain_mlp, heads)
+        y, dx, dwq, dwo, dwu, dwd = out[:6]
+        dgain = out[-1]
+        dwq = jnp.transpose(dwq.reshape(3, heads, e, dm), (3, 0, 1, 2))
+        return (y.reshape(x_in.shape), dx.reshape(x_in.shape), dgain[0:1], dwq[None], dwo.reshape(1, heads, e, dm),
+                dgain[1:2], dwu[None], dwd[None])
 
     act = P('dp', None, None)
     in_specs = (act, P(None, None), P(None, None, None, 'tp', None), P(None, 'tp', None, None), P(None, None),

time: 599 us -> 517 us (0.86)
  Pallas kernels: 360 us -> 474 us
  matrix products: 75.8 us -> 0 us
  waiting for transfers between devices: 72.2 us -> 0 us
  blocking collectives: 29.2 us -> 0 us
  other arithmetic: 25.8 us -> 0.01 us
  local copies, waits for them, and re-layouts: 21.1 us -> 41.4 us
  starting transfers between devices: 13.1 us -> 0 us
    pallas_call x1, Pallas kernels: 360 us -> 474 us  [mega(): pl.pallas_call(functools.partial(body, heads), name='mega', out_shape=out...]
    dot_general x4 -> x0, matrix products: 75.8 us -> none  [wg(): lax.dot_general(p.reshape(tok, -1), q.reshape(tok, -1), (((0,), (0,)), ((...]
    ppermute x12 -> x0, waiting for transfers between devices: 72.2 us -> none  [hop(): return lax.ppermute(v, 'tp', perm)]
    unnamed x35 -> x14, local copies, waits for them, and re-layouts: 7.55 us -> 40 us
    psum x1 -> x0, blocking collectives: 29.2 us -> none  [step(): dgain = lax.psum(dgain, 'tp')]
    ppermute x12 -> x0, starting transfers between devices: 13.1 us -> none  [hop(): return lax.ppermute(v, 'tp', perm)]
    convert_element_type x2 -> x0, other arithmetic: 8.75 us -> none  [the longest x1 7.43 us: reduce_and_gather(): s = (half_of(core).astype(F32) + got.astype(F32)).astype(BF)]
    select_n x1 -> x0, other arithmetic: 8.53 us -> none  [reduce_and_gather(): jnp.where(core == 0, jnp.concatenate([out, other], axis=1), jnp.concatena...]
  transfers between devices with their start and end apart: 12 -> 0, of which waited for: 7 -> 0; matrix products, arithmetic and copies ran while one was open for 14% -> 0% of each run, Pallas kernels for 0% -> 0%
where the time goes in v3:
time: 517 us; the launch traced here: 516 us
  Pallas kernels  474 us (92%)
  local copies, waits for them, and re-layouts  41.4 us (8%)
    pallas_call x1, Pallas kernels, mega(): pl.pallas_call(functools.partial(body, heads), name='mega', out_shape=out...  474 us
    unnamed x14, local copies, waits for them, and re-layouts  40 us

profile of v3, /device:TPU:81, one launch (start us, length us, event | category | flops | bytes accessed | tf_op | source)
XLA Modules:
  0.0 515.6 jit_solution(7063554253163200085)
XLA Ops:
  0.6 473.5 %mega.1 = (bf16[2048,3072]{1,0:T(8,128)(2,1)}, bf16[2048,3072]{1,0:T(8,128)(2,1)}, bf16[1152,3072]{1,0:T(8,128)(2,1)}, bf16[384,3072]{1,0:T(8,128)(2,1)}, bf16[3...) custom-call(bf16[8,256,3072]{2,1,0:T(8,128)(2,1)} %x.1, ...), custom_call_target="tpu_custom_call" | custom-call | flops 115964116992 | bytes 150994944 | tf_op jit(solution)/shard_map/mega/pallas_call | solution.py:628
  474.2 1.4 fusion
  475.6 0.0 copy-start
  475.6 0.0 slice-start
  475.6 12.4 %copy.22 = bf16[8,256,3072]{2,1,0:T(8,128)(2,1)} copy(bf16[8,256,3072]{2,1,0:T(8,128)(2,1)} %bitcast.20) | data formatting | bytes 25165824
  488.0 0.0 copy-done
  488.0 0.0 slice-start.1
  488.0 6.0 %copy.23 = bf16[8,256,3072]{2,1,0:T(8,128)(2,1)} copy(bf16[8,256,3072]{2,1,0:T(8,128)(2,1)S(1)} %bitcast.19) | data formatting | bytes 25165824
  494.1 0.0 slice-done
  494.1 0.4 slice-done.1
  494.5 0.0 copy-start.1
  494.5 3.2 copy.24
  497.7 0.2 copy-done.1
  497.9 1.4 copy.25
  499.3 8.0 %copy.26 = bf16[1,3072,1536]{2,1,0:T(8,128)(2,1)} copy(bf16[1,3072,1536]{2,1,0:T(8,128)(2,1)} %bitcast.22) | data formatting | bytes 18874368
  507.3 8.3 %copy.27 = bf16[1,1536,3072]{2,1,0:T(8,128)(2,1)} copy(bf16[1,1536,3072]{2,1,0:T(8,128)(2,1)} %bitcast.21) | data formatting | bytes 18874368
  (1 shorter events, 0.0 us)
Async XLA Ops:
  475.6 12.4 %copy-start = (bf16[2048,3072]{1,0:T(8,128)(2,1)S(1)}, bf16[2048,3072]{1,0:T(8,128)(2,1)}, u32[]{:S(2)}) copy-start(bf16[2048,3072]{1,0:T(8,128)(2,1)} %get-tuple-element.16) | copy-start | bytes 37748740
  475.6 18.4 %slice-start = ((s8[7077888]{0:T(1024)(128)(4,1)}), s8[4194304]{0:T(1024)(128)(4,1)S(1)}, s32[]{:S(2)}) async-start(s8[7077888]{0:T(1024)(128)(4,1)} %bitcast.23), calls=%async_computation | async-start | bytes 8388608
  488.0 6.5 %slice-start.1 = ((s8[7077888]{0:T(1024)(128)(4,1)}), s8[2883584]{0:T(1024)(128)(4,1)S(1)}, s32[]{:S(2)}) async-start(s8[7077888]{0:T(1024)(128)(4,1)} %bitcast.23), calls=%async_computation.1 | async-start | bytes 5767168
  494.5 3.4 copy-start.1

commit v4 on v3

--- a/solution.py
+++ b/solution.py
@@ -18,12 +18,13 @@
 GELU_C = 0.7978845608028654
 GELU_K = 0.044715
 SLOTS = 3
+PAIRS = 2
 
 ORDER = (
-    ('e5', 27), ('f1', 6), ('c3', 9), ('c1', 3), ('b5', 23), ('b1', 2), ('b3', 8), ('a3', 7), ('f3', 14),
-    ('e3', 13), ('d3', 10), ('MU', 6), ('a1', 1), ('c5', 24), ('a5', 22), ('d4', 19), ('c4', 17), ('YL', 21),
-    ('d5', 25), ('f5', 28), ('e4', 22), ('MD', 6), ('b4', 16), ('d1', 4), ('e1', 5), ('F1', 0), ('YS', 21),
-    ('a4', 15), ('WG', 22), ('MY', 6), ('f4', 23), ('B2', 14),
+    ('a3', 8), ('a5', 21), ('MU', 7), ('d3', 11), ('c4', 17), ('f4', 21), ('B2', 15), ('b4', 16), ('b1', 2),
+    ('d5', 24), ('a4', 15), ('e1', 6), ('a1', 1), ('YL', 20), ('MD', 7), ('d1', 4), ('f3', 14), ('c3', 9),
+    ('d4', 18), ('WG', 22), ('c5', 22), ('f1', 6), ('e5', 25), ('F1', 0), ('c1', 2), ('MY', 7), ('b5', 21),
+    ('b3', 8), ('e4', 19), ('f5', 29), ('YS', 20), ('e3', 13),
 )
 
 
@@ -65,7 +66,7 @@
 def body(heads, x, dy, dyf, wqkv_h, wo_h, wu_h, wd_h, ga, gm,
          y_o, dx_o, dwq_o, dwo_o, dwu_o, dwd_o, nm_o, g_o, a_o, o_o, qkv_o, h_o, dp_o, dq_o, py_o, dgain_o,
          wqkv, wo, wu, wd, S, RD, R1, R2, xb, ab, nb, dyb, gb, qb, qb2, dqb, dqt, ob, obt, hb_, dpb, pyb,
-         xs, xm, gs, own, dgb, dgs, lsem, wsem, dsem, ssem, rsem):
+         xs, xm, gs, own, dgb, dgs, lsem, wsem, dsem, ysem, ssem1, rsem1, ssem, rsem):
     nseq, slen, dm = x.shape
     tok = nseq * slen
     half = slen // CORES
@@ -140,50 +141,48 @@
     dys_ld = lc(dy.at[:, pl.ds(myoff, blk), :], gs, 17)
     out_ref = {1: nm_o, 3: g_o, 4: dx_o, 5: y_o}
     fset = {1: 0, 3: 1, 4: 0, 5: 1}
-    semset = {1: 0, 3: 1, 4: 2, 5: 3}
 
     def out_rows(fl, c, o, n):
         return out_ref[fl].at[pl.ds(pl.multiple_of(c * slen + o, n), n)]
 
     def st_own(fl, c):
-        return lc(own.at[fset[fl], c % 2], out_rows(fl, c, myoff, blk), 21 + semset[fl] * nseq + c)
+        return lc(own.at[fset[fl], c % 2], out_rows(fl, c, myoff, blk), 19 + fset[fl] * 2 + c % 2)
 
     def rc(kind, fl, c, src, dst, dev):
-        f = semset[fl]
+        f = fset[fl]
+        if kind < 5:
+            send, recv = ssem1.at[f, kind * SLOTS + c], rsem1.at[f, kind * SLOTS + c]
+        else:
+            send, recv = (m.at[f, (kind - 5) * nseq + c] for m in (ssem, rsem))
         return pltpu.make_async_remote_copy(
-            src_ref=src, dst_ref=dst, send_sem=ssem.at[f, kind, c], recv_sem=rsem.at[f, kind, c],
+            src_ref=src, dst_ref=dst, send_sem=send, recv_sem=recv,
             device_id={'tp': dev}, device_id_type=MESH)
 
     def c_pair(fl, c):
         f = fset[fl]
-        return rc(0, fl, c, S.at[f, SLOTS], RD.at[f, c % SLOTS], sib)
-
-    def rows(f, s, ch, second):
-        return S.at[f, s, pl.ds(pl.multiple_of(ch * blk + second * hb, hb), hb)]
-
-    def c_relay(fl, c, d):
+        return rc(0, fl, c % PAIRS, S.at[f, SLOTS], RD.at[f, c % PAIRS], sib)
+
+    def c_first(fl, c, d):
         f, s = fset[fl], c % SLOTS
-        return rc(1 + d, fl, c, rows(f, s, ochip, d), R1.at[f, s, d, 0], left if d else right)
-
-    def c_direct(fl, c, d):
-        f, s = fset[fl], c % SLOTS
-        return rc(3 + d, fl, c, rows(f, s, lchip if d else rchip, 1 - d), R1.at[f, s, d, 1], left if d else right)
+        src = S.at[f, s, pl.ds(blk + hb if d else hb, blk)]
+        return rc(1 + d, fl, c % SLOTS, src, R1.at[f, s, d], left if d else right)
 
     def c_second(fl, c, d):
         f, s = fset[fl], c % SLOTS
-        return rc(5 + d, fl, c, rows(f, s, lchip if d else rchip, d), R2.at[f, s, d], left if d else right)
+        src = S.at[f, s, pl.ds(2 * blk + hb if d else 0, hb)]
+        return rc(3 + d, fl, c % SLOTS, src, R2.at[f, s, d], left if d else right)
 
     def c_own(fl, c, d):
         dev = (right, left, sib)[d]
-        return rc(7 + d, fl, c, own.at[fset[fl], c % 2], out_rows(fl, c, myoff, blk), dev)
+        return rc(5 + d, fl, c, own.at[fset[fl], c % 2], out_rows(fl, c, myoff, blk), dev)
 
     def c_fwd(fl, c, d):
         r = out_rows(fl, c, off(rchip if d else lchip, core) + d * hb, hb)
-        return rc(10 + d, fl, c, r, r, left if d else right)
+        return rc(8 + d, fl, c, r, r, left if d else right)
 
     def c_cross(fl, c, d):
         r = out_rows(fl, c, off((lchip, rchip, ochip)[d], core), blk)
-        return rc(12 + d, fl, c, r, r, sib)
+        return rc(10 + d, fl, c, r, r, sib)
 
     def c_gain(k):
         return pltpu.make_async_remote_copy(
@@ -195,47 +194,45 @@
         s = c % SLOTS
         i0 = s * (1 - core) + SLOTS * core
         i1 = s * core + SLOTS * (1 - core)
-        S[f, i0, :, pl.ds(col, n)] = v[:half]
-        S[f, i1, :, pl.ds(col, n)] = v[half:]
+        for b in range(CHIPS):
+            r = pl.ds(pl.multiple_of(((b + CHIPS - 1 - chip) % CHIPS) * blk, blk), blk)
+            S[f, i0, r, pl.ds(col, n)] = v[b * blk:(b + 1) * blk]
+            S[f, i1, r, pl.ds(col, n)] = v[half + b * blk:half + (b + 1) * blk]
 
     def stage_a(fl, c):
         f, s = fset[fl], c % SLOTS
         c_pair(fl, c).wait_recv()
         c_pair(fl, c).wait_send()
-
         for st in {1: (st_a, st_q, st_o), 3: (st_h, st_dp), 4: (st_dq,), 5: ()}[fl]:
             st(c).wait()
 
         def add(t, _):
             r = pl.ds(pl.multiple_of(t * hb, hb), hb)
-            S[f, s, r] = (S[f, s, r].astype(F32) + RD[f, s, r].astype(F32)).astype(BF)
-            return 0
-
-        lax.fori_loop(0, half // hb, add, 0)
-        for d in (0, 1):
-            c_relay(fl, c, d).start()
-        for d in (0, 1):
-            c_direct(fl, c, d).start()
+            S[f, s, r] = (S[f, s, r].astype(F32) + RD[f, c % PAIRS, r].astype(F32)).astype(BF)
+            return 0
+
+        lax.fori_loop(0, half // hb, add, 0, unroll=2)
+        for d in (0, 1):
+            c_first(fl, c, d).start()
 
     def stage_b(fl, c):
         f, s = fset[fl], c % SLOTS
         for d in (0, 1):
-            c_relay(fl, c, d).wait_recv()
-        for d in (0, 1):
-            o = pl.ds(pl.multiple_of((lchip if d else rchip) * blk + d * hb, hb), hb)
-            S[f, s, o] = (S[f, s, o].astype(F32) + R1[f, s, d, 0].astype(F32)).astype(BF)
+            c_first(fl, c, d).wait_recv()
+        for d in (0, 1):
+            o = pl.ds(2 * blk + hb if d else 0, hb)
+            S[f, s, o] = (S[f, s, o].astype(F32) + R1[f, s, d, pl.ds(0 if d else hb, hb)].astype(F32)).astype(BF)
             c_second(fl, c, d).start()
 
     def stage_c(fl, c):
         f, s = fset[fl], c % SLOTS
         for d in (0, 1):
-            c_direct(fl, c, d).wait_recv()
             c_second(fl, c, d).wait_recv()
 
         for k in (0, 1):
             q = pl.ds(k * hb, hb)
-            o = pl.ds(pl.multiple_of(chip * blk + k * hb, hb), hb)
-            tot = S[f, s, o].astype(F32) + R1[f, s, 1 - k, 1].astype(F32) + R2[f, s, k].astype(F32)
+            o = pl.ds(3 * blk + k * hb, hb)
+            tot = S[f, s, o].astype(F32) + R1[f, s, 1 - k, pl.ds(0 if k else hb, hb)].astype(F32) + R2[f, s, k].astype(F32)
             if fl == 1:
                 z = (xs[c, q].astype(F32) + tot).astype(BF)
                 xm[c, q] = z
@@ -257,8 +254,7 @@
             c_own(fl, c, d).start()
         st_own(fl, c).start()
         for d in (0, 1):
-            c_relay(fl, c, d).wait_send()
-            c_direct(fl, c, d).wait_send()
+            c_first(fl, c, d).wait_send()
             c_second(fl, c, d).wait_send()
         if fl == 4:
             @pl.when(c == nseq - 1)
@@ -306,12 +302,6 @@
         return qt, kt, vt, ex / jnp.sum(ex, axis=0, keepdims=True)
 
     def stage_F1(c):
-        @pl.when(c == 0)
-        def _():
-            for w in w1:
-                w.wait()
-            xs_ld.wait()
-
         ld_x(c).wait()
 
         def ln(t, _):
@@ -320,8 +310,14 @@
             ab[r] = (xh * ga[...]).astype(BF)
             return 0
 
-        lax.fori_loop(0, slen // hb, ln, 0)
+        lax.fori_loop(0, slen // hb, ln, 0, unroll=4)
         st_a(c).start()
+
+        @pl.when(c == 0)
+        def _():
+            for w in w1:
+                w.wait()
+            xs_ld.wait()
 
         @pl.when(c + 1 < nseq)
         def _():
@@ -450,10 +446,13 @@
     def y_loads(c):
         s = c % SLOTS
 
-        def part(co):
-            return py_o.at[pl.ds(pl.multiple_of(c * slen + co * half, half), half)]
-
-        return lc(part(1 - core), S.at[1, SLOTS], 19), lc(part(core), S.at[1, s], 20)
+        cps = []
+        for b in range(CHIPS):
+            ch = (chip + 1 + b) % CHIPS
+            for k, (co, t) in enumerate(((1 - core, SLOTS), (core, s))):
+                src = py_o.at[pl.ds(pl.multiple_of(c * slen + co * half + ch * blk, blk), blk)]
+                cps.append(pltpu.make_async_copy(src, S.at[1, t, pl.ds(b * blk, blk)], ysem.at[k, b]))
+        return cps
 
     def stage_YL(c):
         @pl.when(c == nseq - 1)
@@ -614,15 +613,17 @@
     V = pltpu.VMEM
     scratch = [
         V(wqkv.shape, BF), V(wo.shape, BF), V(wu.shape, BF), V(wd.shape, BF),
-        V((2, SLOTS + 1, half, dm), BF), V((2, SLOTS, half, dm), BF),
-        V((2, SLOTS, 2, 2, hb, dm), BF), V((2, SLOTS, 2, hb, dm), BF),
+        V((2, SLOTS + 1, half, dm), BF), V((2, PAIRS, half, dm), BF),
+        V((2, SLOTS, 2, blk, dm), BF), V((2, SLOTS, 2, hb, dm), BF),
         V((slen, dm), BF), V((slen, dm), BF), V((slen, dm), BF), V((slen, dm), BF), V((slen, dm), BF),
         V((3 * he, slen), BF), V((3 * he, slen), BF), V((slen, 3 * he), BF), V((3 * he, slen), BF),
         V((slen, he), BF), V((he, slen), BF), V((slen, ff), BF), V((slen, ff), BF), V((slen, dm), BF),
         V((nseq, blk, dm), BF), V((nseq, blk, dm), BF), V((nseq, blk, dm), BF), V((2, 2, blk, dm), BF), V((2, dm), F32),
         V((CHIPS * CORES, 2, dm), F32),
-        pltpu.SemaphoreType.DMA((21 + 4 * nseq,)), pltpu.SemaphoreType.DMA((5, 2)), pltpu.SemaphoreType.DMA((2, CHIPS * CORES)),
-        pltpu.SemaphoreType.DMA((4, 15, nseq)), pltpu.SemaphoreType.DMA((4, 15, nseq)),
+        pltpu.SemaphoreType.DMA((23,)), pltpu.SemaphoreType.DMA((5, 2)), pltpu.SemaphoreType.DMA((2, CHIPS * CORES)),
+        pltpu.SemaphoreType.DMA((2, CHIPS)),
+        pltpu.SemaphoreType.DMA((2, 5 * SLOTS)), pltpu.SemaphoreType.DMA((2, 5 * SLOTS)),
+        pltpu.SemaphoreType.DMA((2, 8 * nseq)), pltpu.SemaphoreType.DMA((2, 8 * nseq)),
     ]
     flops = 2 * nseq * slen * dm * (4 * he * 2 + ff * 4)
     return pl.pallas_call(

time: 517 us -> 490 us (0.948)
  Pallas kernels: 474 us -> 447 us
    pallas_call x1, Pallas kernels: 474 us -> 447 us  [mega(): pl.pallas_call(functools.partial(body, heads), name='mega', out_shape=out...]
where the time goes in v4:
time: 490 us; the launch traced here: 489 us
  Pallas kernels  447 us (91%)
  local copies, waits for them, and re-layouts  41.4 us (8%)
    pallas_call x1, Pallas kernels, mega(): pl.pallas_call(functools.partial(body, heads), name='mega', out_shape=out...  447 us
    unnamed x14, local copies, waits for them, and re-layouts  40 us

profile of v4, /device:TPU:81, one launch (start us, length us, event | category | flops | bytes accessed | tf_op | source)
XLA Modules:
  0.0 489.2 jit_solution(9887943366809112421)
XLA Ops:
  0.6 447.1 %mega.1 = (bf16[2048,3072]{1,0:T(8,128)(2,1)}, bf16[2048,3072]{1,0:T(8,128)(2,1)}, bf16[1152,3072]{1,0:T(8,128)(2,1)}, bf16[384,3072]{1,0:T(8,128)(2,1)}, bf16[3...) custom-call(bf16[8,256,3072]{2,1,0:T(8,128)(2,1)} %x.1, ...), custom_call_target="tpu_custom_call" | custom-call | flops 115964116992 | bytes 150994944 | tf_op jit(solution)/shard_map/mega/pallas_call | solution.py:629
  447.7 1.4 fusion
  449.2 0.0 copy-start
  449.2 0.0 slice-start
  449.2 12.4 %copy.22 = bf16[8,256,3072]{2,1,0:T(8,128)(2,1)} copy(bf16[8,256,3072]{2,1,0:T(8,128)(2,1)} %bitcast.20) | data formatting | bytes 25165824
  461.6 0.0 copy-done
  461.6 0.0 slice-start.1
  461.6 6.0 %copy.23 = bf16[8,256,3072]{2,1,0:T(8,128)(2,1)} copy(bf16[8,256,3072]{2,1,0:T(8,128)(2,1)S(1)} %bitcast.19) | data formatting | bytes 25165824
  467.6 0.0 slice-done
  467.6 0.4 slice-done.1
  468.1 0.0 copy-start.1
  468.1 3.2 copy.24
  471.2 0.2 copy-done.1
  471.4 1.4 copy.25
  472.9 8.0 %copy.26 = bf16[1,3072,1536]{2,1,0:T(8,128)(2,1)} copy(bf16[1,3072,1536]{2,1,0:T(8,128)(2,1)} %bitcast.22) | data formatting | bytes 18874368
  480.9 8.3 %copy.27 = bf16[1,1536,3072]{2,1,0:T(8,128)(2,1)} copy(bf16[1,1536,3072]{2,1,0:T(8,128)(2,1)} %bitcast.21) | data formatting | bytes 18874368
  (1 shorter events, 0.0 us)
Async XLA Ops:
  449.2 12.4 %copy-start = (bf16[2048,3072]{1,0:T(8,128)(2,1)S(1)}, bf16[2048,3072]{1,0:T(8,128)(2,1)}, u32[]{:S(2)}) copy-start(bf16[2048,3072]{1,0:T(8,128)(2,1)} %get-tuple-element.16) | copy-start | bytes 37748740
  449.2 18.4 %slice-start = ((s8[7077888]{0:T(1024)(128)(4,1)}), s8[4194304]{0:T(1024)(128)(4,1)S(1)}, s32[]{:S(2)}) async-start(s8[7077888]{0:T(1024)(128)(4,1)} %bitcast.23), calls=%async_computation | async-start | bytes 8388608
  461.6 6.5 %slice-start.1 = ((s8[7077888]{0:T(1024)(128)(4,1)}), s8[2883584]{0:T(1024)(128)(4,1)S(1)}, s32[]{:S(2)}) async-start(s8[7077888]{0:T(1024)(128)(4,1)} %bitcast.23), calls=%async_computation.1 | async-start | bytes 5767168
  468.1 3.4 copy-start.1

commit v5 on v4

--- a/solution.py
+++ b/solution.py
@@ -7,6 +7,7 @@
 from jax.experimental import pallas as pl
 from jax.experimental.pallas import tpu as pltpu
 from jax.sharding import PartitionSpec as P
+
 
 LN_EPS = 1e-5
 CORES = 2
@@ -21,10 +22,10 @@
 PAIRS = 2
 
 ORDER = (
-    ('a3', 8), ('a5', 21), ('MU', 7), ('d3', 11), ('c4', 17), ('f4', 21), ('B2', 15), ('b4', 16), ('b1', 2),
-    ('d5', 24), ('a4', 15), ('e1', 6), ('a1', 1), ('YL', 20), ('MD', 7), ('d1', 4), ('f3', 14), ('c3', 9),
-    ('d4', 18), ('WG', 22), ('c5', 22), ('f1', 6), ('e5', 25), ('F1', 0), ('c1', 2), ('MY', 7), ('b5', 21),
-    ('b3', 8), ('e4', 19), ('f5', 29), ('YS', 20), ('e3', 13),
+    ('b4', 14), ('d3', 10), ('f3', 12), ('c4', 15), ('F1', 0), ('c1', 2), ('MU', 6), ('e1', 5), ('b1', 1),
+    ('a4', 13), ('a1', 0), ('YL', 18), ('MD', 6), ('f1', 5), ('WG', 20), ('e3', 11), ('YS', 18), ('c3', 8),
+    ('c5', 20), ('b5', 19), ('MY', 6), ('e4', 18), ('f4', 19), ('a5', 18), ('b3', 7), ('a3', 6), ('d4', 16),
+    ('d1', 3), ('B2', 12),
 )
 
 
@@ -64,7 +65,7 @@
 
 
 def body(heads, x, dy, dyf, wqkv_h, wo_h, wu_h, wd_h, ga, gm,
-         y_o, dx_o, dwq_o, dwo_o, dwu_o, dwd_o, nm_o, g_o, a_o, o_o, qkv_o, h_o, dp_o, dq_o, py_o, dgain_o,
+         ys_o, dx_o, dwq_o, dwo_o, dwu_o, dwd_o, nm_o, g_o, a_o, o_o, qkv_o, h_o, dp_o, dq_o, py_o, dgain_o,
          wqkv, wo, wu, wd, S, RD, R1, R2, xb, ab, nb, dyb, gb, qb, qb2, dqb, dqt, ob, obt, hb_, dpb, pyb,
          xs, xm, gs, own, dgb, dgs, lsem, wsem, dsem, ysem, ssem1, rsem1, ssem, rsem):
     nseq, slen, dm = x.shape
@@ -139,7 +140,7 @@
 
     xs_ld = lc(x.at[:, pl.ds(myoff, blk), :], xs, 16)
     dys_ld = lc(dy.at[:, pl.ds(myoff, blk), :], gs, 17)
-    out_ref = {1: nm_o, 3: g_o, 4: dx_o, 5: y_o}
+    out_ref = {1: nm_o, 3: g_o, 4: dx_o}
     fset = {1: 0, 3: 1, 4: 0, 5: 1}
 
     def out_rows(fl, c, o, n):
@@ -245,14 +246,15 @@
                 own[f, c % 2, q] = v
                 dgb[1:2] += dgn
             elif fl == 5:
-                own[f, c % 2, q] = (xm[c, q].astype(F32) + tot).astype(BF)
+                xm[c, q] = (xm[c, q].astype(F32) + tot).astype(BF)
             else:
                 dr, dgn = ln_bwd(xs[c, q].astype(F32), ga[...], tot)
                 own[f, c % 2, q] = (gs[c, q].astype(F32) + dr).astype(BF)
                 dgb[0:1] += dgn
-        for d in (0, 1, 2):
-            c_own(fl, c, d).start()
-        st_own(fl, c).start()
+        if fl != 5:
+            for d in (0, 1, 2):
+                c_own(fl, c, d).start()
+            st_own(fl, c).start()
         for d in (0, 1):
             c_first(fl, c, d).wait_send()
             c_second(fl, c, d).wait_send()
@@ -306,7 +308,7 @@
 
         def ln(t, _):
             r = pl.ds(pl.multiple_of(t * hb, hb), hb)
-            xh, _r = ln_parts(xb[r].astype(F32))
+            xh, _ = ln_parts(xb[r].astype(F32))
             ab[r] = (xh * ga[...]).astype(BF)
             return 0
 
@@ -334,7 +336,7 @@
         st_q(c).start()
 
         def head(hd, _):
-            _q, _k, vt, p = probs_t(qb, hd)
+            _, _, vt, p = probs_t(qb, hd)
             obt[pl.ds(pl.multiple_of(hd * e, e), e)] = dg(vt, p.astype(BF), 1, 0).astype(BF)
             return 0
 
@@ -582,6 +584,8 @@
 
     lax.fori_loop(0, nseq + max(l for _, l in order), step, 0)
 
+    ys = lc(xm, ys_o, 18)
+    ys.start()
     for b in (0, 1):
         o_store(0, b).wait()
     for k in range(1, tpn):
@@ -592,6 +596,7 @@
     dgain_o[...] = tot
     for k in range(1, tpn):
         c_gain(k).wait_send()
+    ys.wait()
 
 
 def mega(x, dy, wqkv, wo, wu, wd, ga, gm, heads):
@@ -606,7 +611,7 @@
         return jax.ShapeDtypeStruct(shape, BF)
 
     act = arr(tok, dm)
-    outs = (act, act, arr(3 * he, dm), arr(he, dm), arr(dm, ff), arr(ff, dm), act, act, act, arr(tok, he),
+    outs = (arr(nseq, blk, dm), act, arr(3 * he, dm), arr(he, dm), arr(dm, ff), arr(ff, dm), act, act, act, arr(tok, he),
             arr(nseq, 3 * he, slen), arr(tok, ff), arr(tok, ff), arr(tok, 3 * he), act, jax.ShapeDtypeStruct((2, dm), F32))
     hbm = pl.BlockSpec(memory_space=pl.ANY)
     vm = pl.BlockSpec(memory_space=pltpu.VMEM)
@@ -638,8 +643,45 @@
     )(x, dy, dy.reshape(tok, dm), wqkv, wo, wu, wd, ga, gm)
 
 
+def copied(v):
+    rows = tile_of(v.shape[0], 256 * 1536 // v.shape[1] * 2)
+
+    def move(src, dst):
+        dst[...] = src[...]
+
+    spec = pl.BlockSpec((rows, v.shape[1]), lambda i: (i, 0))
+    return pl.pallas_call(
+        move, grid=(v.shape[0] // rows,), in_specs=[spec], out_specs=spec,
+        out_shape=jax.ShapeDtypeStruct(v.shape, v.dtype),
+        cost_estimate=pl.CostEstimate(flops=v.size * 500, bytes_accessed=4 * v.size, transcendentals=0))(v)
+
+
 def solution(mesh):
-    assert mesh.shape['tp'] == CHIPS * CORES
+    tpn = mesh.shape['tp']
+    assert tpn == CHIPS * CORES
+
+    def hop(v, chips_by, cores_by):
+        perm = []
+        for t in range(tpn):
+            ch, co = t // CORES, t % CORES
+            perm.append((t, ((ch + chips_by) % CHIPS) * CORES + (co + cores_by) % CORES))
+        return lax.ppermute(v, 'tp', perm)
+
+    def gather(v, chip, core):
+        nseq, blk, dm = v.shape
+        hb = blk // 2
+        half = blk * CHIPS
+        v_l, v_r = hop(v, 1, 0), hop(v, -1, 0)
+        v_x = hop(v, 0, 1)
+        o0, o1 = hop(v_l[:, :hb], 1, 0), hop(v_r[:, hb:], -1, 0)
+        v_lx, v_rx = hop(v_l, 0, 1), hop(v_r, 0, 1)
+        o0x, o1x = hop(o0, 0, 1), hop(o1, 0, 1)
+        l, r, o = (chip + CHIPS - 1) % CHIPS, (chip + 1) % CHIPS, (chip + 2) % CHIPS
+        out = jnp.zeros((nseq, half * CORES, dm), v.dtype)
+        for co, pieces in ((core, (v, v_l, v_r, o0, o1)), (1 - core, (v_x, v_lx, v_rx, o0x, o1x))):
+            for p, at in zip(pieces, (chip * blk, l * blk, r * blk, o * blk, o * blk + hb)):
+                out = lax.dynamic_update_slice_in_dim(out, p, co * half + at, axis=1)
+        return out
 
     def step(x_in, gain_attn, w_qkv, w_out, gain_mlp, w_up, w_down, dy_out):
         heads, e = w_qkv.shape[3:]
@@ -648,10 +690,14 @@
         wqkv = jnp.transpose(w_qkv[0], (1, 2, 3, 0)).reshape(3 * he, dm)
         wo = w_out[0].reshape(he, dm)
         out = mega(x_in, dy_out, wqkv, wo, w_up[0], w_down[0], gain_attn, gain_mlp, heads)
-        y, dx, dwq, dwo, dwu, dwd = out[:6]
+        ys, dx, dwq, dwo, dwu, dwd = out[:6]
         dgain = out[-1]
+        tp = lax.axis_index('tp')
+        dwu, dwd, dx, dwq, dwo = (copied(v) for v in (
+            dwu, dwd, dx, dwq, dwo))
+        y = gather(ys, tp // CORES, tp % CORES)
         dwq = jnp.transpose(dwq.reshape(3, heads, e, dm), (3, 0, 1, 2))
-        return (y.reshape(x_in.shape), dx.reshape(x_in.shape), dgain[0:1], dwq[None], dwo.reshape(1, heads, e, dm),
+        return (y, dx.reshape(x_in.shape), dgain[0:1], dwq[None], dwo.reshape(1, heads, e, dm),
                 dgain[1:2], dwu[None], dwd[None])
 
     act = P('dp', None, None)
@@ -659,4 +705,5 @@
                 P(None, None, 'tp'), P(None, 'tp', None), act)
     out_specs = (act, act, P('dp', None), P('dp', None, None, 'tp', None), P('dp', 'tp', None, None), P('dp', None),
                  P('dp', None, 'tp'), P('dp', 'tp', None))
-    return jax.shard_map(step, mesh=mesh, in_specs=in_specs, out_specs=out_specs, check_vma=False)
+    step = jax.shard_map(step, mesh=mesh, in_specs=in_specs, out_specs=out_specs, check_vma=False)
+    return step

time: 490 us -> 496 us (1.012)
  local copies, waits for them, and re-layouts: 41.4 us -> 24.1 us
  waiting for transfers between devices: 0 us -> 9.95 us
  starting transfers between devices: 0 us -> 8.04 us
  Pallas kernels: 447 us -> 452 us
    pallas_call x0 -> x5, Pallas kernels: none -> 41.8 us  [copied(): pl.pallas_call(move, grid=(v.shape[0] // rows,), in_specs=[spec], out_spe...]
    unnamed x14 -> x4, local copies, waits for them, and re-layouts: 40 us -> 0.01 us
    pallas_call x1, Pallas kernels: 447 us -> 410 us  [mega(): pl.pallas_call(functools.partial(body, heads), name='mega', out_shape=out...]
    dynamic_update_slice x0 -> x10, local copies, waits for them, and re-layouts: none -> 15.1 us  [gather(): out = lax.dynamic_update_slice_in_dim(out, p, co * half + at, axis=1)]
    ppermute x0 -> x9, waiting for transfers between devices: none -> 9.95 us  [hop(): return lax.ppermute(v, 'tp', perm)]
    ppermute x0 -> x9, starting transfers between devices: none -> 8.04 us  [hop(): return lax.ppermute(v, 'tp', perm)]
    broadcast_in_dim x0 -> x1, local copies, waits for them, and re-layouts: none -> 6.37 us  [gather(): out = jnp.zeros((nseq, half * CORES, dm), v.dtype)]
  transfers between devices with their start and end apart: 0 -> 9, of which waited for: 0 -> 1; matrix products, arithmetic and copies ran while one was open for 0% -> 5% of each run, Pallas kernels for 0% -> 8%
where the time goes in v5:
time: 496 us; the launch traced here: 495 us
  Pallas kernels  452 us (91%)
  local copies, waits for them, and re-layouts  24.1 us (5%)
  waiting for transfers between devices  9.95 us (2%)
  starting transfers between devices  8.04 us (2%)
    pallas_call x1, Pallas kernels, mega(): pl.pallas_call(functools.partial(body, heads), name='mega', out_shape=out...  410 us
    pallas_call x5, Pallas kernels, copied(): pl.pallas_call(move, grid=(v.shape[0] // rows,), in_specs=[spec], out_spe...  41.8 us
    dynamic_update_slice x10, local copies, waits for them, and re-layouts, gather(): out = lax.dynamic_update_slice_in_dim(out, p, co * half + at, axis=1)  15.1 us
    ppermute x9, waiting for transfers between devices, hop(): return lax.ppermute(v, 'tp', perm)  9.95 us
  transfers between devices with their start and end apart: 9, of which 1 were waited for; matrix products, arithmetic and copies ran while one was open for 5% of the time, Pallas kernels for 8%

profile of v5, /device:TPU:81, one launch (start us, length us, event | category | flops | bytes accessed | tf_op | source)
XLA Modules:
  0.0 494.7 jit_solution(13882442500733796424)
XLA Ops:
  0.6 410.1 %mega.1 = (bf16[8,32,3072]{2,1,0:T(8,128)(2,1)}, bf16[2048,3072]{1,0:T(8,128)(2,1)}, bf16[1152,3072]{1,0:T(8,128)(2,1)}, bf16[384,3072]{1,0:T(8,128)(2,1)}, bf16...) custom-call(bf16[8,256,3072]{2,1,0:T(8,128)(2,1)} %x.1, ...), custom_call_target="tpu_custom_call" | custom-call | flops 115964116992 | bytes 150994944 | tf_op jit(solution)/shard_map/mega/pallas_call | solution.py:634
  410.8 0.1 collective-permute-start
  410.9 2.7 collective-permute-start.1
  413.5 0.9 collective-permute-start.4
  414.5 8.6 %shard_map.146 = bf16[3072,1536]{1,0:T(8,128)(2,1)} custom-call(bf16[3072,1536]{1,0:T(8,128)(2,1)} %get-tuple-element.20.src), custom_call_target="tpu_custom_call" | custom-call | flops 2359296000 | bytes 18874368 | tf_op jit(solution)/shard_map/pallas_call | solution.py:653
  423.1 8.6 %shard_map.147 = bf16[1536,3072]{1,0:T(8,128)(2,1)} custom-call(bf16[1536,3072]{1,0:T(8,128)(2,1)} %get-tuple-element.21.src), custom_call_target="tpu_custom_call" | custom-call | flops 2359296000 | bytes 18874368 | tf_op jit(solution)/shard_map/pallas_call | solution.py:653
  431.8 11.4 %shard_map.143 = bf16[2048,3072]{1,0:T(8,128)(2,1)} custom-call(bf16[2048,3072]{1,0:T(8,128)(2,1)} %get-tuple-element.16.src), custom_call_target="tpu_custom_call" | custom-call | flops 3145728000 | bytes 25165824 | tf_op jit(solution)/shard_map/pallas_call | solution.py:653
  443.1 0.0 copy-start
  443.1 0.0 copy-start.1
  443.1 6.4 %broadcast_in_dim.12 = bf16[8,256,3072]{2,1,0:T(8,128)(2,1)} broadcast(bf16[]{:T(256)} %constant.48.clone.1), dimensions={} | broadcast | bytes 12582914 | tf_op jit(solution)/shard_map/broadcast_in_dim | solution.py:680
  449.5 0.0 copy-done
  449.5 1.2 constant_dynamic-update-slice_fusion.9
  450.7 0.0 copy-done.1
  450.7 0.6 fusion
  451.4 9.3 %shard_map.144 = bf16[1152,3072]{1,0:T(8,128)(2,1)} custom-call(bf16[1152,3072]{1,0:T(8,128)(2,1)} %get-tuple-element.18.src), custom_call_target="tpu_custom_call" | custom-call | flops 1769472000 | bytes 14155776 | tf_op jit(solution)/shard_map/pallas_call | solution.py:653
  460.7 0.0 collective-permute-done
  460.7 1.0 slice.16
  461.7 0.0 collective-permute-start.2
  461.7 0.0 collective-permute-done.1
  461.7 1.0 slice.17
  462.7 2.7 collective-permute-start.3
  465.4 3.9 shard_map.145
  469.2 0.6 collective-permute-start.5
  469.8 0.0 collective-permute-start.6
  469.8 1.3 constant_dynamic-update-slice_fusion.8
  471.1 1.3 constant_dynamic-update-slice_fusion.7
  472.4 9.9 %collective-permute-done.2 = bf16[8,16,3072]{2,1,0:T(8,128)(2,1)} collective-permute-done((bf16[8,16,3072]{2,1,0:T(8,128)(2,1)}, bf16[8,16,3072]{2,1,0:T(8,128)(2,1)}, u32[]{:S(2)}, u32[]{:S(2)}) %collective-permute-start.2) | collective-permute-done | bytes 786464 | tf_op jit(solution)/shard_map/ppermute | solution.py:668
  482.3 0.9 collective-permute-start.7
  483.2 0.0 collective-permute-done.3
  483.2 0.2 collective-permute-start.8
  483.4 2.1 constant_dynamic-update-slice_fusion.6
  485.5 2.1 constant_dynamic-update-slice_fusion.5
  487.5 0.0 collective-permute-done.4
  487.6 2.7 constant_dynamic-update-slice_fusion.4
  490.2 0.0 collective-permute-done.5
  490.2 1.3 constant_dynamic-update-slice_fusion.3
  491.5 0.0 collective-permute-done.6
  491.5 1.3 constant_dynamic-update-slice_fusion.2
  492.8 0.0 collective-permute-done.7
  492.8 0.9 constant_dynamic-update-slice_fusion.1
  493.8 0.0 collective-permute-done.8
  493.8 0.9 constant_dynamic-update-slice_fusion
Async XLA Ops:
  410.8 49.9 %collective-permute-start = (bf16[8,32,3072]{2,1,0:T(8,128)(2,1)}, bf16[8,32,3072]{2,1,0:T(8,128)(2,1)S(1)}, u32[]{:S(2)}, u32[]{:S(2)}) collective-permute-start(bf16[8,32,3072]{2,1,0:T(8,128)(2,1)} %get-tuple-element.15), channel_id=1, source_target_pairs={{0,2},{1,3},{2,4},{3,5},{4,6},{5,7},{6,0},{7,1},{8,10},{9,11},{10,... | collective-permute-start | bytes 4718600 | tf_op jit(solution)/shard_map/ppermute | solution.py:668
  410.9 50.8 %collective-permute-start.1 = (bf16[8,32,3072]{2,1,0:T(8,128)(2,1)}, bf16[8,32,3072]{2,1,0:T(8,128)(2,1)S(1)}, u32[]{:S(2)}, u32[]{:S(2)}) collective-permute-start(bf16[8,32,3072]{2,1,0:T(8,128)(2,1)} %get-tuple-element.15), channel_id=1, source_target_pairs={{0,6},{1,7},{2,0},{3,1},{4,2},{5,3},{6,4},{7,5},{8,14},{9,15},{10,... | collective-permute-start | bytes 4718600 | tf_op jit(solution)/shard_map/ppermute | solution.py:668
  413.5 74.0 %collective-permute-start.4 = (bf16[8,32,3072]{2,1,0:T(8,128)(2,1)}, bf16[8,32,3072]{2,1,0:T(8,128)(2,1)}, u32[]{:S(2)}, u32[]{:S(2)}) collective-permute-start(bf16[8,32,3072]{2,1,0:T(8,128)(2,1)} %get-tuple-element.15), channel_id=1, source_target_pairs={{0,1},{1,0},{2,3},{3,2},{4,5},{5,4},{6,7},{7,6},{8,9},{9,8},{10,11... | collective-permute-start | bytes 4718600 | tf_op jit(solution)/shard_map/ppermute | solution.py:668
  443.1 6.4 %copy-start = (bf16[8,32,3072]{2,1,0:T(8,128)(2,1)S(1)}, bf16[8,32,3072]{2,1,0:T(8,128)(2,1)}, u32[]{:S(2)}) copy-start(bf16[8,32,3072]{2,1,0:T(8,128)(2,1)} %get-tuple-element.15) | copy-start | bytes 4718596
  443.1 7.6 %copy-start.1 = (f32[2,3072]{1,0:T(2,128)S(1)}, f32[2,3072]{1,0:T(2,128)}, u32[]{:S(2)}) copy-start(f32[2,3072]{1,0:T(2,128)} %get-tuple-element.17) | copy-start | bytes 73732
  461.7 20.6 %collective-permute-start.2 = (bf16[8,16,3072]{2,1,0:T(8,128)(2,1)}, bf16[8,16,3072]{2,1,0:T(8,128)(2,1)}, u32[]{:S(2)}, u32[]{:S(2)}) collective-permute-start(bf16[8,16,3072]{2,1,0:T(8,128)(2,1)} %slice.16), channel_id=1, source_target_pairs={{0,2},{1,3},{2,4},{3,5},{4,6},{5,7},{6,0},{7,1},{8,10},{9,11},{10,... | collective-permute-start | bytes 2359304 | tf_op jit(solution)/shard_map/ppermute | solution.py:668
  462.7 20.5 %collective-permute-start.3 = (bf16[8,16,3072]{2,1,0:T(8,128)(2,1)}, bf16[8,16,3072]{2,1,0:T(8,128)(2,1)}, u32[]{:S(2)}, u32[]{:S(2)}) collective-permute-start(bf16[8,16,3072]{2,1,0:T(8,128)(2,1)} %slice.17), channel_id=1, source_target_pairs={{0,6},{1,7},{2,0},{3,1},{4,2},{5,3},{6,4},{7,5},{8,14},{9,15},{10,... | collective-permute-start | bytes 2359304 | tf_op jit(solution)/shard_map/ppermute | solution.py:668
  469.2 21.0 %collective-permute-start.5 = (bf16[8,32,3072]{2,1,0:T(8,128)(2,1)S(1)}, bf16[8,32,3072]{2,1,0:T(8,128)(2,1)S(1)}, u32[]{:S(2)}, u32[]{:S(2)}) collective-permute-start(bf16[8,32,3072]{2,1,0:T(8,128)(2,1)S(1)} %collective-permute-done), channel_id=1, source_target_pairs={{0,1},{1,0},{2,3},{3,2},{4,5},{5,4},{6,7},{7,6},{8,9},{9,8},{10,11... | collective-permute-start | bytes 4718600 | tf_op jit(solution)/shard_map/ppermute | solution.py:668
  469.8 21.7 %collective-permute-start.6 = (bf16[8,32,3072]{2,1,0:T(8,128)(2,1)S(1)}, bf16[8,32,3072]{2,1,0:T(8,128)(2,1)S(1)}, u32[]{:S(2)}, u32[]{:S(2)}) collective-permute-start(bf16[8,32,3072]{2,1,0:T(8,128)(2,1)S(1)} %collective-permute-done.1), channel_id=1, source_target_pairs={{0,1},{1,0},{2,3},{3,2},{4,5},{5,4},{6,7},{7,6},{8,9},{9,8},{10,11... | collective-permute-start | bytes 4718600 | tf_op jit(solution)/shard_map/ppermute | solution.py:668
  482.3 10.5 %collective-permute-start.7 = (bf16[8,16,3072]{2,1,0:T(8,128)(2,1)}, bf16[8,16,3072]{2,1,0:T(8,128)(2,1)S(1)}, u32[]{:S(2)}, u32[]{:S(2)}) collective-permute-start(bf16[8,16,3072]{2,1,0:T(8,128)(2,1)} %collective-permute-done.2), channel_id=1, source_target_pairs={{0,1},{1,0},{2,3},{3,2},{4,5},{5,4},{6,7},{7,6},{8,9},{9,8},{10,11... | collective-permute-start | bytes 2359304 | tf_op jit(solution)/shard_map/ppermute | solution.py:668
  483.2 10.6 %collective-permute-start.8 = (bf16[8,16,3072]{2,1,0:T(8,128)(2,1)}, bf16[8,16,3072]{2,1,0:T(8,128)(2,1)S(1)}, u32[]{:S(2)}, u32[]{:S(2)}) collective-permute-start(bf16[8,16,3072]{2,1,0:T(8,128)(2,1)} %collective-permute-done.3), channel_id=1, source_target_pairs={{0,1},{1,0},{2,3},{3,2},{4,5},{5,4},{6,7},{7,6},{8,9},{9,8},{10,11... | collective-permute-start | bytes 2359304 | tf_op jit(solution)/shard_map/ppermute | solution.py:668

commit v6 on v5

--- a/solution.py
+++ b/solution.py
@@ -20,12 +20,13 @@
 GELU_K = 0.044715
 SLOTS = 3
 PAIRS = 2
+TILES = 2
 
 ORDER = (
-    ('b4', 14), ('d3', 10), ('f3', 12), ('c4', 15), ('F1', 0), ('c1', 2), ('MU', 6), ('e1', 5), ('b1', 1),
-    ('a4', 13), ('a1', 0), ('YL', 18), ('MD', 6), ('f1', 5), ('WG', 20), ('e3', 11), ('YS', 18), ('c3', 8),
-    ('c5', 20), ('b5', 19), ('MY', 6), ('e4', 18), ('f4', 19), ('a5', 18), ('b3', 7), ('a3', 6), ('d4', 16),
-    ('d1', 3), ('B2', 12),
+    ('e3', 15), ('MU', 8), ('b1', 3), ('d3', 12), ('WP', 10), ('a1', 2), ('B2', 16), ('F1', 1), ('f1', 7),
+    ('f3', 15), ('e1', 6), ('d1', 5), ('MD', 8), ('YS', 19), ('WG', 17), ('c3', 10), ('c5', 21), ('b5', 20),
+    ('c1', 3), ('a5', 19), ('YL', 18), ('d4', 20), ('e4', 22), ('MY', 8), ('f4', 23), ('c4', 18), ('b3', 9),
+    ('b4', 17), ('a3', 8), ('a4', 16),
 )
 
 
@@ -408,12 +409,6 @@
         st_py(c).start()
 
     def stage_B2(c):
-        @pl.when(c == nseq - 1)
-        def _():
-            start_a(0)
-            for k in (0, 1):
-                b_load(0, k).start()
-
         ld_q(c).start()
         ld_g(c).wait()
         obt[...] = dg(wo[...], gb[...], 1, 1).astype(BF)
@@ -480,8 +475,12 @@
     def a_buf(b, k):
         return wd.at[pl.ds(0, kh), pl.ds(pl.multiple_of((2 * b + k) * he, he), he)]
 
-    def b_buf(p, k):
-        return wqkv.at[pl.ds(0, kh), pl.ds(k * ff, ff)] if p % 2 else wu.at[pl.ds(k * kh, kh)]
+    def b_parts(p):
+        if p % 2 == 0:
+            return [(0, kh, wu.at[pl.ds(0, kh)]), (kh, kh, wu.at[pl.ds(kh, kh)])]
+        q = kh // 2
+        return [(0, kh, wd.at[pl.ds(0, kh), pl.ds(ff, ff)]), (kh, q, wd.at[pl.ds(kh, q), pl.ds(0, ff)]),
+                (kh + q, q, wd.at[pl.ds(kh, q), pl.ds(ff, ff)])]
 
     def o_buf(b):
         return wu.at[pl.ds(pl.multiple_of(tok + b * he, math.gcd(tok, he)), he)]
@@ -490,12 +489,13 @@
         col = pl.multiple_of((w - first[p]) * he, he)
         return pltpu.make_async_copy(gemms[p][0].at[pl.ds(k * kh, kh), pl.ds(col, he)], a_buf(w % 2, k), wsem.at[k, w % 2])
 
-    def b_load(p, k):
-        return pltpu.make_async_copy(gemms[p][1].at[pl.ds(k * kh, kh), pl.ds(gemms[p][4], ff)], b_buf(p, k), wsem.at[2 + k, p % 2])
+    def b_loads(p):
+        return [pltpu.make_async_copy(gemms[p][1].at[pl.ds(t, n), pl.ds(gemms[p][4], ff)], m, wsem.at[3 + q, p % 2])
+                for q, (t, n, m) in enumerate(b_parts(p))]
 
     def o_store(p, w):
         row = pl.multiple_of((w - first[p]) * he, he)
-        return pltpu.make_async_copy(o_buf(w % 2), gemms[p][2].at[pl.ds(row, he), pl.ds(gemms[p][4], ff)], wsem.at[4, w % 2])
+        return pltpu.make_async_copy(o_buf(w % 2), gemms[p][2].at[pl.ds(row, he), pl.ds(gemms[p][4], ff)], wsem.at[2, w % 2])
 
     def in_gemm(p, w):
         return (w >= first[p]) & (w < first[p + 1])
@@ -514,11 +514,11 @@
         for p in range(len(gemms)):
             @pl.when(w == first[p])
             def _():
-                for k in (0, 1):
-                    b_load(p, k).wait()
+                for cp in b_loads(p):
+                    cp.wait()
                 if p + 1 < len(gemms):
-                    for k in (0, 1):
-                        b_load(p + 1, k).start()
+                    for cp in b_loads(p + 1):
+                        cp.start()
 
         @pl.when(w >= 2)
         def _():
@@ -532,8 +532,9 @@
             def _():
                 for j in range(ff // n):
                     acc = None
-                    for k in (0, 1):
-                        t = dg(a_buf(w % 2, k)[...], b_buf(odd, k)[:, pl.ds(j * n, n)], 0, 0)
+                    for t0, nt, m in b_parts(odd):
+                        lhs = a_buf(w % 2, t0 // kh)[pl.ds(t0 % kh, nt)]
+                        t = dg(lhs, m[:, pl.ds(j * n, n)], 0, 0)
                         acc = t if acc is None else acc + t
                     o_buf(w % 2)[:, pl.ds(j * n, n)] = acc.astype(BF)
 
@@ -543,13 +544,18 @@
                 o_store(p, w).start()
 
     def stage_WG(c):
-        per = tiles // nseq
-
         def one(j, _):
-            tile(c * per + j)
-            return 0
-
-        lax.fori_loop(0, per, one, 0)
+            tile(c * TILES + j)
+            return 0
+
+        lax.fori_loop(0, TILES, one, 0)
+
+    def stage_WP(c):
+        @pl.when(c == nseq - 1)
+        def _():
+            start_a(0)
+            for cp in b_loads(0):
+                cp.start()
 
     barrier = pltpu.get_barrier_semaphore()
     for k in range(1, tpn):
@@ -566,15 +572,18 @@
     pl.semaphore_wait(barrier, tpn - 1)
 
     run = {'F1': stage_F1, 'MU': stage_MU, 'MD': stage_MD, 'MY': stage_MY, 'B2': stage_B2,
-           'YL': stage_YL, 'YS': stage_YS, 'WG': stage_WG}
+           'YL': stage_YL, 'YS': stage_YS, 'WG': stage_WG, 'WP': stage_WP}
     hops = {'a': stage_a, 'b': stage_b, 'c': stage_c, 'd': stage_d, 'e': stage_e, 'f': stage_f}
     order = ORDER
+
+    def count(name):
+        return tiles // TILES if name == 'WG' else nseq
 
     def step(i, _):
         for name, lag in order:
             c = i - lag
 
-            @pl.when((c >= 0) & (c < nseq))
+            @pl.when((c >= 0) & (c < count(name)))
             def _():
                 if name in run:
                     run[name](c)
@@ -582,7 +591,7 @@
                     hops[name[0]](int(name[1]), c)
         return 0
 
-    lax.fori_loop(0, nseq + max(l for _, l in order), step, 0)
+    lax.fori_loop(0, max(count(n) + l for n, l in order), step, 0)
 
     ys = lc(xm, ys_o, 18)
     ys.start()
@@ -625,7 +634,7 @@
         V((slen, he), BF), V((he, slen), BF), V((slen, ff), BF), V((slen, ff), BF), V((slen, dm), BF),
         V((nseq, blk, dm), BF), V((nseq, blk, dm), BF), V((nseq, blk, dm), BF), V((2, 2, blk, dm), BF), V((2, dm), F32),
         V((CHIPS * CORES, 2, dm), F32),
-        pltpu.SemaphoreType.DMA((23,)), pltpu.SemaphoreType.DMA((5, 2)), pltpu.SemaphoreType.DMA((2, CHIPS * CORES)),
+        pltpu.SemaphoreType.DMA((23,)), pltpu.SemaphoreType.DMA((6, 2)), pltpu.SemaphoreType.DMA((2, CHIPS * CORES)),
         pltpu.SemaphoreType.DMA((2, CHIPS)),
         pltpu.SemaphoreType.DMA((2, 5 * SLOTS)), pltpu.SemaphoreType.DMA((2, 5 * SLOTS)),
         pltpu.SemaphoreType.DMA((2, 8 * nseq)), pltpu.SemaphoreType.DMA((2, 8 * nseq)),
@@ -643,17 +652,63 @@
     )(x, dy, dy.reshape(tok, dm), wqkv, wo, wu, wd, ga, gm)
 
 
-def copied(v):
-    rows = tile_of(v.shape[0], 256 * 1536 // v.shape[1] * 2)
-
-    def move(src, dst):
-        dst[...] = src[...]
-
-    spec = pl.BlockSpec((rows, v.shape[1]), lambda i: (i, 0))
+def copied(arrays):
+    n = len(arrays)
+    cuts = []
+    for a, v in enumerate(arrays):
+        rows = tile_of(v.shape[0], 256 * 3072 // v.shape[1])
+        cuts += [(a, r, rows) for r in range(0, v.shape[0], rows)]
+
+    def move(*refs):
+        src, dst, buf, isem, osem = refs[:n], refs[n:2 * n], refs[2 * n:3 * n], refs[-2], refs[-1]
+        into = [pltpu.make_async_copy(src[a].at[pl.ds(r, m)], buf[a].at[pl.ds(r, m)], isem.at[k]) for k, (a, r, m) in enumerate(cuts)]
+        out = [pltpu.make_async_copy(buf[a].at[pl.ds(r, m)], dst[a].at[pl.ds(r, m)], osem.at[k]) for k, (a, r, m) in enumerate(cuts)]
+        for cp in into:
+            cp.start()
+        for k in range(len(cuts)):
+            into[k].wait()
+            out[k].start()
+        for cp in out:
+            cp.wait()
+
+    hbm = pl.BlockSpec(memory_space=pl.ANY)
+    size = sum(v.size for v in arrays)
     return pl.pallas_call(
-        move, grid=(v.shape[0] // rows,), in_specs=[spec], out_specs=spec,
-        out_shape=jax.ShapeDtypeStruct(v.shape, v.dtype),
-        cost_estimate=pl.CostEstimate(flops=v.size * 500, bytes_accessed=4 * v.size, transcendentals=0))(v)
+        move, name='copy_all', in_specs=[hbm] * n, out_specs=(hbm,) * n,
+        out_shape=tuple(jax.ShapeDtypeStruct(v.shape, v.dtype) for v in arrays),
+        scratch_shapes=[pltpu.VMEM(v.shape, v.dtype) for v in arrays] + [pltpu.SemaphoreType.DMA((len(cuts),))] * 2,
+        compiler_params=pltpu.CompilerParams(vmem_limit_bytes=VMEM_BYTES),
+        cost_estimate=pl.CostEstimate(flops=size * 500, bytes_accessed=4 * size, transcendentals=0))(*arrays)
+
+
+def placed(out, pieces, shape, rows_of):
+    n = len(pieces)
+    given = [] if out is None else [out]
+
+    def put(*refs):
+        src, dst = refs[:n], refs[n + len(given)]
+        buf, isem, osem = refs[n + len(given) + 1:-2], refs[-2], refs[-1]
+        tp = lax.axis_index('tp')
+        at = rows_of(tp // CORES, tp % CORES)
+        into = [pltpu.make_async_copy(src[k], buf[k], isem.at[k]) for k in range(n)]
+        outc = [pltpu.make_async_copy(
+            buf[k], dst.at[:, pl.ds(pl.multiple_of(at[k], pieces[k].shape[1]), pieces[k].shape[1])], osem.at[k]) for k in range(n)]
+        for cp in into:
+            cp.start()
+        for k in range(n):
+            into[k].wait()
+            outc[k].start()
+        for cp in outc:
+            cp.wait()
+
+    hbm = pl.BlockSpec(memory_space=pl.ANY)
+    return pl.pallas_call(
+        put, in_specs=[hbm] * (n + len(given)), out_specs=hbm, out_shape=jax.ShapeDtypeStruct(shape, BF),
+        scratch_shapes=[pltpu.VMEM(p.shape, p.dtype) for p in pieces] + [pltpu.SemaphoreType.DMA((n,))] * 2,
+        input_output_aliases={n: 0} if given else {},
+        compiler_params=pltpu.CompilerParams(vmem_limit_bytes=VMEM_BYTES),
+        cost_estimate=pl.CostEstimate(flops=sum(p.size for p in pieces) * 500, bytes_accessed=0, transcendentals=0),
+    )(*pieces, *given)
 
 
 def solution(mesh):
@@ -667,7 +722,7 @@
             perm.append((t, ((ch + chips_by) % CHIPS) * CORES + (co + cores_by) % CORES))
         return lax.ppermute(v, 'tp', perm)
 
-    def gather(v, chip, core):
+    def gather(v):
         nseq, blk, dm = v.shape
         hb = blk // 2
         half = blk * CHIPS
@@ -676,12 +731,17 @@
         o0, o1 = hop(v_l[:, :hb], 1, 0), hop(v_r[:, hb:], -1, 0)
         v_lx, v_rx = hop(v_l, 0, 1), hop(v_r, 0, 1)
         o0x, o1x = hop(o0, 0, 1), hop(o1, 0, 1)
-        l, r, o = (chip + CHIPS - 1) % CHIPS, (chip + 1) % CHIPS, (chip + 2) % CHIPS
-        out = jnp.zeros((nseq, half * CORES, dm), v.dtype)
-        for co, pieces in ((core, (v, v_l, v_r, o0, o1)), (1 - core, (v_x, v_lx, v_rx, o0x, o1x))):
-            for p, at in zip(pieces, (chip * blk, l * blk, r * blk, o * blk, o * blk + hb)):
-                out = lax.dynamic_update_slice_in_dim(out, p, co * half + at, axis=1)
-        return out
+
+        def near(chip, core):
+            chips = [chip, (chip + CHIPS - 1) % CHIPS, (chip + 1) % CHIPS]
+            return [co * half + ch * blk for co in (core, 1 - core) for ch in chips]
+
+        def far(chip, core):
+            o = ((chip + 2) % CHIPS) * blk
+            return [co * half + o + k for co in (core, 1 - core) for k in (0, hb)]
+
+        out = placed(None, (v, v_l, v_r, v_x, v_lx, v_rx), (nseq, half * CORES, dm), near)
+        return placed(out, (o0, o1, o0x, o1x), out.shape, far)
 
     def step(x_in, gain_attn, w_qkv, w_out, gain_mlp, w_up, w_down, dy_out):
         heads, e = w_qkv.shape[3:]
@@ -692,10 +752,8 @@
         out = mega(x_in, dy_out, wqkv, wo, w_up[0], w_down[0], gain_attn, gain_mlp, heads)
         ys, dx, dwq, dwo, dwu, dwd = out[:6]
         dgain = out[-1]
-        tp = lax.axis_index('tp')
-        dwu, dwd, dx, dwq, dwo = (copied(v) for v in (
-            dwu, dwd, dx, dwq, dwo))
-        y = gather(ys, tp // CORES, tp % CORES)
+        dx, dwu, dwd, dwq, dwo = copied((dx, dwu, dwd, dwq, dwo))
+        y = gather(ys)
         dwq = jnp.transpose(dwq.reshape(3, heads, e, dm), (3, 0, 1, 2))
         return (y, dx.reshape(x_in.shape), dgain[0:1], dwq[None], dwo.reshape(1, heads, e, dm),
                 dgain[1:2], dwu[None], dwd[None])

time: 496 us -> 488 us (0.984)
  waiting for transfers between devices: 9.95 us -> 34 us
  local copies, waits for them, and re-layouts: 24.1 us -> 5.58 us
  Pallas kernels: 452 us -> 440 us
    ppermute x9, waiting for transfers between devices: 9.95 us -> 34 us  [hop(): return lax.ppermute(v, 'tp', perm)]
    dynamic_update_slice x10 -> x0, local copies, waits for them, and re-layouts: 15.1 us -> none  [gather(): out = lax.dynamic_update_slice_in_dim(out, p, co * half + at, axis=1)]
    pallas_call x1, Pallas kernels: 410 us -> 402 us  [mega(): pl.pallas_call(functools.partial(body, heads), name='mega', out_shape=out...]
    broadcast_in_dim x1 -> x0, local copies, waits for them, and re-layouts: 6.37 us -> none  [gather(): out = jnp.zeros((nseq, half * CORES, dm), v.dtype)]
    pallas_call x5 -> x3, Pallas kernels: 41.8 us -> 37.3 us  [the longest x1 27.2 us: copied(): pl.pallas_call(move, name='copy_all', in_specs=[hbm] * n, out_specs=(hbm,...]
  transfers between devices with their start and end apart: 9 -> 9, of which waited for: 1 -> 1; matrix products, arithmetic and copies ran while one was open for 5% -> 1% of each run, Pallas kernels for 8% -> 7%
where the time goes in v6:
time: 488 us; the launch traced here: 487 us
  Pallas kernels  440 us (90%)
  waiting for transfers between devices  34 us (7%)
  starting transfers between devices  6.74 us (1%)
  local copies, waits for them, and re-layouts  5.58 us (1%)
    pallas_call x1, Pallas kernels, mega(): pl.pallas_call(functools.partial(body, heads), name='mega', out_shape=out...  402 us
    ppermute x9, waiting for transfers between devices, hop(): return lax.ppermute(v, 'tp', perm)  34 us
    pallas_call x1, Pallas kernels, copied(): pl.pallas_call(move, name='copy_all', in_specs=[hbm] * n, out_specs=(hbm,...  27.2 us
    pallas_call x2, Pallas kernels, placed(): pl.pallas_call(put, in_specs=[hbm] * (n + len(given)), out_specs=hbm, out...  10.1 us
  transfers between devices with their start and end apart: 9, of which 1 were waited for; matrix products, arithmetic and copies ran while one was open for 1% of the time, Pallas kernels for 7%

profile of v6, /device:TPU:81, one launch (start us, length us, event | category | flops | bytes accessed | tf_op | source)
XLA Modules:
  0.0 486.9 jit_solution(15802827558876987872)
XLA Ops:
  0.6 402.5 %mega.1 = (bf16[8,32,3072]{2,1,0:T(8,128)(2,1)}, bf16[2048,3072]{1,0:T(8,128)(2,1)}, bf16[1152,3072]{1,0:T(8,128)(2,1)}, bf16[384,3072]{1,0:T(8,128)(2,1)}, bf16...) custom-call(bf16[8,256,3072]{2,1,0:T(8,128)(2,1)} %x.1, ...), custom_call_target="tpu_custom_call" | custom-call | flops 115964116992 | bytes 150994944 | tf_op jit(solution)/shard_map/mega/pallas_call | solution.py:643
  403.1 1.4 collective-permute-start.2
  404.5 0.2 collective-permute-start
  404.7 0.7 collective-permute-start.6
  405.3 34.0 %collective-permute-done.2.refs_2_ = bf16[8,32,3072]{2,1,0:T(8,128)(2,1)} collective-permute-done((bf16[8,32,3072]{2,1,0:T(8,128)(2,1)}, bf16[8,32,3072]{2,1,0:T(8,128)(2,1)}, u32[]{:S(2)}, u32[]{:S(2)}) %collective-permute-start.2) | collective-permute-done | bytes 1572896 | tf_op jit(solution)/shard_map/ppermute | solution.py:723
  439.3 2.1 slice.17
  441.4 2.5 collective-permute-start.3
  443.9 0.0 collective-permute-done.refs_1_
  443.9 2.1 slice.16
  446.0 0.0 collective-permute-start.1
  446.0 1.3 collective-permute-start.8
  447.2 0.0 collective-permute-start.7
  447.2 27.2 %copy_all.1 = (bf16[2048,3072]{1,0:T(8,128)(2,1)}, bf16[3072,1536]{1,0:T(8,128)(2,1)}, bf16[1536,3072]{1,0:T(8,128)(2,1)}, bf16[1152,3072]{1,0:T(8,128)(2,1)}, bf16[384,3072]{1,0:T(8,128)(2,1)}) custom-call(bf16[2048,3072]{1,0:T(8,128)(2,1)} %get-tuple-element.21.refs_0_, bf16[3072,1536]{1,0:T(8,128)(2,1)} %get-tuple-element.22.refs_1_, ...), custom_call_target="tpu_custom_call" | custom-call | flops 10223616000 | bytes 81788928 | tf_op jit(solution)/shard_map/copy_all/pallas_call | solution.py:676
  474.4 0.0 collective-permute-done.3.refs_1_
  474.4 0.6 collective-permute-start.5
  475.0 0.0 collective-permute-done.1.refs_0_
  475.0 0.1 collective-permute-start.4
  475.2 1.4 fusion
  476.6 0.0 collective-permute-done.6.refs_3_
  476.6 0.0 collective-permute-done.8.refs_5_
  476.6 0.0 collective-permute-done.7.refs_4_
  476.6 7.3 %shard_map.143.refs_4_ = bf16[8,256,3072]{2,1,0:T(8,128)(2,1)} custom-call(bf16[8,32,3072]{2,1,0:T(8,128)(2,1)} %get-tuple-element.20.refs_0_, bf16[8,32,3072]{2,1,0:T(8,128)(2,1)} %collective-permute-done.refs_1_, bf16[8,32,3072]{2,1,0:T(8,128)(2,1)} %collective-permute-done.2.refs_2_, bf16[8,32,3072]{2,1,0:T(8,128)(2,1)} %collective-permute-done.6.refs_3_, ...), custom_call_target="tpu_custom_call" | custom-call | flops 2359296000 | tf_op jit(solution)/shard_map/pallas_call | solution.py:705
  483.9 0.0 collective-permute-done.5.refs_3_
  483.9 0.0 collective-permute-done.4.refs_2_
  483.9 2.9 shard_map.144
Async XLA Ops:
  403.1 36.2 %collective-permute-start.2 = (bf16[8,32,3072]{2,1,0:T(8,128)(2,1)}, bf16[8,32,3072]{2,1,0:T(8,128)(2,1)}, u32[]{:S(2)}, u32[]{:S(2)}) collective-permute-start(bf16[8,32,3072]{2,1,0:T(8,128)(2,1)} %get-tuple-element.20.refs_0_), channel_id=1, source_target_pairs={{0,6},{1,7},{2,0},{3,1},{4,2},{5,3},{6,4},{7,5},{8,14},{9,15},{10,... | collective-permute-start | bytes 4718600 | tf_op jit(solution)/shard_map/ppermute | solution.py:723
  404.5 39.4 %collective-permute-start = (bf16[8,32,3072]{2,1,0:T(8,128)(2,1)}, bf16[8,32,3072]{2,1,0:T(8,128)(2,1)}, u32[]{:S(2)}, u32[]{:S(2)}) collective-permute-start(bf16[8,32,3072]{2,1,0:T(8,128)(2,1)} %get-tuple-element.20.refs_0_), channel_id=1, source_target_pairs={{0,2},{1,3},{2,4},{3,5},{4,6},{5,7},{6,0},{7,1},{8,10},{9,11},{10,... | collective-permute-start | bytes 4718600 | tf_op jit(solution)/shard_map/ppermute | solution.py:723
  404.7 72.0 %collective-permute-start.6 = (bf16[8,32,3072]{2,1,0:T(8,128)(2,1)}, bf16[8,32,3072]{2,1,0:T(8,128)(2,1)}, u32[]{:S(2)}, u32[]{:S(2)}) collective-permute-start(bf16[8,32,3072]{2,1,0:T(8,128)(2,1)} %get-tuple-element.20.refs_0_), channel_id=1, source_target_pairs={{0,1},{1,0},{2,3},{3,2},{4,5},{5,4},{6,7},{7,6},{8,9},{9,8},{10,11... | collective-permute-start | bytes 4718600 | tf_op jit(solution)/shard_map/ppermute | solution.py:723
  441.4 33.0 %collective-permute-start.3 = (bf16[8,16,3072]{2,1,0:T(8,128)(2,1)}, bf16[8,16,3072]{2,1,0:T(8,128)(2,1)}, u32[]{:S(2)}, u32[]{:S(2)}) collective-permute-start(bf16[8,16,3072]{2,1,0:T(8,128)(2,1)} %slice.17), channel_id=1, source_target_pairs={{0,6},{1,7},{2,0},{3,1},{4,2},{5,3},{6,4},{7,5},{8,14},{9,15},{10,... | collective-permute-start | bytes 2359304 | tf_op jit(solution)/shard_map/ppermute | solution.py:723
  446.0 29.1 %collective-permute-start.1 = (bf16[8,16,3072]{2,1,0:T(8,128)(2,1)}, bf16[8,16,3072]{2,1,0:T(8,128)(2,1)}, u32[]{:S(2)}, u32[]{:S(2)}) collective-permute-start(bf16[8,16,3072]{2,1,0:T(8,128)(2,1)} %slice.16), channel_id=1, source_target_pairs={{0,2},{1,3},{2,4},{3,5},{4,6},{5,7},{6,0},{7,1},{8,10},{9,11},{10,... | collective-permute-start | bytes 2359304 | tf_op jit(solution)/shard_map/ppermute | solution.py:723
  446.0 30.7 %collective-permute-start.8 = (bf16[8,32,3072]{2,1,0:T(8,128)(2,1)}, bf16[8,32,3072]{2,1,0:T(8,128)(2,1)}, u32[]{:S(2)}, u32[]{:S(2)}) collective-permute-start(bf16[8,32,3072]{2,1,0:T(8,128)(2,1)} %collective-permute-done.2.refs_2_), channel_id=1, source_target_pairs={{0,1},{1,0},{2,3},{3,2},{4,5},{5,4},{6,7},{7,6},{8,9},{9,8},{10,11... | collective-permute-start | bytes 4718600 | tf_op jit(solution)/shard_map/ppermute | solution.py:723
  447.2 29.4 %collective-permute-start.7 = (bf16[8,32,3072]{2,1,0:T(8,128)(2,1)}, bf16[8,32,3072]{2,1,0:T(8,128)(2,1)}, u32[]{:S(2)}, u32[]{:S(2)}) collective-permute-start(bf16[8,32,3072]{2,1,0:T(8,128)(2,1)} %collective-permute-done.refs_1_), channel_id=1, source_target_pairs={{0,1},{1,0},{2,3},{3,2},{4,5},{5,4},{6,7},{7,6},{8,9},{9,8},{10,11... | collective-permute-start | bytes 4718600 | tf_op jit(solution)/shard_map/ppermute | solution.py:723
  474.4 9.5 %collective-permute-start.5 = (bf16[8,16,3072]{2,1,0:T(8,128)(2,1)}, bf16[8,16,3072]{2,1,0:T(8,128)(2,1)}, u32[]{:S(2)}, u32[]{:S(2)}) collective-permute-start(bf16[8,16,3072]{2,1,0:T(8,128)(2,1)} %collective-permute-done.3.refs_1_), channel_id=1, source_target_pairs={{0,1},{1,0},{2,3},{3,2},{4,5},{5,4},{6,7},{7,6},{8,9},{9,8},{10,11... | collective-permute-start | bytes 2359304 | tf_op jit(solution)/shard_map/ppermute | solution.py:723
  475.0 8.9 %collective-permute-start.4 = (bf16[8,16,3072]{2,1,0:T(8,128)(2,1)}, bf16[8,16,3072]{2,1,0:T(8,128)(2,1)}, u32[]{:S(2)}, u32[]{:S(2)}) collective-permute-start(bf16[8,16,3072]{2,1,0:T(8,128)(2,1)} %collective-permute-done.1.refs_0_), channel_id=1, source_target_pairs={{0,1},{1,0},{2,3},{3,2},{4,5},{5,4},{6,7},{7,6},{8,9},{9,8},{10,11... | collective-permute-start | bytes 2359304 | tf_op jit(solution)/shard_map/ppermute | solution.py:723

commit v7 on v6

--- a/solution.py
+++ b/solution.py
@@ -66,9 +66,9 @@
 
 
 def body(heads, x, dy, dyf, wqkv_h, wo_h, wu_h, wd_h, ga, gm,
-         ys_o, dx_o, dwq_o, dwo_o, dwu_o, dwd_o, nm_o, g_o, a_o, o_o, qkv_o, h_o, dp_o, dq_o, py_o, dgain_o,
+         ya_o, yb_o, dx_o, dwq_o, dwo_o, dwu_o, dwd_o, nm_o, g_o, a_o, o_o, qkv_o, h_o, dp_o, dq_o, py_o, dgain_o,
          wqkv, wo, wu, wd, S, RD, R1, R2, xb, ab, nb, dyb, gb, qb, qb2, dqb, dqt, ob, obt, hb_, dpb, pyb,
-         xs, xm, gs, own, dgb, dgs, lsem, wsem, dsem, ysem, ssem1, rsem1, ssem, rsem):
+         xs, xm, gs, own, dgb, dgs, lsem, wsem, dsem, ysem, qsem, ssem1, rsem1, ssem, rsem):
     nseq, slen, dm = x.shape
     tok = nseq * slen
     half = slen // CORES
@@ -100,7 +100,13 @@
     def lc(src, dst, k):
         return pltpu.make_async_copy(src, dst, lsem.at[k])
 
-    w1 = (lc(wqkv_h, wqkv, 0), lc(wo_h, wo, 1))
+    qt = tile_of(3 * wo.shape[0], 3 * wo.shape[0] // 2)
+
+    def ld_wqkv(t):
+        r = pl.ds(pl.multiple_of(t * qt, qt), qt)
+        return pltpu.make_async_copy(wqkv_h.at[r], wqkv.at[r], qsem.at[t])
+
+    ld_wo = lc(wo_h, wo, 1)
     w2 = (lc(wu_h, wu, 2), lc(wd_h, wd, 3))
 
     def ld_x(c):
@@ -236,6 +242,11 @@
             o = pl.ds(3 * blk + k * hb, hb)
             tot = S[f, s, o].astype(F32) + R1[f, s, 1 - k, pl.ds(0 if k else hb, hb)].astype(F32) + R2[f, s, k].astype(F32)
             if fl == 1:
+                if k == 0:
+                    @pl.when(c == 0)
+                    def _():
+                        xs_ld.wait()
+
                 z = (xs[c, q].astype(F32) + tot).astype(BF)
                 xm[c, q] = z
                 xh, _ = ln_parts(z.astype(F32))
@@ -304,9 +315,7 @@
         ex = jnp.exp(s - jnp.max(s, axis=0, keepdims=True))
         return qt, kt, vt, ex / jnp.sum(ex, axis=0, keepdims=True)
 
-    def stage_F1(c):
-        ld_x(c).wait()
-
+    def norm_rows():
         def ln(t, _):
             r = pl.ds(pl.multiple_of(t * hb, hb), hb)
             xh, _ = ln_parts(xb[r].astype(F32))
@@ -314,21 +323,24 @@
             return 0
 
         lax.fori_loop(0, slen // hb, ln, 0, unroll=4)
+
+    def stage_F1(c):
+        @pl.when(c > 0)
+        def _():
+            ld_x(c).wait()
+            norm_rows()
+
         st_a(c).start()
 
-        @pl.when(c == 0)
-        def _():
-            for w in w1:
-                w.wait()
-            xs_ld.wait()
-
         @pl.when(c + 1 < nseq)
         def _():
             ld_x(c + 1).start()
 
-        qt = tile_of(3 * he, 3 * he // 2)
-
         def qkv(t, _):
+            @pl.when(c == 0)
+            def _():
+                ld_wqkv(t).wait()
+
             r = pl.ds(pl.multiple_of(t * qt, qt), qt)
             qb[r] = dg(wqkv[r], ab[...], 1, 1).astype(BF)
             return 0
@@ -347,6 +359,14 @@
             ob[:, t * tr:(t + 1) * tr] = obt[t * tr:(t + 1) * tr].T
         st_o(c).start()
         n = tile_of(dm, 1024)
+
+        @pl.when(c == 0)
+        def _():
+            ld_wo.wait()
+            for w in w2:
+                w.start()
+            for w in (xs_ld, dys_ld, ld_dy(0)):
+                w.start()
 
         def proj(t, _):
             col = pl.multiple_of(t * n, n)
@@ -557,18 +577,16 @@
             for cp in b_loads(0):
                 cp.start()
 
+    ld_x(0).start()
+    for t in (0, 1):
+        ld_wqkv(t).start()
+    ld_wo.start()
     barrier = pltpu.get_barrier_semaphore()
     for k in range(1, tpn):
         pl.semaphore_signal(barrier, inc=1, device_id={'tp': (tp + k) % tpn}, device_id_type=MESH)
-    ld_x(0).start()
-    for w in w1:
-        w.start()
-    xs_ld.start()
-    for w in w2:
-        w.start()
-    dys_ld.start()
-    ld_dy(0).start()
     dgb[...] = jnp.zeros_like(dgb)
+    ld_x(0).wait()
+    norm_rows()
     pl.semaphore_wait(barrier, tpn - 1)
 
     run = {'F1': stage_F1, 'MU': stage_MU, 'MD': stage_MD, 'MY': stage_MY, 'B2': stage_B2,
@@ -593,8 +611,9 @@
 
     lax.fori_loop(0, max(count(n) + l for n, l in order), step, 0)
 
-    ys = lc(xm, ys_o, 18)
-    ys.start()
+    ys = [lc(xm.at[pl.ds(k * nseq // 2, nseq // 2)], r, (0, 18)[k]) for k, r in enumerate((ya_o, yb_o))]
+    for cp in ys:
+        cp.start()
     for b in (0, 1):
         o_store(0, b).wait()
     for k in range(1, tpn):
@@ -605,7 +624,8 @@
     dgain_o[...] = tot
     for k in range(1, tpn):
         c_gain(k).wait_send()
-    ys.wait()
+    for cp in ys:
+        cp.wait()
 
 
 def mega(x, dy, wqkv, wo, wu, wd, ga, gm, heads):
@@ -620,7 +640,7 @@
         return jax.ShapeDtypeStruct(shape, BF)
 
     act = arr(tok, dm)
-    outs = (arr(nseq, blk, dm), act, arr(3 * he, dm), arr(he, dm), arr(dm, ff), arr(ff, dm), act, act, act, arr(tok, he),
+    outs = (arr(nseq // 2, blk, dm), arr(nseq // 2, blk, dm), act, arr(3 * he, dm), arr(he, dm), arr(dm, ff), arr(ff, dm), act, act, act, arr(tok, he),
             arr(nseq, 3 * he, slen), arr(tok, ff), arr(tok, ff), arr(tok, 3 * he), act, jax.ShapeDtypeStruct((2, dm), F32))
     hbm = pl.BlockSpec(memory_space=pl.ANY)
     vm = pl.BlockSpec(memory_space=pltpu.VMEM)
@@ -635,7 +655,7 @@
         V((nseq, blk, dm), BF), V((nseq, blk, dm), BF), V((nseq, blk, dm), BF), V((2, 2, blk, dm), BF), V((2, dm), F32),
         V((CHIPS * CORES, 2, dm), F32),
         pltpu.SemaphoreType.DMA((23,)), pltpu.SemaphoreType.DMA((6, 2)), pltpu.SemaphoreType.DMA((2, CHIPS * CORES)),
-        pltpu.SemaphoreType.DMA((2, CHIPS)),
+        pltpu.SemaphoreType.DMA((2, CHIPS)), pltpu.SemaphoreType.DMA((2,)),
         pltpu.SemaphoreType.DMA((2, 5 * SLOTS)), pltpu.SemaphoreType.DMA((2, 5 * SLOTS)),
         pltpu.SemaphoreType.DMA((2, 8 * nseq)), pltpu.SemaphoreType.DMA((2, 8 * nseq)),
     ]
@@ -645,7 +665,7 @@
         name='mega',
         out_shape=outs,
         in_specs=[hbm] * 7 + [vm] * 2,
-        out_specs=(hbm,) * 15 + (vm,),
+        out_specs=(hbm,) * 16 + (vm,),
         scratch_shapes=scratch,
         compiler_params=pltpu.CompilerParams(collective_id=0, has_side_effects=True, vmem_limit_bytes=VMEM_BYTES),
         cost_estimate=pl.CostEstimate(flops=flops, bytes_accessed=12 * nseq * slen * dm * 2, transcendentals=0),
@@ -674,14 +694,14 @@
     hbm = pl.BlockSpec(memory_space=pl.ANY)
     size = sum(v.size for v in arrays)
     return pl.pallas_call(
-        move, name='copy_all', in_specs=[hbm] * n, out_specs=(hbm,) * n,
+        move, in_specs=[hbm] * n, out_specs=(hbm,) * n,
         out_shape=tuple(jax.ShapeDtypeStruct(v.shape, v.dtype) for v in arrays),
         scratch_shapes=[pltpu.VMEM(v.shape, v.dtype) for v in arrays] + [pltpu.SemaphoreType.DMA((len(cuts),))] * 2,
         compiler_params=pltpu.CompilerParams(vmem_limit_bytes=VMEM_BYTES),
         cost_estimate=pl.CostEstimate(flops=size * 500, bytes_accessed=4 * size, transcendentals=0))(*arrays)
 
 
-def placed(out, pieces, shape, rows_of):
+def placed(out, pieces, shape, at_of):
     n = len(pieces)
     given = [] if out is None else [out]
 
@@ -689,10 +709,11 @@
         src, dst = refs[:n], refs[n + len(given)]
         buf, isem, osem = refs[n + len(given) + 1:-2], refs[-2], refs[-1]
         tp = lax.axis_index('tp')
-        at = rows_of(tp // CORES, tp % CORES)
+        at = at_of(tp // CORES, tp % CORES)
         into = [pltpu.make_async_copy(src[k], buf[k], isem.at[k]) for k in range(n)]
         outc = [pltpu.make_async_copy(
-            buf[k], dst.at[:, pl.ds(pl.multiple_of(at[k], pieces[k].shape[1]), pieces[k].shape[1])], osem.at[k]) for k in range(n)]
+            buf[k], dst.at[pl.ds(at[k][0], p.shape[0]), pl.ds(pl.multiple_of(at[k][1], p.shape[1]), p.shape[1])], osem.at[k])
+            for k, p in enumerate(pieces)]
         for cp in into:
             cp.start()
         for k in range(n):
@@ -722,26 +743,26 @@
             perm.append((t, ((ch + chips_by) % CHIPS) * CORES + (co + cores_by) % CORES))
         return lax.ppermute(v, 'tp', perm)
 
-    def gather(v):
-        nseq, blk, dm = v.shape
-        hb = blk // 2
+    def gather(va, vb):
+        ns, blk, dm = va.shape
         half = blk * CHIPS
-        v_l, v_r = hop(v, 1, 0), hop(v, -1, 0)
-        v_x = hop(v, 0, 1)
-        o0, o1 = hop(v_l[:, :hb], 1, 0), hop(v_r[:, hb:], -1, 0)
-        v_lx, v_rx = hop(v_l, 0, 1), hop(v_r, 0, 1)
-        o0x, o1x = hop(o0, 0, 1), hop(o1, 0, 1)
-
-        def near(chip, core):
-            chips = [chip, (chip + CHIPS - 1) % CHIPS, (chip + 1) % CHIPS]
-            return [co * half + ch * blk for co in (core, 1 - core) for ch in chips]
-
-        def far(chip, core):
+        la, rb = hop(va, 1, 0), hop(vb, -1, 0)
+        lb, ra = hop(vb, 1, 0), hop(va, -1, 0)
+        oa, ob = hop(la, 1, 0), hop(rb, -1, 0)
+        near = [va, vb, la, lb, ra, rb]
+        near += [hop(p, 0, 1) for p in near]
+        far = [oa, ob, hop(oa, 0, 1), hop(ob, 0, 1)]
+
+        def near_at(chip, core):
+            chips = (chip, (chip + CHIPS - 1) % CHIPS, (chip + 1) % CHIPS)
+            return [(k * ns, co * half + ch * blk) for co in (core, 1 - core) for ch in chips for k in (0, 1)]
+
+        def far_at(chip, core):
             o = ((chip + 2) % CHIPS) * blk
-            return [co * half + o + k for co in (core, 1 - core) for k in (0, hb)]
-
-        out = placed(None, (v, v_l, v_r, v_x, v_lx, v_rx), (nseq, half * CORES, dm), near)
-        return placed(out, (o0, o1, o0x, o1x), out.shape, far)
+            return [(k * ns, co * half + o) for co in (core, 1 - core) for k in (0, 1)]
+
+        out = placed(None, near, (2 * ns, half * CORES, dm), near_at)
+        return placed(out, far, out.shape, far_at)
 
     def step(x_in, gain_attn, w_qkv, w_out, gain_mlp, w_up, w_down, dy_out):
         heads, e = w_qkv.shape[3:]
@@ -750,10 +771,11 @@
         wqkv = jnp.transpose(w_qkv[0], (1, 2, 3, 0)).reshape(3 * he, dm)
         wo = w_out[0].reshape(he, dm)
         out = mega(x_in, dy_out, wqkv, wo, w_up[0], w_down[0], gain_attn, gain_mlp, heads)
-        ys, dx, dwq, dwo, dwu, dwd = out[:6]
+        ya, yb, dx, dwq, dwo, dwu, dwd = out[:7]
         dgain = out[-1]
-        dx, dwu, dwd, dwq, dwo = copied((dx, dwu, dwd, dwq, dwo))
-        y = gather(ys)
+        dx, dwu, dwo = copied((dx, dwu, dwo))
+        dwd, dwq = copied((dwd, dwq))
+        y = gather(ya, yb)
         dwq = jnp.transpose(dwq.reshape(3, heads, e, dm), (3, 0, 1, 2))
         return (y, dx.reshape(x_in.shape), dgain[0:1], dwq[None], dwo.reshape(1, heads, e, dm),
                 dgain[1:2], dwu[None], dwd[None])

time: 488 us -> 485 us (level)
  starting transfers between devices: 6.74 us -> 13.8 us
  waiting for transfers between devices: 34 us -> 28.1 us
    ppermute x9 -> x14, starting transfers between devices: 6.74 us -> 13.8 us  [hop(): return lax.ppermute(v, 'tp', perm)]
    ppermute x9 -> x14, waiting for transfers between devices: 34 us -> 28.1 us  [hop(): return lax.ppermute(v, 'tp', perm)]
    pallas_call x1 -> x2, Pallas kernels: 27.2 us -> 28.8 us  [copied(): pl.pallas_call(move, in_specs=[hbm] * n, out_specs=(hbm,) * n, out_shape=...]
  transfers between devices with their start and end apart: 9 -> 14, of which waited for: 1 -> 3; matrix products, arithmetic and copies ran while one was open for 1% -> 0% of each run, Pallas kernels for 7% -> 7%
where the time goes in v7:
time: 485 us
  Pallas kernels  439 us (91%)
  waiting for transfers between devices  28.1 us (6%)
  starting transfers between devices  13.8 us (3%)
    pallas_call x1, Pallas kernels, mega(): pl.pallas_call(functools.partial(body, heads), name='mega', out_shape=out...  400 us
    pallas_call x2, Pallas kernels, copied(): pl.pallas_call(move, in_specs=[hbm] * n, out_specs=(hbm,) * n, out_shape=...  28.8 us
    ppermute x14, waiting for transfers between devices, hop(): return lax.ppermute(v, 'tp', perm)  28.1 us
    ppermute x14, starting transfers between devices, hop(): return lax.ppermute(v, 'tp', perm)  13.8 us
    pallas_call x2, Pallas kernels, placed(): pl.pallas_call(put, in_specs=[hbm] * (n + len(given)), out_specs=hbm, out...  10.1 us
  transfers between devices with their start and end apart: 14, of which 3 were waited for; matrix products, arithmetic and copies ran while one was open for 0% of the time, Pallas kernels for 7%

profile of v7, /device:TPU:81, one launch (start us, length us, event | category | flops | bytes accessed | tf_op | source)
XLA Modules:
  0.0 484.7 jit_solution(17450660481044596320)
XLA Ops:
  0.6 400.2 %mega.1 = (bf16[4,32,3072]{2,1,0:T(8,128)(2,1)}, bf16[4,32,3072]{2,1,0:T(8,128)(2,1)}, bf16[2048,3072]{1,0:T(8,128)(2,1)}, bf16[1152,3072]{1,0:T(8,128)(2,1)}, b...) custom-call(bf16[8,256,3072]{2,1,0:T(8,128)(2,1)} %x.1, ...), custom_call_target="tpu_custom_call" | custom-call | flops 115964116992 | bytes 150994944 | tf_op jit(solution)/shard_map/mega/pallas_call | solution.py:663
  400.9 0.2 collective-permute-start.8
  401.1 1.3 collective-permute-start.7
  402.4 0.2 collective-permute-start
  402.6 2.5 collective-permute-start.2
  405.1 1.2 collective-permute-start.9
  406.3 0.0 collective-permute-done.8.refs_6_
  406.3 0.0 collective-permute-start.6
  406.3 13.9 %collective-permute-done.7.refs_4_ = bf16[4,32,3072]{2,1,0:T(8,128)(2,1)S(1)} collective-permute-done((bf16[4,32,3072]{2,1,0:T(8,128)(2,1)}, bf16[4,32,3072]{2,1,0:T(8,128)(2,1)S(1)}, u32[]{:S(2)}, u32[]{:S(2)}) %collective-permute-start.7) | collective-permute-done | bytes 786464 | tf_op jit(solution)/shard_map/ppermute | solution.py:744
  420.2 0.0 copy-start
  420.2 0.9 copy-done
  421.1 2.0 collective-permute-start.12
  423.0 0.0 collective-permute-done.refs_2_
  423.0 0.1 collective-permute-start.1
  423.1 13.9 %collective-permute-done.2.refs_5_ = bf16[4,32,3072]{2,1,0:T(8,128)(2,1)} collective-permute-done((bf16[4,32,3072]{2,1,0:T(8,128)(2,1)}, bf16[4,32,3072]{2,1,0:T(8,128)(2,1)}, u32[]{:S(2)}, u32[]{:S(2)}) %collective-permute-start.2) | collective-permute-done | bytes 786464 | tf_op jit(solution)/shard_map/ppermute | solution.py:744
  437.0 2.5 collective-permute-start.3
  439.5 1.4 fusion
  440.9 0.0 collective-permute-done.9.refs_7_
  440.9 0.0 copy-start.1
  440.9 1.6 collective-permute-start.10
  442.5 0.0 collective-permute-done.6.refs_3_
  442.6 0.1 collective-permute-start.13
  442.7 0.0 collective-permute-done.12.refs_10_
  442.7 0.0 copy-done.1
  442.7 0.0 copy-start.2
  442.7 0.6 collective-permute-start.11
  443.3 0.3 copy-done.2
  443.6 12.1 %shard_map.146 = (bf16[1536,3072]{1,0:T(8,128)(2,1)}, bf16[1152,3072]{1,0:T(8,128)(2,1)}) custom-call(bf16[1536,3072]{1,0:T(8,128)(2,1)} %get-tuple-element.28.refs_0_, bf16[1152,3072]{1,0:T(8,128)(2,1)} %get-tuple-element.29.refs_1_), custom_call_target="tpu_custom_call" | custom-call | flops 4128768000 | bytes 33030144 | tf_op jit(solution)/shard_map/pallas_call | solution.py:696
  455.7 0.3 collective-permute-done.1.refs_0_
  456.1 1.5 collective-permute-start.4
  457.6 0.0 collective-permute-done.3.refs_1_
  457.6 0.0 collective-permute-start.5
  457.6 16.7 %shard_map.145 = (bf16[2048,3072]{1,0:T(8,128)(2,1)}, bf16[3072,1536]{1,0:T(8,128)(2,1)}, bf16[384,3072]{1,0:T(8,128)(2,1)}) custom-call(bf16[2048,3072]{1,0:T(8,128)(2,1)} %get-tuple-element.23.refs_0_, bf16[3072,1536]{1,0:T(8,128)(2,1)} %get-tuple-element.24.refs_1_, bf16[384,3072]{1,0:T(8,128)(2,1)} %get-tuple-element.25.refs_2_), custom_call_target="tpu_custom_call" | custom-call | flops 6094848000 | bytes 48758784 | tf_op jit(solution)/shard_map/pallas_call | solution.py:696
  474.3 0.0 collective-permute-done.10.refs_8_
  474.3 0.0 collective-permute-done.11.refs_9_
  474.3 0.0 collective-permute-done.13.refs_11_
  474.3 7.3 %shard_map.143.refs_4_ = bf16[8,256,3072]{2,1,0:T(8,128)(2,1)} custom-call(bf16[4,32,3072]{2,1,0:T(8,128)(2,1)} %get-tuple-element.21.refs_0_, bf16[4,32,3072]{2,1,0:T(8,128)(2,1)} %get-tuple-element.22.refs_1_, bf16[4,32,3072]{2,1,0:T(8,128)(2,1)} %collective-permute-done.refs_2_, bf16[4,32,3072]{2,1,0:T(8,128)(2,1)} %collective-permute-done.6.refs_3_, ...), custom_call_target="tpu_custom_call" | custom-call | flops 2359296000 | tf_op jit(solution)/shard_map/pallas_call | solution.py:726
  481.6 0.0 collective-permute-done.4.refs_2_
  481.6 0.0 collective-permute-done.5.refs_3_
  481.6 2.9 shard_map.144
Async XLA Ops:
  400.9 5.4 %collective-permute-start.8 = (bf16[4,32,3072]{2,1,0:T(8,128)(2,1)}, bf16[4,32,3072]{2,1,0:T(8,128)(2,1)}, u32[]{:S(2)}, u32[]{:S(2)}) collective-permute-start(bf16[4,32,3072]{2,1,0:T(8,128)(2,1)} %get-tuple-element.21.refs_0_), channel_id=1, source_target_pairs={{0,1},{1,0},{2,3},{3,2},{4,5},{5,4},{6,7},{7,6},{8,9},{9,8},{10,11... | collective-permute-start | bytes 2359304 | tf_op jit(solution)/shard_map/ppermute | solution.py:744
  401.1 19.0 %collective-permute-start.7 = (bf16[4,32,3072]{2,1,0:T(8,128)(2,1)}, bf16[4,32,3072]{2,1,0:T(8,128)(2,1)S(1)}, u32[]{:S(2)}, u32[]{:S(2)}) collective-permute-start(bf16[4,32,3072]{2,1,0:T(8,128)(2,1)} %get-tuple-element.21.refs_0_), channel_id=1, source_target_pairs={{0,6},{1,7},{2,0},{3,1},{4,2},{5,3},{6,4},{7,5},{8,14},{9,15},{10,... | collective-permute-start | bytes 2359304 | tf_op jit(solution)/shard_map/ppermute | solution.py:744
  402.4 20.6 %collective-permute-start = (bf16[4,32,3072]{2,1,0:T(8,128)(2,1)}, bf16[4,32,3072]{2,1,0:T(8,128)(2,1)}, u32[]{:S(2)}, u32[]{:S(2)}) collective-permute-start(bf16[4,32,3072]{2,1,0:T(8,128)(2,1)} %get-tuple-element.21.refs_0_), channel_id=1, source_target_pairs={{0,2},{1,3},{2,4},{3,5},{4,6},{5,7},{6,0},{7,1},{8,10},{9,11},{10,... | collective-permute-start | bytes 2359304 | tf_op jit(solution)/shard_map/ppermute | solution.py:744
  402.6 34.4 %collective-permute-start.2 = (bf16[4,32,3072]{2,1,0:T(8,128)(2,1)}, bf16[4,32,3072]{2,1,0:T(8,128)(2,1)}, u32[]{:S(2)}, u32[]{:S(2)}) collective-permute-start(bf16[4,32,3072]{2,1,0:T(8,128)(2,1)} %get-tuple-element.22.refs_1_), channel_id=1, source_target_pairs={{0,6},{1,7},{2,0},{3,1},{4,2},{5,3},{6,4},{7,5},{8,14},{9,15},{10,... | collective-permute-start | bytes 2359304 | tf_op jit(solution)/shard_map/ppermute | solution.py:744
  405.1 35.9 %collective-permute-start.9 = (bf16[4,32,3072]{2,1,0:T(8,128)(2,1)}, bf16[4,32,3072]{2,1,0:T(8,128)(2,1)S(1)}, u32[]{:S(2)}, u32[]{:S(2)}) collective-permute-start(bf16[4,32,3072]{2,1,0:T(8,128)(2,1)} %get-tuple-element.22.refs_1_), channel_id=1, source_target_pairs={{0,1},{1,0},{2,3},{3,2},{4,5},{5,4},{6,7},{7,6},{8,9},{9,8},{10,11... | collective-permute-start | bytes 2359304 | tf_op jit(solution)/shard_map/ppermute | solution.py:744
  406.3 36.3 %collective-permute-start.6 = (bf16[4,32,3072]{2,1,0:T(8,128)(2,1)}, bf16[4,32,3072]{2,1,0:T(8,128)(2,1)}, u32[]{:S(2)}, u32[]{:S(2)}) collective-permute-start(bf16[4,32,3072]{2,1,0:T(8,128)(2,1)} %get-tuple-element.22.refs_1_), channel_id=1, source_target_pairs={{0,2},{1,3},{2,4},{3,5},{4,6},{5,7},{6,0},{7,1},{8,10},{9,11},{10,... | collective-permute-start | bytes 2359304 | tf_op jit(solution)/shard_map/ppermute | solution.py:744
  420.2 0.9 copy-start
  421.1 21.6 %collective-permute-start.12 = (bf16[4,32,3072]{2,1,0:T(8,128)(2,1)S(1)}, bf16[4,32,3072]{2,1,0:T(8,128)(2,1)S(1)}, u32[]{:S(2)}, u32[]{:S(2)}) collective-permute-start(bf16[4,32,3072]{2,1,0:T(8,128)(2,1)S(1)} %collective-permute-done.7.refs_4_), channel_id=1, source_target_pairs={{0,1},{1,0},{2,3},{3,2},{4,5},{5,4},{6,7},{7,6},{8,9},{9,8},{10,11... | collective-permute-start | bytes 2359304 | tf_op jit(solution)/shard_map/ppermute | solution.py:744
  423.0 33.0 %collective-permute-start.1 = (bf16[4,32,3072]{2,1,0:T(8,128)(2,1)}, bf16[4,32,3072]{2,1,0:T(8,128)(2,1)}, u32[]{:S(2)}, u32[]{:S(2)}) collective-permute-start(bf16[4,32,3072]{2,1,0:T(8,128)(2,1)} %collective-permute-done.refs_2_), channel_id=1, source_target_pairs={{0,2},{1,3},{2,4},{3,5},{4,6},{5,7},{6,0},{7,1},{8,10},{9,11},{10,... | collective-permute-start | bytes 2359304 | tf_op jit(solution)/shard_map/ppermute | solution.py:744
  437.0 20.6 %collective-permute-start.3 = (bf16[4,32,3072]{2,1,0:T(8,128)(2,1)}, bf16[4,32,3072]{2,1,0:T(8,128)(2,1)}, u32[]{:S(2)}, u32[]{:S(2)}) collective-permute-start(bf16[4,32,3072]{2,1,0:T(8,128)(2,1)} %collective-permute-done.2.refs_5_), channel_id=1, source_target_pairs={{0,6},{1,7},{2,0},{3,1},{4,2},{5,3},{6,4},{7,5},{8,14},{9,15},{10,... | collective-permute-start | bytes 2359304 | tf_op jit(solution)/shard_map/ppermute | solution.py:744
  440.9 1.8 copy-start.1
  440.9 33.4 %collective-permute-start.10 = (bf16[4,32,3072]{2,1,0:T(8,128)(2,1)}, bf16[4,32,3072]{2,1,0:T(8,128)(2,1)}, u32[]{:S(2)}, u32[]{:S(2)}) collective-permute-start(bf16[4,32,3072]{2,1,0:T(8,128)(2,1)} %collective-permute-done.refs_2_), channel_id=1, source_target_pairs={{0,1},{1,0},{2,3},{3,2},{4,5},{5,4},{6,7},{7,6},{8,9},{9,8},{10,11... | collective-permute-start | bytes 2359304 | tf_op jit(solution)/shard_map/ppermute | solution.py:744
  442.6 31.8 %collective-permute-start.13 = (bf16[4,32,3072]{2,1,0:T(8,128)(2,1)}, bf16[4,32,3072]{2,1,0:T(8,128)(2,1)}, u32[]{:S(2)}, u32[]{:S(2)}) collective-permute-start(bf16[4,32,3072]{2,1,0:T(8,128)(2,1)} %collective-permute-done.2.refs_5_), channel_id=1, source_target_pairs={{0,1},{1,0},{2,3},{3,2},{4,5},{5,4},{6,7},{7,6},{8,9},{9,8},{10,11... | collective-permute-start | bytes 2359304 | tf_op jit(solution)/shard_map/ppermute | solution.py:744
  442.7 0.9 copy-start.2
  442.7 31.6 %collective-permute-start.11 = (bf16[4,32,3072]{2,1,0:T(8,128)(2,1)}, bf16[4,32,3072]{2,1,0:T(8,128)(2,1)}, u32[]{:S(2)}, u32[]{:S(2)}) collective-permute-start(bf16[4,32,3072]{2,1,0:T(8,128)(2,1)} %collective-permute-done.6.refs_3_), channel_id=1, source_target_pairs={{0,1},{1,0},{2,3},{3,2},{4,5},{5,4},{6,7},{7,6},{8,9},{9,8},{10,11... | collective-permute-start | bytes 2359304 | tf_op jit(solution)/shard_map/ppermute | solution.py:744
  456.1 25.6 %collective-permute-start.4 = (bf16[4,32,3072]{2,1,0:T(8,128)(2,1)}, bf16[4,32,3072]{2,1,0:T(8,128)(2,1)}, u32[]{:S(2)}, u32[]{:S(2)}) collective-permute-start(bf16[4,32,3072]{2,1,0:T(8,128)(2,1)} %collective-permute-done.1.refs_0_), channel_id=1, source_target_pairs={{0,1},{1,0},{2,3},{3,2},{4,5},{5,4},{6,7},{7,6},{8,9},{9,8},{10,11... | collective-permute-start | bytes 2359304 | tf_op jit(solution)/shard_map/ppermute | solution.py:744
  457.6 24.1 %collective-permute-start.5 = (bf16[4,32,3072]{2,1,0:T(8,128)(2,1)}, bf16[4,32,3072]{2,1,0:T(8,128)(2,1)}, u32[]{:S(2)}, u32[]{:S(2)}) collective-permute-start(bf16[4,32,3072]{2,1,0:T(8,128)(2,1)} %collective-permute-done.3.refs_1_), channel_id=1, source_target_pairs={{0,1},{1,0},{2,3},{3,2},{4,5},{5,4},{6,7},{7,6},{8,9},{9,8},{10,11... | collective-permute-start | bytes 2359304 | tf_op jit(solution)/shard_map/ppermute | solution.py:744

commit v8 on v7

--- a/solution.py
+++ b/solution.py
@@ -23,10 +23,10 @@
 TILES = 2
 
 ORDER = (
-    ('e3', 15), ('MU', 8), ('b1', 3), ('d3', 12), ('WP', 10), ('a1', 2), ('B2', 16), ('F1', 1), ('f1', 7),
-    ('f3', 15), ('e1', 6), ('d1', 5), ('MD', 8), ('YS', 19), ('WG', 17), ('c3', 10), ('c5', 21), ('b5', 20),
-    ('c1', 3), ('a5', 19), ('YL', 18), ('d4', 20), ('e4', 22), ('MY', 8), ('f4', 23), ('c4', 18), ('b3', 9),
-    ('b4', 17), ('a3', 8), ('a4', 16),
+    ('e3', 15), ('b4', 18), ('e1', 7), ('f3', 16), ('MY', 9), ('a4', 17), ('b3', 10), ('WG', 17), ('a3', 9),
+    ('WP', 9), ('d1', 5), ('d3', 12), ('MU', 8), ('c5', 21), ('c1', 3), ('b1', 2), ('f4', 27), ('e4', 22),
+    ('b5', 20), ('a5', 19), ('B2', 16), ('a1', 1), ('MD', 8), ('YL', 18), ('f1', 7), ('c3', 10), ('F1', 0),
+    ('d4', 20), ('c4', 18), ('YS', 18),
 )
 
 
@@ -313,7 +313,7 @@
         keep = lax.broadcasted_iota(jnp.int32, (slen, slen), 0) <= lax.broadcasted_iota(jnp.int32, (slen, slen), 1)
         s = jnp.where(keep, s, -1e30)
         ex = jnp.exp(s - jnp.max(s, axis=0, keepdims=True))
-        return qt, kt, vt, ex / jnp.sum(ex, axis=0, keepdims=True)
+        return qt, kt, vt, ex * (1.0 / jnp.sum(ex, axis=0, keepdims=True))
 
     def norm_rows():
         def ln(t, _):
@@ -353,7 +353,7 @@
             obt[pl.ds(pl.multiple_of(hd * e, e), e)] = dg(vt, p.astype(BF), 1, 0).astype(BF)
             return 0
 
-        lax.fori_loop(0, heads, head, 0)
+        lax.fori_loop(0, heads, head, 0, unroll=True)
         tr = tile_of(he, 128)
         for t in range(he // tr):
             ob[:, t * tr:(t + 1) * tr] = obt[t * tr:(t + 1) * tr].T
@@ -385,7 +385,7 @@
 
         ld_nm(c).wait()
         ld_dy(c).wait()
-        n = tile_of(ff, 512)
+        n = tile_of(ff, 768)
 
         def up(t, _):
             col = pl.ds(pl.multiple_of(t * n, n), n)
@@ -404,7 +404,7 @@
         def _():
             ld_dy(c + 1).start()
 
-    m = tile_of(dm, 512)
+    m = tile_of(dm, 1024)
 
     def stage_MD(c):
         def down(t, _):
@@ -445,12 +445,12 @@
             dqt[pl.ds(pl.multiple_of(he + hd * e, e), e)] = dg(qt, ds, 1, 1).astype(BF)
             return 0
 
-        lax.fori_loop(0, heads, head, 0)
+        lax.fori_loop(0, heads, head, 0, unroll=2)
         tr = tile_of(3 * he, 128)
         for t in range(3 * he // tr):
             dqb[:, t * tr:(t + 1) * tr] = dqt[t * tr:(t + 1) * tr].T
         st_dq(c).start()
-        n = tile_of(dm, 512)
+        n = tile_of(dm, 1024)
 
         def proj(t, _):
             col = pl.multiple_of(t * n, n)
@@ -748,21 +748,25 @@
         half = blk * CHIPS
         la, rb = hop(va, 1, 0), hop(vb, -1, 0)
         lb, ra = hop(vb, 1, 0), hop(va, -1, 0)
-        oa, ob = hop(la, 1, 0), hop(rb, -1, 0)
+        n2 = ns // 2
+        opp = [(hop(la[k * n2:(k + 1) * n2], 1, 0), hop(rb[k * n2:(k + 1) * n2], -1, 0))
+               for k in (0, 1)]
         near = [va, vb, la, lb, ra, rb]
         near += [hop(p, 0, 1) for p in near]
-        far = [oa, ob, hop(oa, 0, 1), hop(ob, 0, 1)]
+        far = [p + tuple(hop(v, 0, 1) for v in p) for p in opp]
 
         def near_at(chip, core):
             chips = (chip, (chip + CHIPS - 1) % CHIPS, (chip + 1) % CHIPS)
             return [(k * ns, co * half + ch * blk) for co in (core, 1 - core) for ch in chips for k in (0, 1)]
 
-        def far_at(chip, core):
+        def far_at(part, chip, core):
             o = ((chip + 2) % CHIPS) * blk
-            return [(k * ns, co * half + o) for co in (core, 1 - core) for k in (0, 1)]
+            return [(k * ns + part * n2, co * half + o) for co in (core, 1 - core) for k in (0, 1)]
 
         out = placed(None, near, (2 * ns, half * CORES, dm), near_at)
-        return placed(out, far, out.shape, far_at)
+        for k in (0, 1):
+            out = placed(out, far[k], out.shape, functools.partial(far_at, k))
+        return out
 
     def step(x_in, gain_attn, w_qkv, w_out, gain_mlp, w_up, w_down, dy_out):
         heads, e = w_qkv.shape[3:]

time: 485 us -> 492 us (1.014)
  Pallas kernels: 439 us -> 429 us
  waiting for transfers between devices: 28.1 us -> 36.2 us
  starting transfers between devices: 13.8 us -> 19.3 us
    pallas_call x1, Pallas kernels: 400 us -> 389 us  [mega(): pl.pallas_call(functools.partial(body, heads), name='mega', out_shape=out...]
    ppermute x14 -> x18, waiting for transfers between devices: 28.1 us -> 36.2 us  [hop(): return lax.ppermute(v, 'tp', perm)]
    ppermute x14 -> x18, starting transfers between devices: 13.8 us -> 19.3 us  [hop(): return lax.ppermute(v, 'tp', perm)]
    pallas_call x2 -> x3, Pallas kernels: 10.1 us -> 11.7 us  [placed(): pl.pallas_call(put, in_specs=[hbm] * (n + len(given)), out_specs=hbm, out...]
  transfers between devices with their start and end apart: 14 -> 18, of which waited for: 3 -> 4; matrix products, arithmetic and copies ran while one was open for 0% -> 1% of each run, Pallas kernels for 7% -> 8%
where the time goes in v8:
time: 492 us; the launch traced here: 491 us
  Pallas kernels  429 us (87%)
  waiting for transfers between devices  36.2 us (7%)
  starting transfers between devices  19.3 us (4%)
  local copies, waits for them, and re-layouts  5.26 us (1%)
    pallas_call x1, Pallas kernels, mega(): pl.pallas_call(functools.partial(body, heads), name='mega', out_shape=out...  389 us
    ppermute x18, waiting for transfers between devices, hop(): return lax.ppermute(v, 'tp', perm)  36.2 us
    pallas_call x2, Pallas kernels, copied(): pl.pallas_call(move, in_specs=[hbm] * n, out_specs=(hbm,) * n, out_shape=...  28.8 us
    ppermute x18, starting transfers between devices, hop(): return lax.ppermute(v, 'tp', perm)  19.3 us
    pallas_call x3, Pallas kernels, placed(): pl.pallas_call(put, in_specs=[hbm] * (n + len(given)), out_specs=hbm, out...  11.7 us
  transfers between devices with their start and end apart: 18, of which 4 were waited for; matrix products, arithmetic and copies ran while one was open for 1% of the time, Pallas kernels for 8%

profile of v8, /device:TPU:81, one launch (start us, length us, event | category | flops | bytes accessed | tf_op | source)
XLA Modules:
  0.0 490.9 jit_solution(806145761617341602)
XLA Ops:
  0.6 388.7 %mega.1 = (bf16[4,32,3072]{2,1,0:T(8,128)(2,1)}, bf16[4,32,3072]{2,1,0:T(8,128)(2,1)}, bf16[2048,3072]{1,0:T(8,128)(2,1)}, bf16[1152,3072]{1,0:T(8,128)(2,1)}, b...) custom-call(bf16[8,256,3072]{2,1,0:T(8,128)(2,1)} %x.1, ...), custom_call_target="tpu_custom_call" | custom-call | flops 115964116992 | bytes 150994944 | tf_op jit(solution)/shard_map/mega/pallas_call | solution.py:663
  389.3 0.1 collective-permute-start
  389.4 2.6 collective-permute-start.2
  392.1 1.0 collective-permute-start.12
  393.1 0.0 collective-permute-start.11
  393.1 0.0 collective-permute-start.13
  393.1 16.5 %collective-permute-done.refs_2_ = bf16[4,32,3072]{2,1,0:T(8,128)(2,1)} collective-permute-done((bf16[4,32,3072]{2,1,0:T(8,128)(2,1)}, bf16[4,32,3072]{2,1,0:T(8,128)(2,1)}, u32[]{:S(2)}, u32[]{:S(2)}) %collective-permute-start) | collective-permute-done | bytes 786464 | tf_op jit(solution)/shard_map/ppermute | solution.py:744
  409.6 0.0 collective-permute-start.10
  409.6 1.2 fusion.1
  410.8 0.0 collective-permute-done.2.refs_5_
  410.8 0.1 collective-permute-start.6
  410.9 1.9 fusion
  412.8 0.0 collective-permute-done.12.refs_6_
  412.9 0.6 collective-permute-start.1
  413.4 12.0 %collective-permute-done.11.refs_4_ = bf16[4,32,3072]{2,1,0:T(8,128)(2,1)} collective-permute-done((bf16[4,32,3072]{2,1,0:T(8,128)(2,1)}, bf16[4,32,3072]{2,1,0:T(8,128)(2,1)}, u32[]{:S(2)}, u32[]{:S(2)}) %collective-permute-start.11) | collective-permute-done | bytes 786464 | tf_op jit(solution)/shard_map/ppermute | solution.py:744
  425.5 3.4 collective-permute-start.7
  428.9 0.0 collective-permute-done.13.refs_7_
  428.9 1.8 collective-permute-start.14
  430.7 0.0 collective-permute-done.10.refs_3_
  430.7 2.1 collective-permute-start.16
  432.8 4.5 collective-permute-done.6.refs_0_
  437.3 3.8 collective-permute-start.15
  441.2 1.4 fusion.2
  442.6 3.1 collective-permute-done.1.refs_0_
  445.7 0.0 collective-permute-start.3
  445.8 0.0 collective-permute-done.7.refs_1_
  445.8 0.7 copy-done
  446.5 2.1 collective-permute-start.17
  448.6 0.0 copy-done.1
  448.6 0.0 copy-done.2
  448.6 16.7 %shard_map.146 = (bf16[2048,3072]{1,0:T(8,128)(2,1)}, bf16[3072,1536]{1,0:T(8,128)(2,1)}, bf16[384,3072]{1,0:T(8,128)(2,1)}) custom-call(bf16[2048,3072]{1,0:T(8,128)(2,1)} %get-tuple-element.23.refs_0_, bf16[3072,1536]{1,0:T(8,128)(2,1)} %get-tuple-element.24.refs_1_, bf16[384,3072]{1,0:T(8,128)(2,1)} %get-tuple-element.25.refs_2_), custom_call_target="tpu_custom_call" | custom-call | flops 6094848000 | bytes 48758784 | tf_op jit(solution)/shard_map/pallas_call | solution.py:696
  465.3 0.0 collective-permute-done.3.refs_1_
  465.4 0.9 collective-permute-start.8
  466.2 0.0 collective-permute-done.16.refs_10_
  466.2 0.1 collective-permute-start.4
  466.3 0.0 collective-permute-done.14.refs_8_
  466.4 0.4 collective-permute-start.9
  466.7 0.0 collective-permute-done.15.refs_9_
  466.7 0.1 collective-permute-start.5
  466.9 12.1 %shard_map.147 = (bf16[1536,3072]{1,0:T(8,128)(2,1)}, bf16[1152,3072]{1,0:T(8,128)(2,1)}) custom-call(bf16[1536,3072]{1,0:T(8,128)(2,1)} %get-tuple-element.28.refs_0_, bf16[1152,3072]{1,0:T(8,128)(2,1)} %get-tuple-element.29.refs_1_), custom_call_target="tpu_custom_call" | custom-call | flops 4128768000 | bytes 33030144 | tf_op jit(solution)/shard_map/pallas_call | solution.py:696
  479.0 0.0 collective-permute-done.17.refs_11_
  479.0 7.3 %shard_map.143.refs_4_ = bf16[8,256,3072]{2,1,0:T(8,128)(2,1)} custom-call(bf16[4,32,3072]{2,1,0:T(8,128)(2,1)} %get-tuple-element.21.refs_0_, bf16[4,32,3072]{2,1,0:T(8,128)(2,1)} %get-tuple-element.22.refs_1_, bf16[4,32,3072]{2,1,0:T(8,128)(2,1)} %collective-permute-done.refs_2_, bf16[4,32,3072]{2,1,0:T(8,128)(2,1)} %collective-permute-done.10.refs_3_, ...), custom_call_target="tpu_custom_call" | custom-call | flops 2359296000 | tf_op jit(solution)/shard_map/pallas_call | solution.py:726
  486.3 0.0 collective-permute-done.8.refs_2_
  486.3 0.0 collective-permute-done.9.refs_3_
  486.3 2.2 shard_map.144.refs_4_
  488.5 0.0 collective-permute-done.4.refs_2_
  488.5 0.0 collective-permute-done.5.refs_3_
  488.5 2.2 shard_map.145
  (3 shorter events, 0.0 us)
Async XLA Ops:
  389.3 20.3 %collective-permute-start = (bf16[4,32,3072]{2,1,0:T(8,128)(2,1)}, bf16[4,32,3072]{2,1,0:T(8,128)(2,1)}, u32[]{:S(2)}, u32[]{:S(2)}) collective-permute-start(bf16[4,32,3072]{2,1,0:T(8,128)(2,1)} %get-tuple-element.21.refs_0_), channel_id=1, source_target_pairs={{0,2},{1,3},{2,4},{3,5},{4,6},{5,7},{6,0},{7,1},{8,10},{9,11},{10,... | collective-permute-start | bytes 2359304 | tf_op jit(solution)/shard_map/ppermute | solution.py:744
  389.4 21.4 %collective-permute-start.2 = (bf16[4,32,3072]{2,1,0:T(8,128)(2,1)}, bf16[4,32,3072]{2,1,0:T(8,128)(2,1)}, u32[]{:S(2)}, u32[]{:S(2)}) collective-permute-start(bf16[4,32,3072]{2,1,0:T(8,128)(2,1)} %get-tuple-element.22.refs_1_), channel_id=1, source_target_pairs={{0,6},{1,7},{2,0},{3,1},{4,2},{5,3},{6,4},{7,5},{8,14},{9,15},{10,... | collective-permute-start | bytes 2359304 | tf_op jit(solution)/shard_map/ppermute | solution.py:744
  392.1 20.8 %collective-permute-start.12 = (bf16[4,32,3072]{2,1,0:T(8,128)(2,1)}, bf16[4,32,3072]{2,1,0:T(8,128)(2,1)}, u32[]{:S(2)}, u32[]{:S(2)}) collective-permute-start(bf16[4,32,3072]{2,1,0:T(8,128)(2,1)} %get-tuple-element.21.refs_0_), channel_id=1, source_target_pairs={{0,1},{1,0},{2,3},{3,2},{4,5},{5,4},{6,7},{7,6},{8,9},{9,8},{10,11... | collective-permute-start | bytes 2359304 | tf_op jit(solution)/shard_map/ppermute | solution.py:744
  393.1 32.4 %collective-permute-start.11 = (bf16[4,32,3072]{2,1,0:T(8,128)(2,1)}, bf16[4,32,3072]{2,1,0:T(8,128)(2,1)}, u32[]{:S(2)}, u32[]{:S(2)}) collective-permute-start(bf16[4,32,3072]{2,1,0:T(8,128)(2,1)} %get-tuple-element.21.refs_0_), channel_id=1, source_target_pairs={{0,6},{1,7},{2,0},{3,1},{4,2},{5,3},{6,4},{7,5},{8,14},{9,15},{10,... | collective-permute-start | bytes 2359304 | tf_op jit(solution)/shard_map/ppermute | solution.py:744
  393.1 35.8 %collective-permute-start.13 = (bf16[4,32,3072]{2,1,0:T(8,128)(2,1)}, bf16[4,32,3072]{2,1,0:T(8,128)(2,1)}, u32[]{:S(2)}, u32[]{:S(2)}) collective-permute-start(bf16[4,32,3072]{2,1,0:T(8,128)(2,1)} %get-tuple-element.22.refs_1_), channel_id=1, source_target_pairs={{0,1},{1,0},{2,3},{3,2},{4,5},{5,4},{6,7},{7,6},{8,9},{9,8},{10,11... | collective-permute-start | bytes 2359304 | tf_op jit(solution)/shard_map/ppermute | solution.py:744
  409.6 21.1 %collective-permute-start.10 = (bf16[4,32,3072]{2,1,0:T(8,128)(2,1)}, bf16[4,32,3072]{2,1,0:T(8,128)(2,1)}, u32[]{:S(2)}, u32[]{:S(2)}) collective-permute-start(bf16[4,32,3072]{2,1,0:T(8,128)(2,1)} %get-tuple-element.22.refs_1_), channel_id=1, source_target_pairs={{0,2},{1,3},{2,4},{3,5},{4,6},{5,7},{6,0},{7,1},{8,10},{9,11},{10,... | collective-permute-start | bytes 2359304 | tf_op jit(solution)/shard_map/ppermute | solution.py:744
  410.8 26.5 %collective-permute-start.6 = (bf16[2,32,3072]{2,1,0:T(8,128)(2,1)S(1)}, bf16[2,32,3072]{2,1,0:T(8,128)(2,1)S(1)}, u32[]{:S(2)}, u32[]{:S(2)}) collective-permute-start(bf16[2,32,3072]{2,1,0:T(8,128)(2,1)S(1)} %get-tuple-element.36), channel_id=1, source_target_pairs={{0,2},{1,3},{2,4},{3,5},{4,6},{5,7},{6,0},{7,1},{8,10},{9,11},{10,... | collective-permute-start | bytes 1179656 | tf_op jit(solution)/shard_map/ppermute | solution.py:744
  412.9 32.9 %collective-permute-start.1 = (bf16[2,32,3072]{2,1,0:T(8,128)(2,1)S(1)}, bf16[2,32,3072]{2,1,0:T(8,128)(2,1)S(1)}, u32[]{:S(2)}, u32[]{:S(2)}) collective-permute-start(bf16[2,32,3072]{2,1,0:T(8,128)(2,1)S(1)} %get-tuple-element.37), channel_id=1, source_target_pairs={{0,2},{1,3},{2,4},{3,5},{4,6},{5,7},{6,0},{7,1},{8,10},{9,11},{10,... | collective-permute-start | bytes 1179656 | tf_op jit(solution)/shard_map/ppermute | solution.py:744
  425.5 20.3 %collective-permute-start.7 = (bf16[2,32,3072]{2,1,0:T(8,128)(2,1)S(1)}, bf16[2,32,3072]{2,1,0:T(8,128)(2,1)S(1)}, u32[]{:S(2)}, u32[]{:S(2)}) collective-permute-start(bf16[2,32,3072]{2,1,0:T(8,128)(2,1)S(1)} %get-tuple-element.34), channel_id=1, source_target_pairs={{0,6},{1,7},{2,0},{3,1},{4,2},{5,3},{6,4},{7,5},{8,14},{9,15},{10,... | collective-permute-start | bytes 1179656 | tf_op jit(solution)/shard_map/ppermute | solution.py:744
  428.9 37.5 %collective-permute-start.14 = (bf16[4,32,3072]{2,1,0:T(8,128)(2,1)}, bf16[4,32,3072]{2,1,0:T(8,128)(2,1)}, u32[]{:S(2)}, u32[]{:S(2)}) collective-permute-start(bf16[4,32,3072]{2,1,0:T(8,128)(2,1)} %collective-permute-done.refs_2_), channel_id=1, source_target_pairs={{0,1},{1,0},{2,3},{3,2},{4,5},{5,4},{6,7},{7,6},{8,9},{9,8},{10,11... | collective-permute-start | bytes 2359304 | tf_op jit(solution)/shard_map/ppermute | solution.py:744
  430.7 35.5 %collective-permute-start.16 = (bf16[4,32,3072]{2,1,0:T(8,128)(2,1)}, bf16[4,32,3072]{2,1,0:T(8,128)(2,1)}, u32[]{:S(2)}, u32[]{:S(2)}) collective-permute-start(bf16[4,32,3072]{2,1,0:T(8,128)(2,1)} %collective-permute-done.11.refs_4_), channel_id=1, source_target_pairs={{0,1},{1,0},{2,3},{3,2},{4,5},{5,4},{6,7},{7,6},{8,9},{9,8},{10,11... | collective-permute-start | bytes 2359304 | tf_op jit(solution)/shard_map/ppermute | solution.py:744
  437.3 11.3 %copy-start.1 = (bf16[2,32,3072]{2,1,0:T(8,128)(2,1)}, bf16[2,32,3072]{2,1,0:T(8,128)(2,1)S(1)}, u32[]{:S(2)}) copy-start(bf16[2,32,3072]{2,1,0:T(8,128)(2,1)S(1)} %collective-permute-done.6.refs_0_) | copy-start | bytes 1179652
  437.3 29.4 %collective-permute-start.15 = (bf16[4,32,3072]{2,1,0:T(8,128)(2,1)}, bf16[4,32,3072]{2,1,0:T(8,128)(2,1)}, u32[]{:S(2)}, u32[]{:S(2)}) collective-permute-start(bf16[4,32,3072]{2,1,0:T(8,128)(2,1)} %collective-permute-done.10.refs_3_), channel_id=1, source_target_pairs={{0,1},{1,0},{2,3},{3,2},{4,5},{5,4},{6,7},{7,6},{8,9},{9,8},{10,11... | collective-permute-start | bytes 2359304 | tf_op jit(solution)/shard_map/ppermute | solution.py:744
  445.7 0.7 copy-start
  445.7 19.6 %collective-permute-start.3 = (bf16[2,32,3072]{2,1,0:T(8,128)(2,1)}, bf16[2,32,3072]{2,1,0:T(8,128)(2,1)}, u32[]{:S(2)}, u32[]{:S(2)}) collective-permute-start(bf16[2,32,3072]{2,1,0:T(8,128)(2,1)} %get-tuple-element.35), channel_id=1, source_target_pairs={{0,6},{1,7},{2,0},{3,1},{4,2},{5,3},{6,4},{7,5},{8,14},{9,15},{10,... | collective-permute-start | bytes 1179656 | tf_op jit(solution)/shard_map/ppermute | solution.py:744
  446.5 2.1 copy-start.2
  446.5 32.5 %collective-permute-start.17 = (bf16[4,32,3072]{2,1,0:T(8,128)(2,1)}, bf16[4,32,3072]{2,1,0:T(8,128)(2,1)}, u32[]{:S(2)}, u32[]{:S(2)}) collective-permute-start(bf16[4,32,3072]{2,1,0:T(8,128)(2,1)} %collective-permute-done.2.refs_5_), channel_id=1, source_target_pairs={{0,1},{1,0},{2,3},{3,2},{4,5},{5,4},{6,7},{7,6},{8,9},{9,8},{10,11... | collective-permute-start | bytes 2359304 | tf_op jit(solution)/shard_map/ppermute | solution.py:744
  465.4 20.9 %collective-permute-start.8 = (bf16[2,32,3072]{2,1,0:T(8,128)(2,1)}, bf16[2,32,3072]{2,1,0:T(8,128)(2,1)}, u32[]{:S(2)}, u32[]{:S(2)}) collective-permute-start(bf16[2,32,3072]{2,1,0:T(8,128)(2,1)} %copy-done.1), channel_id=1, source_target_pairs={{0,1},{1,0},{2,3},{3,2},{4,5},{5,4},{6,7},{7,6},{8,9},{9,8},{10,11... | collective-permute-start | bytes 1179656 | tf_op jit(solution)/shard_map/ppermute | solution.py:744
  466.2 22.3 %collective-permute-start.4 = (bf16[2,32,3072]{2,1,0:T(8,128)(2,1)}, bf16[2,32,3072]{2,1,0:T(8,128)(2,1)}, u32[]{:S(2)}, u32[]{:S(2)}) collective-permute-start(bf16[2,32,3072]{2,1,0:T(8,128)(2,1)} %copy-done), channel_id=1, source_target_pairs={{0,1},{1,0},{2,3},{3,2},{4,5},{5,4},{6,7},{7,6},{8,9},{9,8},{10,11... | collective-permute-start | bytes 1179656 | tf_op jit(solution)/shard_map/ppermute | solution.py:744
  466.4 20.0 %collective-permute-start.9 = (bf16[2,32,3072]{2,1,0:T(8,128)(2,1)}, bf16[2,32,3072]{2,1,0:T(8,128)(2,1)}, u32[]{:S(2)}, u32[]{:S(2)}) collective-permute-start(bf16[2,32,3072]{2,1,0:T(8,128)(2,1)} %copy-done.2), channel_id=1, source_target_pairs={{0,1},{1,0},{2,3},{3,2},{4,5},{5,4},{6,7},{7,6},{8,9},{9,8},{10,11... | collective-permute-start | bytes 1179656 | tf_op jit(solution)/shard_map/ppermute | solution.py:744
  466.7 21.8 %collective-permute-start.5 = (bf16[2,32,3072]{2,1,0:T(8,128)(2,1)}, bf16[2,32,3072]{2,1,0:T(8,128)(2,1)}, u32[]{:S(2)}, u32[]{:S(2)}) collective-permute-start(bf16[2,32,3072]{2,1,0:T(8,128)(2,1)} %collective-permute-done.3.refs_1_), channel_id=1, source_target_pairs={{0,1},{1,0},{2,3},{3,2},{4,5},{5,4},{6,7},{7,6},{8,9},{9,8},{10,11... | collective-permute-start | bytes 1179656 | tf_op jit(solution)/shard_map/ppermute | solution.py:744

commit v9 on v7

--- a/solution.py
+++ b/solution.py
@@ -23,10 +23,10 @@
 TILES = 2
 
 ORDER = (
-    ('e3', 15), ('MU', 8), ('b1', 3), ('d3', 12), ('WP', 10), ('a1', 2), ('B2', 16), ('F1', 1), ('f1', 7),
-    ('f3', 15), ('e1', 6), ('d1', 5), ('MD', 8), ('YS', 19), ('WG', 17), ('c3', 10), ('c5', 21), ('b5', 20),
-    ('c1', 3), ('a5', 19), ('YL', 18), ('d4', 20), ('e4', 22), ('MY', 8), ('f4', 23), ('c4', 18), ('b3', 9),
-    ('b4', 17), ('a3', 8), ('a4', 16),
+    ('a3', 9), ('b5', 20), ('a1', 1), ('a5', 19), ('F1', 0), ('d4', 20), ('MU', 8), ('f1', 7), ('c4', 18),
+    ('YL', 18), ('d1', 4), ('B2', 16), ('WP', 9), ('b4', 17), ('d3', 11), ('f3', 15), ('YS', 18), ('a4', 16),
+    ('c3', 10), ('WG', 16), ('e1', 5), ('MD', 8), ('c1', 2), ('MY', 8), ('e4', 21), ('c5', 20), ('e3', 14),
+    ('b3', 9), ('f4', 22), ('b1', 1),
 )
 
 
@@ -216,10 +216,10 @@
 
         def add(t, _):
             r = pl.ds(pl.multiple_of(t * hb, hb), hb)
-            S[f, s, r] = (S[f, s, r].astype(F32) + RD[f, c % PAIRS, r].astype(F32)).astype(BF)
-            return 0
-
-        lax.fori_loop(0, half // hb, add, 0, unroll=2)
+            S[f, s, r] = S[f, s, r] + RD[f, c % PAIRS, r]
+            return 0
+
+        lax.fori_loop(0, half // hb, add, 0, unroll=8)
         for d in (0, 1):
             c_first(fl, c, d).start()
 
@@ -313,7 +313,7 @@
         keep = lax.broadcasted_iota(jnp.int32, (slen, slen), 0) <= lax.broadcasted_iota(jnp.int32, (slen, slen), 1)
         s = jnp.where(keep, s, -1e30)
         ex = jnp.exp(s - jnp.max(s, axis=0, keepdims=True))
-        return qt, kt, vt, ex / jnp.sum(ex, axis=0, keepdims=True)
+        return qt, kt, vt, ex * (1.0 / jnp.sum(ex, axis=0, keepdims=True))
 
     def norm_rows():
         def ln(t, _):
@@ -322,7 +322,7 @@
             ab[r] = (xh * ga[...]).astype(BF)
             return 0
 
-        lax.fori_loop(0, slen // hb, ln, 0, unroll=4)
+        lax.fori_loop(0, slen // hb, ln, 0, unroll=8)
 
     def stage_F1(c):
         @pl.when(c > 0)
@@ -353,12 +353,12 @@
             obt[pl.ds(pl.multiple_of(hd * e, e), e)] = dg(vt, p.astype(BF), 1, 0).astype(BF)
             return 0
 
-        lax.fori_loop(0, heads, head, 0)
+        lax.fori_loop(0, heads, head, 0, unroll=True)
         tr = tile_of(he, 128)
         for t in range(he // tr):
             ob[:, t * tr:(t + 1) * tr] = obt[t * tr:(t + 1) * tr].T
         st_o(c).start()
-        n = tile_of(dm, 1024)
+        n = tile_of(dm, 3072)
 
         @pl.when(c == 0)
         def _():
@@ -385,7 +385,7 @@
 
         ld_nm(c).wait()
         ld_dy(c).wait()
-        n = tile_of(ff, 512)
+        n = tile_of(ff, 1536)
 
         def up(t, _):
             col = pl.ds(pl.multiple_of(t * n, n), n)
@@ -404,7 +404,7 @@
         def _():
             ld_dy(c + 1).start()
 
-    m = tile_of(dm, 512)
+    m = tile_of(dm, 3072)
 
     def stage_MD(c):
         def down(t, _):
@@ -445,12 +445,12 @@
             dqt[pl.ds(pl.multiple_of(he + hd * e, e), e)] = dg(qt, ds, 1, 1).astype(BF)
             return 0
 
-        lax.fori_loop(0, heads, head, 0)
+        lax.fori_loop(0, heads, head, 0, unroll=2)
         tr = tile_of(3 * he, 128)
         for t in range(3 * he // tr):
             dqb[:, t * tr:(t + 1) * tr] = dqt[t * tr:(t + 1) * tr].T
         st_dq(c).start()
-        n = tile_of(dm, 512)
+        n = tile_of(dm, 3072)
 
         def proj(t, _):
             col = pl.multiple_of(t * n, n)

time: 485 us -> 468 us (0.965)
  Pallas kernels: 439 us -> 422 us
    pallas_call x1, Pallas kernels: 400 us -> 383 us  [mega(): pl.pallas_call(functools.partial(body, heads), name='mega', out_shape=out...]
  transfers between devices with their start and end apart: 14 -> 14, of which waited for: 3 -> 3; matrix products, arithmetic and copies ran while one was open for 0% -> 0% of each run, Pallas kernels for 7% -> 8%
where the time goes in v9:
time: 468 us
  Pallas kernels  422 us (90%)
  waiting for transfers between devices  28.2 us (6%)
  starting transfers between devices  13.7 us (3%)
    pallas_call x1, Pallas kernels, mega(): pl.pallas_call(functools.partial(body, heads), name='mega', out_shape=out...  383 us
    pallas_call x2, Pallas kernels, copied(): pl.pallas_call(move, in_specs=[hbm] * n, out_specs=(hbm,) * n, out_shape=...  28.8 us
    ppermute x14, waiting for transfers between devices, hop(): return lax.ppermute(v, 'tp', perm)  28.2 us
    ppermute x14, starting transfers between devices, hop(): return lax.ppermute(v, 'tp', perm)  13.7 us
    pallas_call x2, Pallas kernels, placed(): pl.pallas_call(put, in_specs=[hbm] * (n + len(given)), out_specs=hbm, out...  10.1 us
  transfers between devices with their start and end apart: 14, of which 3 were waited for; matrix products, arithmetic and copies ran while one was open for 0% of the time, Pallas kernels for 8%

profile of v9, /device:TPU:81, one launch (start us, length us, event | category | flops | bytes accessed | tf_op | source)
XLA Modules:
  0.0 467.5 jit_solution(10971311599191945337)
XLA Ops:
  0.6 383.1 %mega.1 = (bf16[4,32,3072]{2,1,0:T(8,128)(2,1)}, bf16[4,32,3072]{2,1,0:T(8,128)(2,1)}, bf16[2048,3072]{1,0:T(8,128)(2,1)}, bf16[1152,3072]{1,0:T(8,128)(2,1)}, b...) custom-call(bf16[8,256,3072]{2,1,0:T(8,128)(2,1)} %x.1, ...), custom_call_target="tpu_custom_call" | custom-call | flops 115964116992 | bytes 150994944 | tf_op jit(solution)/shard_map/mega/pallas_call | solution.py:663
  383.8 0.2 collective-permute-start.8
  384.0 1.2 collective-permute-start.7
  385.3 0.2 collective-permute-start
  385.5 2.5 collective-permute-start.2
  387.9 1.2 collective-permute-start.9
  389.2 0.0 collective-permute-done.8.refs_6_
  389.2 0.0 collective-permute-start.6
  389.2 13.9 %collective-permute-done.7.refs_4_ = bf16[4,32,3072]{2,1,0:T(8,128)(2,1)S(1)} collective-permute-done((bf16[4,32,3072]{2,1,0:T(8,128)(2,1)}, bf16[4,32,3072]{2,1,0:T(8,128)(2,1)S(1)}, u32[]{:S(2)}, u32[]{:S(2)}) %collective-permute-start.7) | collective-permute-done | bytes 786464 | tf_op jit(solution)/shard_map/ppermute | solution.py:744
  403.1 0.0 copy-start
  403.1 0.9 copy-done
  404.0 2.0 collective-permute-start.12
  405.9 0.0 collective-permute-done.refs_2_
  406.0 0.0 collective-permute-start.1
  406.0 14.0 %collective-permute-done.2.refs_5_ = bf16[4,32,3072]{2,1,0:T(8,128)(2,1)} collective-permute-done((bf16[4,32,3072]{2,1,0:T(8,128)(2,1)}, bf16[4,32,3072]{2,1,0:T(8,128)(2,1)}, u32[]{:S(2)}, u32[]{:S(2)}) %collective-permute-start.2) | collective-permute-done | bytes 786464 | tf_op jit(solution)/shard_map/ppermute | solution.py:744
  419.9 2.5 collective-permute-start.3
  422.4 1.4 fusion
  423.8 0.0 collective-permute-done.9.refs_7_
  423.8 0.0 copy-start.1
  423.8 1.6 collective-permute-start.10
  425.4 0.0 collective-permute-done.6.refs_3_
  425.4 0.1 collective-permute-start.13
  425.6 0.0 collective-permute-done.12.refs_10_
  425.6 0.0 copy-done.1
  425.6 0.0 copy-start.2
  425.6 0.6 collective-permute-start.11
  426.2 0.3 copy-done.2
  426.5 12.1 %shard_map.146 = (bf16[1536,3072]{1,0:T(8,128)(2,1)}, bf16[1152,3072]{1,0:T(8,128)(2,1)}) custom-call(bf16[1536,3072]{1,0:T(8,128)(2,1)} %get-tuple-element.28.refs_0_, bf16[1152,3072]{1,0:T(8,128)(2,1)} %get-tuple-element.29.refs_1_), custom_call_target="tpu_custom_call" | custom-call | flops 4128768000 | bytes 33030144 | tf_op jit(solution)/shard_map/pallas_call | solution.py:696
  438.6 0.3 collective-permute-done.1.refs_0_
  438.9 1.5 collective-permute-start.4
  440.5 0.0 collective-permute-done.3.refs_1_
  440.5 0.0 collective-permute-start.5
  440.5 16.7 %shard_map.145 = (bf16[2048,3072]{1,0:T(8,128)(2,1)}, bf16[3072,1536]{1,0:T(8,128)(2,1)}, bf16[384,3072]{1,0:T(8,128)(2,1)}) custom-call(bf16[2048,3072]{1,0:T(8,128)(2,1)} %get-tuple-element.23.refs_0_, bf16[3072,1536]{1,0:T(8,128)(2,1)} %get-tuple-element.24.refs_1_, bf16[384,3072]{1,0:T(8,128)(2,1)} %get-tuple-element.25.refs_2_), custom_call_target="tpu_custom_call" | custom-call | flops 6094848000 | bytes 48758784 | tf_op jit(solution)/shard_map/pallas_call | solution.py:696
  457.2 0.0 collective-permute-done.10.refs_8_
  457.2 0.0 collective-permute-done.11.refs_9_
  457.2 0.0 collective-permute-done.13.refs_11_
  457.2 7.3 %shard_map.143.refs_4_ = bf16[8,256,3072]{2,1,0:T(8,128)(2,1)} custom-call(bf16[4,32,3072]{2,1,0:T(8,128)(2,1)} %get-tuple-element.21.refs_0_, bf16[4,32,3072]{2,1,0:T(8,128)(2,1)} %get-tuple-element.22.refs_1_, bf16[4,32,3072]{2,1,0:T(8,128)(2,1)} %collective-permute-done.refs_2_, bf16[4,32,3072]{2,1,0:T(8,128)(2,1)} %collective-permute-done.6.refs_3_, ...), custom_call_target="tpu_custom_call" | custom-call | flops 2359296000 | tf_op jit(solution)/shard_map/pallas_call | solution.py:726
  464.5 0.0 collective-permute-done.4.refs_2_
  464.5 0.0 collective-permute-done.5.refs_3_
  464.5 2.9 shard_map.144
Async XLA Ops:
  383.8 5.4 %collective-permute-start.8 = (bf16[4,32,3072]{2,1,0:T(8,128)(2,1)}, bf16[4,32,3072]{2,1,0:T(8,128)(2,1)}, u32[]{:S(2)}, u32[]{:S(2)}) collective-permute-start(bf16[4,32,3072]{2,1,0:T(8,128)(2,1)} %get-tuple-element.21.refs_0_), channel_id=1, source_target_pairs={{0,1},{1,0},{2,3},{3,2},{4,5},{5,4},{6,7},{7,6},{8,9},{9,8},{10,11... | collective-permute-start | bytes 2359304 | tf_op jit(solution)/shard_map/ppermute | solution.py:744
  384.0 19.0 %collective-permute-start.7 = (bf16[4,32,3072]{2,1,0:T(8,128)(2,1)}, bf16[4,32,3072]{2,1,0:T(8,128)(2,1)S(1)}, u32[]{:S(2)}, u32[]{:S(2)}) collective-permute-start(bf16[4,32,3072]{2,1,0:T(8,128)(2,1)} %get-tuple-element.21.refs_0_), channel_id=1, source_target_pairs={{0,6},{1,7},{2,0},{3,1},{4,2},{5,3},{6,4},{7,5},{8,14},{9,15},{10,... | collective-permute-start | bytes 2359304 | tf_op jit(solution)/shard_map/ppermute | solution.py:744
  385.3 20.7 %collective-permute-start = (bf16[4,32,3072]{2,1,0:T(8,128)(2,1)}, bf16[4,32,3072]{2,1,0:T(8,128)(2,1)}, u32[]{:S(2)}, u32[]{:S(2)}) collective-permute-start(bf16[4,32,3072]{2,1,0:T(8,128)(2,1)} %get-tuple-element.21.refs_0_), channel_id=1, source_target_pairs={{0,2},{1,3},{2,4},{3,5},{4,6},{5,7},{6,0},{7,1},{8,10},{9,11},{10,... | collective-permute-start | bytes 2359304 | tf_op jit(solution)/shard_map/ppermute | solution.py:744
  385.5 34.4 %collective-permute-start.2 = (bf16[4,32,3072]{2,1,0:T(8,128)(2,1)}, bf16[4,32,3072]{2,1,0:T(8,128)(2,1)}, u32[]{:S(2)}, u32[]{:S(2)}) collective-permute-start(bf16[4,32,3072]{2,1,0:T(8,128)(2,1)} %get-tuple-element.22.refs_1_), channel_id=1, source_target_pairs={{0,6},{1,7},{2,0},{3,1},{4,2},{5,3},{6,4},{7,5},{8,14},{9,15},{10,... | collective-permute-start | bytes 2359304 | tf_op jit(solution)/shard_map/ppermute | solution.py:744
  387.9 35.9 %collective-permute-start.9 = (bf16[4,32,3072]{2,1,0:T(8,128)(2,1)}, bf16[4,32,3072]{2,1,0:T(8,128)(2,1)S(1)}, u32[]{:S(2)}, u32[]{:S(2)}) collective-permute-start(bf16[4,32,3072]{2,1,0:T(8,128)(2,1)} %get-tuple-element.22.refs_1_), channel_id=1, source_target_pairs={{0,1},{1,0},{2,3},{3,2},{4,5},{5,4},{6,7},{7,6},{8,9},{9,8},{10,11... | collective-permute-start | bytes 2359304 | tf_op jit(solution)/shard_map/ppermute | solution.py:744
  389.2 36.3 %collective-permute-start.6 = (bf16[4,32,3072]{2,1,0:T(8,128)(2,1)}, bf16[4,32,3072]{2,1,0:T(8,128)(2,1)}, u32[]{:S(2)}, u32[]{:S(2)}) collective-permute-start(bf16[4,32,3072]{2,1,0:T(8,128)(2,1)} %get-tuple-element.22.refs_1_), channel_id=1, source_target_pairs={{0,2},{1,3},{2,4},{3,5},{4,6},{5,7},{6,0},{7,1},{8,10},{9,11},{10,... | collective-permute-start | bytes 2359304 | tf_op jit(solution)/shard_map/ppermute | solution.py:744
  403.1 0.9 copy-start
  404.0 21.6 %collective-permute-start.12 = (bf16[4,32,3072]{2,1,0:T(8,128)(2,1)S(1)}, bf16[4,32,3072]{2,1,0:T(8,128)(2,1)S(1)}, u32[]{:S(2)}, u32[]{:S(2)}) collective-permute-start(bf16[4,32,3072]{2,1,0:T(8,128)(2,1)S(1)} %collective-permute-done.7.refs_4_), channel_id=1, source_target_pairs={{0,1},{1,0},{2,3},{3,2},{4,5},{5,4},{6,7},{7,6},{8,9},{9,8},{10,11... | collective-permute-start | bytes 2359304 | tf_op jit(solution)/shard_map/ppermute | solution.py:744
  406.0 33.0 %collective-permute-start.1 = (bf16[4,32,3072]{2,1,0:T(8,128)(2,1)}, bf16[4,32,3072]{2,1,0:T(8,128)(2,1)}, u32[]{:S(2)}, u32[]{:S(2)}) collective-permute-start(bf16[4,32,3072]{2,1,0:T(8,128)(2,1)} %collective-permute-done.refs_2_), channel_id=1, source_target_pairs={{0,2},{1,3},{2,4},{3,5},{4,6},{5,7},{6,0},{7,1},{8,10},{9,11},{10,... | collective-permute-start | bytes 2359304 | tf_op jit(solution)/shard_map/ppermute | solution.py:744
  419.9 20.5 %collective-permute-start.3 = (bf16[4,32,3072]{2,1,0:T(8,128)(2,1)}, bf16[4,32,3072]{2,1,0:T(8,128)(2,1)}, u32[]{:S(2)}, u32[]{:S(2)}) collective-permute-start(bf16[4,32,3072]{2,1,0:T(8,128)(2,1)} %collective-permute-done.2.refs_5_), channel_id=1, source_target_pairs={{0,6},{1,7},{2,0},{3,1},{4,2},{5,3},{6,4},{7,5},{8,14},{9,15},{10,... | collective-permute-start | bytes 2359304 | tf_op jit(solution)/shard_map/ppermute | solution.py:744
  423.8 1.8 copy-start.1
  423.8 33.4 %collective-permute-start.10 = (bf16[4,32,3072]{2,1,0:T(8,128)(2,1)}, bf16[4,32,3072]{2,1,0:T(8,128)(2,1)}, u32[]{:S(2)}, u32[]{:S(2)}) collective-permute-start(bf16[4,32,3072]{2,1,0:T(8,128)(2,1)} %collective-permute-done.refs_2_), channel_id=1, source_target_pairs={{0,1},{1,0},{2,3},{3,2},{4,5},{5,4},{6,7},{7,6},{8,9},{9,8},{10,11... | collective-permute-start | bytes 2359304 | tf_op jit(solution)/shard_map/ppermute | solution.py:744
  425.4 31.8 %collective-permute-start.13 = (bf16[4,32,3072]{2,1,0:T(8,128)(2,1)}, bf16[4,32,3072]{2,1,0:T(8,128)(2,1)}, u32[]{:S(2)}, u32[]{:S(2)}) collective-permute-start(bf16[4,32,3072]{2,1,0:T(8,128)(2,1)} %collective-permute-done.2.refs_5_), channel_id=1, source_target_pairs={{0,1},{1,0},{2,3},{3,2},{4,5},{5,4},{6,7},{7,6},{8,9},{9,8},{10,11... | collective-permute-start | bytes 2359304 | tf_op jit(solution)/shard_map/ppermute | solution.py:744
  425.6 0.9 copy-start.2
  425.6 31.6 %collective-permute-start.11 = (bf16[4,32,3072]{2,1,0:T(8,128)(2,1)}, bf16[4,32,3072]{2,1,0:T(8,128)(2,1)}, u32[]{:S(2)}, u32[]{:S(2)}) collective-permute-start(bf16[4,32,3072]{2,1,0:T(8,128)(2,1)} %collective-permute-done.6.refs_3_), channel_id=1, source_target_pairs={{0,1},{1,0},{2,3},{3,2},{4,5},{5,4},{6,7},{7,6},{8,9},{9,8},{10,11... | collective-permute-start | bytes 2359304 | tf_op jit(solution)/shard_map/ppermute | solution.py:744
  438.9 25.6 %collective-permute-start.4 = (bf16[4,32,3072]{2,1,0:T(8,128)(2,1)}, bf16[4,32,3072]{2,1,0:T(8,128)(2,1)}, u32[]{:S(2)}, u32[]{:S(2)}) collective-permute-start(bf16[4,32,3072]{2,1,0:T(8,128)(2,1)} %collective-permute-done.1.refs_0_), channel_id=1, source_target_pairs={{0,1},{1,0},{2,3},{3,2},{4,5},{5,4},{6,7},{7,6},{8,9},{9,8},{10,11... | collective-permute-start | bytes 2359304 | tf_op jit(solution)/shard_map/ppermute | solution.py:744
  440.5 24.1 %collective-permute-start.5 = (bf16[4,32,3072]{2,1,0:T(8,128)(2,1)}, bf16[4,32,3072]{2,1,0:T(8,128)(2,1)}, u32[]{:S(2)}, u32[]{:S(2)}) collective-permute-start(bf16[4,32,3072]{2,1,0:T(8,128)(2,1)} %collective-permute-done.3.refs_1_), channel_id=1, source_target_pairs={{0,1},{1,0},{2,3},{3,2},{4,5},{5,4},{6,7},{7,6},{8,9},{9,8},{10,11... | collective-permute-start | bytes 2359304 | tf_op jit(solution)/shard_map/ppermute | solution.py:744

commit v10 on v9

--- a/solution.py
+++ b/solution.py
@@ -751,18 +751,20 @@
         oa, ob = hop(la, 1, 0), hop(rb, -1, 0)
         near = [va, vb, la, lb, ra, rb]
         near += [hop(p, 0, 1) for p in near]
-        far = [oa, ob, hop(oa, 0, 1), hop(ob, 0, 1)]
+        far = [(oa, ob), (hop(oa, 0, 1), hop(ob, 0, 1))]
 
         def near_at(chip, core):
             chips = (chip, (chip + CHIPS - 1) % CHIPS, (chip + 1) % CHIPS)
             return [(k * ns, co * half + ch * blk) for co in (core, 1 - core) for ch in chips for k in (0, 1)]
 
-        def far_at(chip, core):
+        def far_at(other, chip, core):
             o = ((chip + 2) % CHIPS) * blk
-            return [(k * ns, co * half + o) for co in (core, 1 - core) for k in (0, 1)]
+            return [(k * ns, (1 - core if other else core) * half + o) for k in (0, 1)]
 
         out = placed(None, near, (2 * ns, half * CORES, dm), near_at)
-        return placed(out, far, out.shape, far_at)
+        for k in (0, 1):
+            out = placed(out, far[k], out.shape, functools.partial(far_at, k))
+        return out
 
     def step(x_in, gain_attn, w_qkv, w_out, gain_mlp, w_up, w_down, dy_out):
         heads, e = w_qkv.shape[3:]

time: 468 us -> 470 us (level)
    pallas_call x2 -> x3, Pallas kernels: 10.1 us -> 11.9 us  [placed(): pl.pallas_call(put, in_specs=[hbm] * (n + len(given)), out_specs=hbm, out...]
where the time goes in v10:
time: 470 us; the launch traced here: 469 us
  Pallas kernels  424 us (90%)
  waiting for transfers between devices  28.2 us (6%)
  starting transfers between devices  13.7 us (3%)
    pallas_call x1, Pallas kernels, mega(): pl.pallas_call(functools.partial(body, heads), name='mega', out_shape=out...  383 us
    pallas_call x2, Pallas kernels, copied(): pl.pallas_call(move, in_specs=[hbm] * n, out_specs=(hbm,) * n, out_shape=...  28.8 us
    ppermute x14, waiting for transfers between devices, hop(): return lax.ppermute(v, 'tp', perm)  28.2 us
    ppermute x14, starting transfers between devices, hop(): return lax.ppermute(v, 'tp', perm)  13.7 us
    pallas_call x3, Pallas kernels, placed(): pl.pallas_call(put, in_specs=[hbm] * (n + len(given)), out_specs=hbm, out...  11.9 us
  transfers between devices with their start and end apart: 14, of which 3 were waited for; matrix products, arithmetic and copies ran while one was open for 0% of the time, Pallas kernels for 8%

profile of v10, /device:TPU:81, one launch (start us, length us, event | category | flops | bytes accessed | tf_op | source)
XLA Modules:
  0.0 469.3 jit_solution(6869206351248475505)
XLA Ops:
  0.6 383.1 %mega.1 = (bf16[4,32,3072]{2,1,0:T(8,128)(2,1)}, bf16[4,32,3072]{2,1,0:T(8,128)(2,1)}, bf16[2048,3072]{1,0:T(8,128)(2,1)}, bf16[1152,3072]{1,0:T(8,128)(2,1)}, b...) custom-call(bf16[8,256,3072]{2,1,0:T(8,128)(2,1)} %x.1, ...), custom_call_target="tpu_custom_call" | custom-call | flops 115964116992 | bytes 150994944 | tf_op jit(solution)/shard_map/mega/pallas_call | solution.py:663
  383.8 0.2 collective-permute-start.8
  384.0 1.2 collective-permute-start.7
  385.3 0.2 collective-permute-start
  385.5 2.5 collective-permute-start.3
  387.9 1.2 collective-permute-start.9
  389.2 0.0 collective-permute-done.8.refs_6_
  389.2 0.0 collective-permute-start.6
  389.2 13.9 %collective-permute-done.7.refs_4_ = bf16[4,32,3072]{2,1,0:T(8,128)(2,1)S(1)} collective-permute-done((bf16[4,32,3072]{2,1,0:T(8,128)(2,1)}, bf16[4,32,3072]{2,1,0:T(8,128)(2,1)S(1)}, u32[]{:S(2)}, u32[]{:S(2)}) %collective-permute-start.7) | collective-permute-done | bytes 786464 | tf_op jit(solution)/shard_map/ppermute | solution.py:744
  403.1 0.0 copy-start
  403.1 0.9 copy-done
  404.0 2.0 collective-permute-start.12
  405.9 0.0 collective-permute-done.refs_2_
  406.0 0.0 collective-permute-start.1
  406.0 14.0 %collective-permute-done.3.refs_5_ = bf16[4,32,3072]{2,1,0:T(8,128)(2,1)} collective-permute-done((bf16[4,32,3072]{2,1,0:T(8,128)(2,1)}, bf16[4,32,3072]{2,1,0:T(8,128)(2,1)}, u32[]{:S(2)}, u32[]{:S(2)}) %collective-permute-start.3) | collective-permute-done | bytes 786464 | tf_op jit(solution)/shard_map/ppermute | solution.py:744
  419.9 2.5 collective-permute-start.4
  422.4 1.4 fusion
  423.8 0.0 collective-permute-done.9.refs_7_
  423.8 0.0 copy-start.1
  423.8 1.6 collective-permute-start.10
  425.4 0.0 collective-permute-done.6.refs_3_
  425.4 0.1 collective-permute-start.13
  425.6 0.0 collective-permute-done.12.refs_10_
  425.6 0.0 copy-done.1
  425.6 0.0 copy-start.2
  425.6 0.6 collective-permute-start.11
  426.2 0.3 copy-done.2
  426.5 12.1 %shard_map.147 = (bf16[1536,3072]{1,0:T(8,128)(2,1)}, bf16[1152,3072]{1,0:T(8,128)(2,1)}) custom-call(bf16[1536,3072]{1,0:T(8,128)(2,1)} %get-tuple-element.28.refs_0_, bf16[1152,3072]{1,0:T(8,128)(2,1)} %get-tuple-element.29.refs_1_), custom_call_target="tpu_custom_call" | custom-call | flops 4128768000 | bytes 33030144 | tf_op jit(solution)/shard_map/pallas_call | solution.py:696
  438.6 0.3 collective-permute-done.1.refs_0_
  438.9 1.5 collective-permute-start.2
  440.5 0.0 collective-permute-done.4.refs_1_
  440.5 0.0 collective-permute-start.5
  440.5 16.7 %shard_map.146 = (bf16[2048,3072]{1,0:T(8,128)(2,1)}, bf16[3072,1536]{1,0:T(8,128)(2,1)}, bf16[384,3072]{1,0:T(8,128)(2,1)}) custom-call(bf16[2048,3072]{1,0:T(8,128)(2,1)} %get-tuple-element.23.refs_0_, bf16[3072,1536]{1,0:T(8,128)(2,1)} %get-tuple-element.24.refs_1_, bf16[384,3072]{1,0:T(8,128)(2,1)} %get-tuple-element.25.refs_2_), custom_call_target="tpu_custom_call" | custom-call | flops 6094848000 | bytes 48758784 | tf_op jit(solution)/shard_map/pallas_call | solution.py:696
  457.2 0.0 collective-permute-done.10.refs_8_
  457.2 0.0 collective-permute-done.11.refs_9_
  457.2 0.0 collective-permute-done.13.refs_11_
  457.2 7.3 %shard_map.143.refs_2_ = bf16[8,256,3072]{2,1,0:T(8,128)(2,1)} custom-call(bf16[4,32,3072]{2,1,0:T(8,128)(2,1)} %get-tuple-element.21.refs_0_, bf16[4,32,3072]{2,1,0:T(8,128)(2,1)} %get-tuple-element.22.refs_1_, bf16[4,32,3072]{2,1,0:T(8,128)(2,1)} %collective-permute-done.refs_2_, bf16[4,32,3072]{2,1,0:T(8,128)(2,1)} %collective-permute-done.6.refs_3_, ...), custom_call_target="tpu_custom_call" | custom-call | flops 2359296000 | tf_op jit(solution)/shard_map/pallas_call | solution.py:726
  464.5 2.3 shard_map.144.refs_2_
  466.8 0.0 collective-permute-done.2.refs_0_
  466.8 0.0 collective-permute-done.5.refs_1_
  466.8 2.3 shard_map.145
Async XLA Ops:
  383.8 5.4 %collective-permute-start.8 = (bf16[4,32,3072]{2,1,0:T(8,128)(2,1)}, bf16[4,32,3072]{2,1,0:T(8,128)(2,1)}, u32[]{:S(2)}, u32[]{:S(2)}) collective-permute-start(bf16[4,32,3072]{2,1,0:T(8,128)(2,1)} %get-tuple-element.21.refs_0_), channel_id=1, source_target_pairs={{0,1},{1,0},{2,3},{3,2},{4,5},{5,4},{6,7},{7,6},{8,9},{9,8},{10,11... | collective-permute-start | bytes 2359304 | tf_op jit(solution)/shard_map/ppermute | solution.py:744
  384.0 19.0 %collective-permute-start.7 = (bf16[4,32,3072]{2,1,0:T(8,128)(2,1)}, bf16[4,32,3072]{2,1,0:T(8,128)(2,1)S(1)}, u32[]{:S(2)}, u32[]{:S(2)}) collective-permute-start(bf16[4,32,3072]{2,1,0:T(8,128)(2,1)} %get-tuple-element.21.refs_0_), channel_id=1, source_target_pairs={{0,6},{1,7},{2,0},{3,1},{4,2},{5,3},{6,4},{7,5},{8,14},{9,15},{10,... | collective-permute-start | bytes 2359304 | tf_op jit(solution)/shard_map/ppermute | solution.py:744
  385.3 20.7 %collective-permute-start = (bf16[4,32,3072]{2,1,0:T(8,128)(2,1)}, bf16[4,32,3072]{2,1,0:T(8,128)(2,1)}, u32[]{:S(2)}, u32[]{:S(2)}) collective-permute-start(bf16[4,32,3072]{2,1,0:T(8,128)(2,1)} %get-tuple-element.21.refs_0_), channel_id=1, source_target_pairs={{0,2},{1,3},{2,4},{3,5},{4,6},{5,7},{6,0},{7,1},{8,10},{9,11},{10,... | collective-permute-start | bytes 2359304 | tf_op jit(solution)/shard_map/ppermute | solution.py:744
  385.5 34.4 %collective-permute-start.3 = (bf16[4,32,3072]{2,1,0:T(8,128)(2,1)}, bf16[4,32,3072]{2,1,0:T(8,128)(2,1)}, u32[]{:S(2)}, u32[]{:S(2)}) collective-permute-start(bf16[4,32,3072]{2,1,0:T(8,128)(2,1)} %get-tuple-element.22.refs_1_), channel_id=1, source_target_pairs={{0,6},{1,7},{2,0},{3,1},{4,2},{5,3},{6,4},{7,5},{8,14},{9,15},{10,... | collective-permute-start | bytes 2359304 | tf_op jit(solution)/shard_map/ppermute | solution.py:744
  387.9 35.9 %collective-permute-start.9 = (bf16[4,32,3072]{2,1,0:T(8,128)(2,1)}, bf16[4,32,3072]{2,1,0:T(8,128)(2,1)S(1)}, u32[]{:S(2)}, u32[]{:S(2)}) collective-permute-start(bf16[4,32,3072]{2,1,0:T(8,128)(2,1)} %get-tuple-element.22.refs_1_), channel_id=1, source_target_pairs={{0,1},{1,0},{2,3},{3,2},{4,5},{5,4},{6,7},{7,6},{8,9},{9,8},{10,11... | collective-permute-start | bytes 2359304 | tf_op jit(solution)/shard_map/ppermute | solution.py:744
  389.2 36.3 %collective-permute-start.6 = (bf16[4,32,3072]{2,1,0:T(8,128)(2,1)}, bf16[4,32,3072]{2,1,0:T(8,128)(2,1)}, u32[]{:S(2)}, u32[]{:S(2)}) collective-permute-start(bf16[4,32,3072]{2,1,0:T(8,128)(2,1)} %get-tuple-element.22.refs_1_), channel_id=1, source_target_pairs={{0,2},{1,3},{2,4},{3,5},{4,6},{5,7},{6,0},{7,1},{8,10},{9,11},{10,... | collective-permute-start | bytes 2359304 | tf_op jit(solution)/shard_map/ppermute | solution.py:744
  403.1 0.9 copy-start
  404.0 21.6 %collective-permute-start.12 = (bf16[4,32,3072]{2,1,0:T(8,128)(2,1)S(1)}, bf16[4,32,3072]{2,1,0:T(8,128)(2,1)S(1)}, u32[]{:S(2)}, u32[]{:S(2)}) collective-permute-start(bf16[4,32,3072]{2,1,0:T(8,128)(2,1)S(1)} %collective-permute-done.7.refs_4_), channel_id=1, source_target_pairs={{0,1},{1,0},{2,3},{3,2},{4,5},{5,4},{6,7},{7,6},{8,9},{9,8},{10,11... | collective-permute-start | bytes 2359304 | tf_op jit(solution)/shard_map/ppermute | solution.py:744
  406.0 33.0 %collective-permute-start.1 = (bf16[4,32,3072]{2,1,0:T(8,128)(2,1)}, bf16[4,32,3072]{2,1,0:T(8,128)(2,1)}, u32[]{:S(2)}, u32[]{:S(2)}) collective-permute-start(bf16[4,32,3072]{2,1,0:T(8,128)(2,1)} %collective-permute-done.refs_2_), channel_id=1, source_target_pairs={{0,2},{1,3},{2,4},{3,5},{4,6},{5,7},{6,0},{7,1},{8,10},{9,11},{10,... | collective-permute-start | bytes 2359304 | tf_op jit(solution)/shard_map/ppermute | solution.py:744
  419.9 20.5 %collective-permute-start.4 = (bf16[4,32,3072]{2,1,0:T(8,128)(2,1)}, bf16[4,32,3072]{2,1,0:T(8,128)(2,1)}, u32[]{:S(2)}, u32[]{:S(2)}) collective-permute-start(bf16[4,32,3072]{2,1,0:T(8,128)(2,1)} %collective-permute-done.3.refs_5_), channel_id=1, source_target_pairs={{0,6},{1,7},{2,0},{3,1},{4,2},{5,3},{6,4},{7,5},{8,14},{9,15},{10,... | collective-permute-start | bytes 2359304 | tf_op jit(solution)/shard_map/ppermute | solution.py:744
  423.8 1.8 copy-start.1
  423.8 33.4 %collective-permute-start.10 = (bf16[4,32,3072]{2,1,0:T(8,128)(2,1)}, bf16[4,32,3072]{2,1,0:T(8,128)(2,1)}, u32[]{:S(2)}, u32[]{:S(2)}) collective-permute-start(bf16[4,32,3072]{2,1,0:T(8,128)(2,1)} %collective-permute-done.refs_2_), channel_id=1, source_target_pairs={{0,1},{1,0},{2,3},{3,2},{4,5},{5,4},{6,7},{7,6},{8,9},{9,8},{10,11... | collective-permute-start | bytes 2359304 | tf_op jit(solution)/shard_map/ppermute | solution.py:744
  425.4 31.8 %collective-permute-start.13 = (bf16[4,32,3072]{2,1,0:T(8,128)(2,1)}, bf16[4,32,3072]{2,1,0:T(8,128)(2,1)}, u32[]{:S(2)}, u32[]{:S(2)}) collective-permute-start(bf16[4,32,3072]{2,1,0:T(8,128)(2,1)} %collective-permute-done.3.refs_5_), channel_id=1, source_target_pairs={{0,1},{1,0},{2,3},{3,2},{4,5},{5,4},{6,7},{7,6},{8,9},{9,8},{10,11... | collective-permute-start | bytes 2359304 | tf_op jit(solution)/shard_map/ppermute | solution.py:744
  425.6 0.9 copy-start.2
  425.6 31.6 %collective-permute-start.11 = (bf16[4,32,3072]{2,1,0:T(8,128)(2,1)}, bf16[4,32,3072]{2,1,0:T(8,128)(2,1)}, u32[]{:S(2)}, u32[]{:S(2)}) collective-permute-start(bf16[4,32,3072]{2,1,0:T(8,128)(2,1)} %collective-permute-done.6.refs_3_), channel_id=1, source_target_pairs={{0,1},{1,0},{2,3},{3,2},{4,5},{5,4},{6,7},{7,6},{8,9},{9,8},{10,11... | collective-permute-start | bytes 2359304 | tf_op jit(solution)/shard_map/ppermute | solution.py:744
  438.9 27.9 %collective-permute-start.2 = (bf16[4,32,3072]{2,1,0:T(8,128)(2,1)}, bf16[4,32,3072]{2,1,0:T(8,128)(2,1)}, u32[]{:S(2)}, u32[]{:S(2)}) collective-permute-start(bf16[4,32,3072]{2,1,0:T(8,128)(2,1)} %collective-permute-done.1.refs_0_), channel_id=1, source_target_pairs={{0,1},{1,0},{2,3},{3,2},{4,5},{5,4},{6,7},{7,6},{8,9},{9,8},{10,11... | collective-permute-start | bytes 2359304 | tf_op jit(solution)/shard_map/ppermute | solution.py:744
  440.5 26.4 %collective-permute-start.5 = (bf16[4,32,3072]{2,1,0:T(8,128)(2,1)}, bf16[4,32,3072]{2,1,0:T(8,128)(2,1)}, u32[]{:S(2)}, u32[]{:S(2)}) collective-permute-start(bf16[4,32,3072]{2,1,0:T(8,128)(2,1)} %collective-permute-done.4.refs_1_), channel_id=1, source_target_pairs={{0,1},{1,0},{2,3},{3,2},{4,5},{5,4},{6,7},{7,6},{8,9},{9,8},{10,11... | collective-permute-start | bytes 2359304 | tf_op jit(solution)/shard_map/ppermute | solution.py:744
